TPU v7x, 32 devices: a whole 2x2x4 slice. The times are simulated.
32 devices in a mesh: cell: 16 (over z, y, x), gene: 2 (over core).
Axes of the slice: x: 2, y: 2, z: 4, core: 2. Of those that a mesh axis runs over, the one named last changes fastest.
Arguments:
- tiles: bfloat16 [2, 1024, 128, 128], P('gene', 'cell'), may hold values from -8 to 8
- tile_row: int32 [2, 1024], P('gene', 'cell'), may hold values from 0 to 7, as said below
- tile_col: int32 [2, 1024], P('gene', 'cell'), may hold values from 0 to 15
- tile_count: int32 [2, 16], P('gene', 'cell'), may hold values from 1 to 64, as said below
- start_basis: bfloat16 [64, 4096], P(None, 'gene'), may hold values from -0.09375 to 0.09375
Outputs:
- basis: bfloat16 [64, 16384], P(None, 'cell')
- loadings: float32 [64, 4096], P(None, ('gene', 'cell'))
Inputs may be any that keep to these rules, and one draw needn't show every extreme that they name: `tile_row`: tile row of each slot, within 0 to 7; the slots of one device name distinct (row, column) pairs. `tile_count`: slots in use; for each index of gene some device uses all 64.
All inputs are finite; a program needn't handle non-finite values.
Results may differ from a plain program's by a relative error of at most 0.018.
Values may be sent and summed in bfloat16 or wider, within the bound.
No kernel may reach another device: no remote copies, remote signals or barrier semaphores. Data moves between devices by JAX's collectives and lax.ppermute only.
A program may use at most 64 MiB of HBM per device.

v0:
```python
import jax
import jax.numpy as jnp
from jax import lax
from jax.sharding import PartitionSpec as P

ROW_BLOCKS = 8


def solve_lower(lower, right):
    return lax.linalg.triangular_solve(lower, right, left_side=True, lower=True)


def gram_of(scores):
    return jnp.dot(
        scores, scores.T, precision=lax.Precision.HIGHEST, preferred_element_type=jnp.float32
    )


def orthonormal(scores, first_total):
    first = first_total(gram_of(scores))
    lower_one = jnp.linalg.cholesky(first)
    return solve_lower(lower_one, scores)


def local(tiles, tile_row, tile_col, tile_count, start_basis):
    blocks_local = tiles[0]
    slot_count = blocks_local.shape[0]
    tile_size = blocks_local.shape[-1]
    width = start_basis.shape[0]
    gene_dev = start_basis.shape[1]
    gene_blocks = gene_dev // tile_size
    row_blocks = ROW_BLOCKS
    cell_dev = row_blocks * tile_size
    row_index = tile_row[0]
    col_index = tile_col[0]
    live = jnp.arange(slot_count) < tile_count[0, 0]
    row_target = jnp.where(live, row_index, row_blocks)
    col_target = jnp.where(live, col_index, gene_blocks)

    def first_total(gram):
        return lax.psum(gram, ("cell", "gene"))

    def merge_halves(partial_scores):
        return lax.psum_scatter(partial_scores, "gene", scatter_dimension=1, tiled=True)

    def scores_of(basis):
        picked = jnp.take(basis.reshape(width, gene_blocks, tile_size), col_index, axis=1)
        products = jnp.einsum(
            "ksg,srg->skr", picked, blocks_local, preferred_element_type=jnp.float32
        )
        summed = jax.ops.segment_sum(products, row_target, num_segments=row_blocks + 1)[:row_blocks]
        return merge_halves(jnp.transpose(summed, (1, 0, 2)).reshape(width, cell_dev))

    def loadings_of(ortho_half):
        picked = jnp.take(ortho_half.reshape(width, row_blocks, tile_size), row_index, axis=1)
        products = jnp.einsum(
            "ksr,srg->skg", picked, blocks_local, preferred_element_type=jnp.float32
        )
        summed = jax.ops.segment_sum(products, col_target, num_segments=gene_blocks + 1)[
            :gene_blocks
        ]
        return jnp.transpose(summed, (1, 0, 2)).reshape(width, gene_dev)

    ortho = orthonormal(scores_of(start_basis), first_total)
    ortho_half = ortho.astype(jnp.bfloat16)
    ortho_rows = lax.all_gather(ortho_half, "gene", axis=1, tiled=True)
    partial_value = loadings_of(ortho_rows)
    next_basis = lax.psum(partial_value, "cell").astype(jnp.bfloat16)
    ortho_two = orthonormal(scores_of(next_basis), first_total)
    scale = jnp.sqrt(jnp.float32(lax.axis_size("cell") * cell_dev))
    ortho_two_half = ortho_two.astype(jnp.bfloat16)
    basis_piece = (ortho_two * scale).astype(jnp.bfloat16)
    final_rows, basis = (
        lax.all_gather(ortho_two_half, "gene", axis=1, tiled=True),
        lax.all_gather(basis_piece, "gene", axis=1, tiled=True),
    )
    loadings = lax.psum_scatter(loadings_of(final_rows), "cell", scatter_dimension=1, tiled=True)
    return (basis, loadings)


def solution(mesh):
    return jax.shard_map(
        local,
        mesh=mesh,
        in_specs=(
            P("gene", "cell", None, None),
            P("gene", "cell"),
            P("gene", "cell"),
            P("gene", "cell"),
            P(None, "gene"),
        ),
        out_specs=(P(None, "cell"), P(None, ("gene", "cell"))),
        check_vma=False,
    )
```

profile of v0, /device:TPU:0, one launch (start us, length us, event | category | flops | bytes accessed | tf_op | source)
XLA Modules:
  0.0 349.8 jit_solution(15291023441210544630)
XLA Ops:
  7.2 0.0 copy-start
  7.2 0.0 copy-start.1
  7.2 0.0 copy-start.2
  7.2 0.0 reduce-scatter.4.cloned.1.call-start
  7.2 0.8 compare_select_fusion
  8.0 0.7 compare_and_fusion
  8.7 1.0 copy_bitcast_fusion.5
  10.4 0.7 gather_fusion
  11.1 0.0 copy-done.1
  11.2 0.0 copy-done.2
  11.2 0.0 copy-done
  11.2 2.9 fusion.6
  14.1 7.1 %scatter_fusion = f32[9,64,128]{2,1,0:T(8,128)S(1)} fusion(f32[9,64,128]{2,1,0:T(8,128)S(1)} %broadcast.69.clone, s32[64]{0:T(128)S(1)} %get-tuple-element.8, f32[64,64,128]{2,1,0:T(8,128)} %fusion.6), kind=kCustom, calls=%fused_computation.4 | custom fusion | flops 524288 | bytes 6291712 | tf_op jit(solution)/shard_map/scatter-add | solution.py:51
  21.2 0.7 copy_bitcast_fusion.3
  21.9 0.0 reduce-scatter.4.cloned.1.call-update
  21.9 0.0 reduce-scatter.6.cloned.1.call-start
  22.0 10.5 %reduce-scatter.4.cloned.1.call-done = f32[64,512]{1,0:T(8,128)} async-done(((f32[64,1024]{1,0:T(8,128)}), f32[64,512]{1,0:T(8,128)}) %reduce-scatter.4.cloned.1.call-update) | async-done | bytes 131088 | tf_op jit(solution)/shard_map/reduce_scatter | solution.py:44
  32.5 1.2 fusion.40
  33.8 40.6 %psum.21 = f32[64,64]{0,1:T(8,128)S(1)} all-reduce(f32[64,64]{0,1:T(8,128)S(1)} %fusion.40), channel_id=1, replica_groups=mesh['cell'=16,'gene'=2] {'cell','gene'}, use_global_device_ids=true, to_apply=%region_2.4 | all-reduce | flops 4096 | bytes 32768 | tf_op jit(solution)/shard_map/psum | solution.py:41
  74.4 0.1 copy.20
  74.5 5.8 %cholesky.44 = f32[64,64]{1,0:T(8,128)S(1)} custom-call(f32[64,64]{1,0:T(8,128)S(1)} %fusion.30), custom_call_target="Cholesky" | custom-call | tf_op jit(solution)/shard_map/jit(cholesky)/cholesky | solution.py:21
  80.3 0.6 compare_reduce_fusion.1
  81.0 0.7 fusion.24
  81.6 4.9 %custom-call.6 = f32[1,64,64]{1,2,0:T(8,128)S(1)} custom-call(f32[1,64,64]{2,1,0:T(8,128)S(1)} %fusion.24), custom_call_target="InvertDiagBlocksLowerTriangular" | custom-call | tf_op jit(solution)/shard_map/triangular_solve/custom-call.0 | solution.py:10
  86.5 1.2 convolution_convert_fusion
  87.8 1.9 all_gather.9
  89.7 0.7 gather_fusion.1
  90.5 2.1 fusion.4
  92.6 7.1 %scatter_fusion.1 = f32[17,64,128]{2,1,0:T(8,128)S(1)} fusion(f32[17,64,128]{2,1,0:T(8,128)S(1)} %broadcast.70.clone, s32[64]{0:T(128)S(1)} %get-tuple-element.9, f32[64,64,128]{2,1,0:T(8,128)} %fusion.4), kind=kCustom, calls=%fused_computation.5 | custom fusion | flops 524288 | bytes 6291712 | tf_op jit(solution)/shard_map/scatter-add | solution.py:59
  99.7 81.6 %all-reduce.1 = bf16[64,2048]{1,0:T(8,128)(2,1)S(1)} all-reduce(f32[64,2048]{1,0:T(8,128)S(1)} %copy_bitcast_fusion.1), channel_id=1, replica_groups=mesh['cell'=16,'gene'=2] {'cell'}, use_global_device_ids=true, to_apply=%region_6.11 | all-reduce | flops 131072 | bytes 786432 | tf_op jit(solution)/shard_map/psum | solution.py:68
  181.3 0.1 copy_bitcast_fusion.4
  181.4 0.8 gather_fusion.2
  182.1 2.9 fusion.2
  185.1 7.1 %scatter_fusion.2 = f32[9,64,128]{2,1,0:T(8,128)S(1)} fusion(f32[9,64,128]{2,1,0:T(8,128)S(1)} %broadcast.69, s32[64]{0:T(128)S(1)} %get-tuple-element.8, f32[64,64,128]{2,1,0:T(8,128)} %fusion.2), kind=kCustom, calls=%fused_computation.6 | custom fusion | flops 524288 | bytes 6291712 | tf_op jit(solution)/shard_map/scatter-add | solution.py:51
  192.1 0.7 copy_bitcast_fusion.2
  192.8 0.0 reduce-scatter.6.cloned.1.call-update
  192.9 0.0 reduce-scatter.8.cloned.1.call-start
  192.9 4.2 %reduce-scatter.6.cloned.1.call-done = f32[64,512]{1,0:T(8,128)} async-done(((f32[64,1024]{1,0:T(8,128)}), f32[64,512]{1,0:T(8,128)}) %reduce-scatter.6.cloned.1.call-update) | async-done | bytes 131088 | tf_op jit(solution)/shard_map/reduce_scatter | solution.py:44
  197.1 1.2 fusion.41
  198.3 40.7 %psum.23 = f32[64,64]{0,1:T(8,128)S(1)} all-reduce(f32[64,64]{0,1:T(8,128)S(1)} %fusion.41), channel_id=1, replica_groups=mesh['cell'=16,'gene'=2] {'cell','gene'}, use_global_device_ids=true, to_apply=%region_9.14 | all-reduce | flops 4096 | bytes 32768 | tf_op jit(solution)/shard_map/psum | solution.py:41
  239.1 0.1 copy.26
  239.2 5.8 %cholesky.55 = f32[64,64]{1,0:T(8,128)S(1)} custom-call(f32[64,64]{1,0:T(8,128)S(1)} %fusion.28), custom_call_target="Cholesky" | custom-call | tf_op jit(solution)/shard_map/jit(cholesky)/cholesky | solution.py:21
  245.1 0.6 compare_reduce_fusion
  245.7 0.7 fusion.25
  246.4 4.9 %custom-call.7 = f32[1,64,64]{1,2,0:T(8,128)S(1)} custom-call(f32[1,64,64]{2,1,0:T(8,128)S(1)} %fusion.25), custom_call_target="InvertDiagBlocksLowerTriangular" | custom-call | tf_op jit(solution)/shard_map/triangular_solve/custom-call.0 | solution.py:10
  251.3 1.2 fusion.39
  252.5 1.9 all_gather.11
  254.4 0.7 gather_fusion.3
  255.2 2.1 fusion
  257.3 7.1 %scatter_fusion.3 = f32[17,64,128]{2,1,0:T(8,128)S(1)} fusion(f32[17,64,128]{2,1,0:T(8,128)S(1)} %broadcast.70, s32[64]{0:T(128)S(1)} %get-tuple-element.9, f32[64,64,128]{2,1,0:T(8,128)} %fusion), kind=kCustom, calls=%fused_computation.7 | custom fusion | flops 524288 | bytes 6291712 | tf_op jit(solution)/shard_map/scatter-add | solution.py:59
  264.4 0.8 copy_bitcast_fusion
  265.2 0.0 reduce-scatter.8.cloned.1.call-update
  265.2 1.9 all_gather.10
  267.1 75.5 %reduce-scatter.8.cloned.1.call-done = f32[64,128]{1,0:T(8,128)} async-done(((f32[64,2048]{1,0:T(8,128)}), f32[64,128]{1,0:T(8,128)}) %reduce-scatter.8.cloned.1.call-update) | async-done | bytes 32784 | tf_op jit(solution)/shard_map/reduce_scatter | solution.py:77
  342.7 0.7 copy.55
  (16 shorter events, 0.3 us)
Async XLA Ops:
  7.2 4.0 %copy-start = (bf16[1,64,128,128]{3,2,1,0:T(8,128)(2,1)S(1)}, bf16[1,64,128,128]{3,2,1,0:T(8,128)(2,1)}, u32[]{:S(2)}) copy-start(bf16[1,64,128,128]{3,2,1,0:T(8,128)(2,1)} %param.12) | copy-start | bytes 6291460
  7.2 4.0 %copy-start.1 = (s32[1,64]{1,0:T(1,128)S(1)}, s32[1,64]{1,0:T(1,128)}, u32[]{:S(2)}) copy-start(s32[1,64]{1,0:T(1,128)} %param.14) | copy-start | bytes 772
  7.2 4.0 %copy-start.2 = (s32[1,64]{1,0:T(1,128)S(1)}, s32[1,64]{1,0:T(1,128)}, u32[]{:S(2)}) copy-start(s32[1,64]{1,0:T(1,128)} %param.13) | copy-start | bytes 772
  7.2 25.3 %reduce-scatter.4.cloned.1.call-start = ((), (), s32[]{:S(2)}) async-start(), calls=%async_computation.3 | async-start | bytes 393216 | tf_op jit(solution)/shard_map/reduce_scatter | solution.py:44
  21.9 175.2 %reduce-scatter.6.cloned.1.call-start = ((), (), s32[]{:S(2)}) async-start(), calls=%async_computation.4 | async-start | bytes 393216 | tf_op jit(solution)/shard_map/reduce_scatter | solution.py:44
  192.9 149.8 %reduce-scatter.8.cloned.1.call-start = ((), (), s32[]{:S(2)}) async-start(), calls=%async_computation.5 | async-start | bytes 557056 | tf_op jit(solution)/shard_map/reduce_scatter | solution.py:77
Sparse Core Ops, SparseCore 0:
  22.0 10.4 reduce-scatter.3
  193.0 4.0 reduce-scatter.5
  265.4 77.2 reduce-scatter.7
where the time goes:
time: 351 us; the launch traced here: 350 us
  blocking collectives  169 us (48%)
  waiting for transfers between devices  90.3 us (26%)
  other arithmetic  53.9 us (15%)
  matrix products  14.9 us (4%)
  between operations  14.7 us (4%)
  local copies, waits for them, and re-layouts  7.35 us (2%)
    psum x1, blocking collectives, local(): next_basis = lax.psum(partial_value, 'cell').astype(jnp.bfloat16)  81.6 us
    psum x2, blocking collectives, first_total(): return lax.psum(gram, ('cell', 'gene'))  81.3 us
    reduce_scatter x1, waiting for transfers between devices, local(): lax.psum_scatter(loadings_of(final_rows), 'cell', scatter_dimension=1, ti...  75.5 us
    reduce_scatter x2, waiting for transfers between devices, merge_halves(): lax.psum_scatter(partial_scores, 'gene', scatter_dimension=1, tiled=True)  14.7 us
    scatter-add x2, other arithmetic, scores_of(): jax.ops.segment_sum(products, row_target, num_segments=row_blocks + 1)  14.1 us
    scatter-add x2, other arithmetic, loadings_of(): jax.ops.segment_sum(products, col_target, num_segments=gene_blocks + 1)  14.1 us
    another operation x6, other arithmetic, orthonormal(): lower_one = jnp.linalg.cholesky(first)  13 us
    another operation x4, other arithmetic, solve_lower(): return lax.linalg.triangular_solve(lower, right, left_side=True, lower=True)  11.1 us
  transfers between devices with their start and end apart: 3, of which 3 were waited for; matrix products, arithmetic and copies ran while one was open for 0% of the time, Pallas kernels for 0%

commit v1 on v0

v1 whole, which is shorter than its diff:
```python
import functools

import jax
import jax.numpy as jnp
from jax import lax
from jax.experimental import pallas as pl
from jax.experimental.pallas import tpu as pltpu
from jax.sharding import PartitionSpec as P

ROW_BLOCKS = 8
BF = jnp.bfloat16
F32 = jnp.float32
HIGH = lax.Precision.HIGHEST
NT = (((1,), (1,)), ((), ()))
TN = (((0,), (0,)), ((), ()))
NN = (((1,), (0,)), ((), ()))
VMEM = pl.BlockSpec(memory_space=pltpu.VMEM)
SMEM = pl.BlockSpec(memory_space=pltpu.SMEM)
ANY = pl.BlockSpec(memory_space=pl.ANY)


def dot(a, b, dims, precision=None):
    return lax.dot_general(a, b, dims, precision=precision, preferred_element_type=F32)


def dense_kernel(row, col, count, tiles, basis, x_ref, s_ref, held, sems):
    tile = tiles.shape[-1]
    rows = x_ref.shape[0] // tile
    cols = x_ref.shape[1] // tile

    def place(r, c):
        return x_ref.at[pl.ds(pl.multiple_of(r * tile, tile), tile), pl.ds(pl.multiple_of(c * tile, tile), tile)]

    def copy(s):
        return pltpu.make_async_copy(tiles.at[s], place(row[0, s], col[0, s]), sems.at[s])

    for i in range(rows * cols):
        held[i] = 0
    live = count[0, 0]

    def start(s, _):
        copy(s).start()
        held[row[0, s] * cols + col[0, s]] = 1
        return 0

    lax.fori_loop(0, live, start, 0)

    def clear(i, _):
        @pl.when(held[i] == 0)
        def _():
            spot = place(i // cols, lax.rem(i, cols))
            spot[...] = jnp.zeros((tile, tile), BF)

        return 0

    lax.fori_loop(0, rows * cols, clear, 0)

    def finish(s, _):
        copy(s).wait()
        return 0

    lax.fori_loop(0, live, finish, 0)
    s_ref[...] = dot(basis[...], x_ref[...], NT)


def scores_kernel(pieces, x, s_ref):
    s_ref[...] = dot(pieces[...], x[...], NT)


def share_kernel(me, own, other, x, y_ref, gram_ref, total_ref=None):
    total = own[...] + other[...]
    if total_ref is not None:
        total_ref[...] = total
    k = total.shape[0]
    high = total.astype(BF)
    low = (total - high.astype(F32)).astype(BF)
    both = jnp.concatenate([high, low], axis=0)
    g = dot(both, high, NT)
    h = dot(both, low, NT)
    gram_ref[...] = (g[:k] + (g[k:] + h[:k])) + h[k:]
    y = dot(both, x[...], NN)
    y = y[:k] + y[k:]
    if len(y_ref.shape) == 2:
        y_ref[...] = y
    else:
        n, _, wide = y_ref.shape
        for q in range(n):
            y_ref[jnp.bitwise_xor(me[0], q)] = y[:, q * wide : (q + 1) * wide]


def lower_inverse(gram, block=8):
    k = gram.shape[0]
    eye = (lax.broadcasted_iota(jnp.int32, (k, k), 0) == lax.broadcasted_iota(jnp.int32, (k, k), 1)).astype(F32)
    rest = jnp.concatenate([gram, eye], axis=1)
    wide = rest.shape[1]
    ids = lax.broadcasted_iota(jnp.int32, (block, wide), 0)
    done = []
    for j in range(0, k, block):
        panel = rest[:block]
        diag = [jnp.broadcast_to(panel[:, j + i : j + i + 1], (block, wide)) for i in range(block)]
        scale = jnp.zeros((block, wide), F32)
        for i in range(block):
            pivot = diag[i][i : i + 1, :]
            scale = jnp.where(ids == i, lax.rsqrt(pivot), scale)
            if i + 1 < block:
                factor = jnp.where(ids > i, diag[i] * (1.0 / pivot), 0.0)
                panel = panel - factor * panel[i : i + 1, :]
                for m in range(i + 1, block):
                    diag[m] = diag[m] - factor * diag[m][i : i + 1, :]
        panel = panel * scale
        done.append(panel)
        if j + block < k:
            update = dot(panel[:, :k], panel, TN, HIGH)
            rest = rest[block:] - update[j + block :]
    return jnp.concatenate(done, axis=0)


def solve(factor, right):
    return dot(factor, jnp.concatenate([jnp.zeros_like(right), right], axis=0), NN, HIGH)


def added(refs):
    total = refs[0][...]
    for r in refs[1:]:
        total = total + r[...]
    return total


def basis_kernel(parts, *refs):
    grams, pieces, out = refs[:parts], refs[parts : 2 * parts], refs[-1]
    out[...] = solve(lower_inverse(added(grams)), added(pieces)).astype(BF)


def final_kernel(parts, scale, *refs):
    grams, pieces = refs[:parts], refs[parts : 2 * parts]
    total, basis_ref, load_ref = refs[2 * parts :]
    factor = lower_inverse(added(grams))
    load_ref[...] = solve(factor, added(pieces))
    basis_ref[...] = (solve(factor, total[...]) * scale).astype(BF)


def stages_of(n):
    stages = []
    step = 1
    while step < n:
        count = min(4, n // step)
        stages.append((step, count))
        step *= count
    return stages


def hop(value, distance, n):
    return lax.ppermute(value, "cell", [(i, i ^ distance) for i in range(n)])


def reduce_both(y, gram, n):
    stages = stages_of(n)
    for at, (step, count) in enumerate(stages):
        left = y.shape[0] // count
        y = y.reshape((left, count) + y.shape[1:])
        pieces = [y[:, 0]] + [hop(y[:, d], d * step, n) for d in range(1, count)]
        grams = [gram] + [hop(gram, d * step, n) for d in range(1, count)]
        if at + 1 < len(stages):
            y, gram = sum(pieces[1:], pieces[0]), sum(grams[1:], grams[0])
    return grams, [p[0] for p in pieces]


def gather(piece, n):
    whole = piece[None]
    for step, count in reversed(stages_of(n)):
        parts = [whole] + [hop(whole, d * step, n) for d in range(1, count)]
        whole = jnp.stack(parts, axis=1).reshape((-1,) + piece.shape)
    return whole


def local(tiles, tile_row, tile_col, tile_count, start_basis):
    n = lax.axis_size("cell")
    me = lax.axis_index("cell").astype(jnp.int32)
    slots, tile = tiles.shape[1], tiles.shape[-1]
    k, genes = start_basis.shape
    cells = ROW_BLOCKS * tile
    wide = genes // n
    aligned = wide % 128 == 0
    me_ref = me.reshape(1)

    x, half = pl.pallas_call(
        dense_kernel,
        out_shape=(jax.ShapeDtypeStruct((cells, genes), BF), jax.ShapeDtypeStruct((k, cells), F32)),
        in_specs=[SMEM, SMEM, SMEM, ANY, VMEM],
        out_specs=(VMEM, VMEM),
        scratch_shapes=[pltpu.SMEM((ROW_BLOCKS * (genes // tile),), jnp.int32), pltpu.SemaphoreType.DMA((slots,))],
        name="dense",
    )(tile_row, tile_col, tile_count, tiles[0], start_basis)

    def share(half, keep):
        other = lax.ppermute(half, "gene", [(0, 1), (1, 0)])
        y_shape = (n, k, wide) if aligned else (k, genes)
        shapes = [jax.ShapeDtypeStruct(y_shape, F32), jax.ShapeDtypeStruct((k, k), F32)]
        if keep:
            shapes.append(jax.ShapeDtypeStruct((k, cells), F32))
        y, gram, *total = pl.pallas_call(
            share_kernel,
            out_shape=tuple(shapes),
            in_specs=[SMEM, VMEM, VMEM, VMEM],
            out_specs=(VMEM,) * len(shapes),
            name="share",
        )(me_ref, half, other, x)
        if not aligned:
            y = jnp.transpose(y.reshape(k, n, wide), (1, 0, 2))[jnp.arange(n) ^ me]
        grams, pieces = reduce_both(y, gram, n)
        return grams, pieces, total

    grams, pieces, _ = share(half, False)
    piece = pl.pallas_call(
        functools.partial(basis_kernel, len(grams)),
        out_shape=jax.ShapeDtypeStruct((k, wide), BF),
        in_specs=[VMEM] * (2 * len(grams)),
        out_specs=VMEM,
        name="basis",
    )(*grams, *pieces)
    whole = gather(piece, n)[jnp.arange(n) ^ me]
    basis = jnp.transpose(whole, (1, 0, 2)).reshape(k, genes)
    half = pl.pallas_call(
        scores_kernel,
        out_shape=jax.ShapeDtypeStruct((k, cells), F32),
        in_specs=[VMEM, VMEM],
        out_specs=VMEM,
        name="scores",
    )(basis, x)
    grams, pieces, (total,) = share(half, True)
    scale = float(n * cells) ** 0.5
    return pl.pallas_call(
        functools.partial(final_kernel, len(grams), scale),
        out_shape=(jax.ShapeDtypeStruct((k, cells), BF), jax.ShapeDtypeStruct((k, wide), F32)),
        in_specs=[VMEM] * (2 * len(grams) + 1),
        out_specs=(VMEM, VMEM),
        name="final",
    )(*grams, *pieces, total)


def solution(mesh):
    return jax.shard_map(
        local,
        mesh=mesh,
        in_specs=(
            P("gene", "cell", None, None),
            P("gene", "cell"),
            P("gene", "cell"),
            P("gene", "cell"),
            P(None, "gene"),
        ),
        out_specs=(P(None, "cell"), P(None, ("gene", "cell"))),
        check_vma=False,
    )
```

time: 351 us -> 106 us (0.30)
  blocking collectives: 169 us -> 0 us
  waiting for transfers between devices: 90.3 us -> 19.1 us
  other arithmetic: 53.9 us -> 4.21 us
  starting transfers between devices: 0.12 us -> 43.5 us
  Pallas kernels: 0 us -> 29.6 us
  matrix products: 14.9 us -> 0 us
  between operations: 14.7 us -> 1.48 us
    psum x3 -> x0, blocking collectives: 163 us -> none  [the longest x1 81.6 us: local(): next_basis = lax.psum(partial_value, 'cell').astype(jnp.bfloat16)]
    reduce_scatter x3 -> x0, waiting for transfers between devices: 90.2 us -> none  [the longest x1 75.5 us: local(): lax.psum_scatter(loadings_of(final_rows), 'cell', scatter_dimension=1, ti...]
    ppermute x0 -> x32, starting transfers between devices: none -> 43.5 us  [the longest x30 43.3 us: hop(): return lax.ppermute(value, 'cell', [(i, i ^ distance) for i in range(n)])]
    pallas_call x0 -> x6, Pallas kernels: none -> 29.6 us  [the longest x2 7.97 us: share(): pl.pallas_call(share_kernel, out_shape=tuple(shapes), in_specs=[SMEM, VME...]
    scatter-add x4 -> x0, other arithmetic: 28.2 us -> none  [the longest x2 14.1 us: scores_of(): jax.ops.segment_sum(products, row_target, num_segments=row_blocks + 1)]
    another operation x10 -> x2, other arithmetic: 24.1 us -> 0.77 us  [gather(): whole = jnp.stack(parts, axis=1).reshape((-1,) + piece.shape)]
    ppermute x0 -> x32, waiting for transfers between devices: none -> 19.1 us  [the longest x30 15.8 us: hop(): return lax.ppermute(value, 'cell', [(i, i ^ distance) for i in range(n)])]
    dot_general x6 -> x0, matrix products: 12.4 us -> none  [the longest x2 5.79 us: scores_of(): jnp.einsum('ksg,srg->skr', picked, blocks_local, preferred_element_type=j...]
  transfers between devices with their start and end apart: 3 -> 32, of which waited for: 3 -> 15; matrix products, arithmetic and copies ran while one was open for 0% -> 6% of each run, Pallas kernels for 0% -> 0%
where the time goes in v1:
time: 106 us; the launch traced here: 105 us
  starting transfers between devices  43.5 us (41%)
  Pallas kernels  29.6 us (28%)
  waiting for transfers between devices  19.1 us (18%)
  local copies, waits for them, and re-layouts  7.25 us (7%)
  other arithmetic  4.21 us (4%)
  between operations  1.48 us (1%)
    ppermute x30, starting transfers between devices, hop(): return lax.ppermute(value, 'cell', [(i, i ^ distance) for i in range(n)])  43.3 us
    ppermute x30, waiting for transfers between devices, hop(): return lax.ppermute(value, 'cell', [(i, i ^ distance) for i in range(n)])  15.8 us
    pallas_call x2, Pallas kernels, share(): pl.pallas_call(share_kernel, out_shape=tuple(shapes), in_specs=[SMEM, VME...  7.97 us
    pallas_call x1, Pallas kernels, local(): pl.pallas_call(dense_kernel, out_shape=(jax.ShapeDtypeStruct((cells, gene...  7.08 us
    pallas_call x1, Pallas kernels, local(): pl.pallas_call(functools.partial(final_kernel, len(grams), scale), out_sh...  5.34 us
    pallas_call x1, Pallas kernels, local(): pl.pallas_call(functools.partial(basis_kernel, len(grams)), out_shape=jax...  4.82 us
    pallas_call x1, Pallas kernels, local(): pl.pallas_call(scores_kernel, out_shape=jax.ShapeDtypeStruct((k, cells),...  4.36 us
    squeeze x4, local copies, waits for them, and re-layouts, reduce_both(): pieces = [y[:, 0]] + [hop(y[:, d], d * step, n) for d in range(1, count)]  3.33 us
  transfers between devices with their start and end apart: 32, of which 15 were waited for; matrix products, arithmetic and copies ran while one was open for 6% of the time, Pallas kernels for 0%

profile of v1, /device:TPU:0, one launch (start us, length us, event | category | flops | bytes accessed | tf_op | source)
XLA Modules:
  0.0 105.1 jit_solution(16291966143288824421)
XLA Ops:
  1.3 7.1 %dense.1 = (bf16[1024,2048]{1,0:T(8,128)(2,1)}, f32[64,1024]{1,0:T(8,128)}) custom-call(s32[1,64]{1,0:T(1,128)} %row.1, s32[1,64]{1,0:T(1,128)} %col.1, s32[1,1]{1,0:T(1,128)S(6)} %copy.27.count, bf16[64,128,128]{2,1,0:T(8,128)(2,1)} %bitcast.99, bf16[64,2048]{1,0:T(8,128)(2,1)} %basis.2), custom_call_target="tpu_custom_call" | custom-call | tf_op jit(solution)/shard_map/dense/pallas_call | solution.py:186
  8.4 0.3 collective-permute-start
  8.6 1.5 %collective-permute-done.other = f32[64,1024]{1,0:T(8,128)S(1)} collective-permute-done((f32[64,1024]{1,0:T(8,128)}, f32[64,1024]{1,0:T(8,128)S(1)}, u32[]{:S(2)}, u32[]{:S(2)}) %collective-permute-start) | collective-permute-done | bytes 262176 | tf_op jit(solution)/shard_map/ppermute | solution.py:196
  10.2 0.7 copy-done
  10.9 4.0 %share.2 = (f32[16,64,128]{2,1,0:T(8,128)}, f32[64,64]{1,0:T(8,128)}) custom-call(s32[1]{0:T(128)} %bitcast.me, f32[64,1024]{1,0:T(8,128)} %get-tuple-element.9.own, f32[64,1024]{1,0:T(8,128)} %copy-done, bf16[1024,2048]{1,0:T(8,128)(2,1)} %get-tuple-element.10.x), custom_call_target="tpu_custom_call" | custom-call | tf_op jit(solution)/shard_map/share/pallas_call | solution.py:201
  14.9 3.9 %collective-permute-start.3 = (f32[64,64]{1,0:T(8,128)}, f32[64,64]{1,0:T(8,128)S(1)}, u32[]{:S(2)}, u32[]{:S(2)}) collective-permute-start(f32[64,64]{1,0:T(8,128)} %get-tuple-element.11), channel_id=1, source_target_pairs={{0,6},{2,4},{4,2},{6,0},{8,14},{10,12},{12,10},{14,8},{16,22},{18,... | collective-permute-start | bytes 49160 | tf_op jit(solution)/shard_map/ppermute | solution.py:153
  18.8 0.6 collective-permute-start.2
  19.4 1.1 %slice_bitcast_fusion.6 = (f32[4,64,128]{2,1,0:T(8,128)S(1)}, f32[4,64,128]{2,1,0:T(8,128)S(1)}, f32[4,64,128]{2,1,0:T(8,128)S(1)}) fusion(f32[4,4,64,128]{3,2,1,0:T(8,128)} %bitcast.103), kind=kLoop, calls=%fused_computation.13 | loop fusion | bytes 786432 | tf_op jit(solution)/shard_map/squeeze | solution.py:161
  20.5 2.1 %collective-permute-start.7 = (f32[4,64,128]{2,1,0:T(8,128)S(1)}, f32[4,64,128]{2,1,0:T(8,128)S(1)}, u32[]{:S(2)}, u32[]{:S(2)}) collective-permute-start(f32[4,64,128]{2,1,0:T(8,128)S(1)} %get-tuple-element.19), channel_id=1, source_target_pairs={{0,2},{2,0},{4,6},{6,4},{8,10},{10,8},{12,14},{14,12},{16,18},{18,... | collective-permute-start | bytes 393224 | tf_op jit(solution)/shard_map/ppermute | solution.py:153
  22.5 1.4 %collective-permute-start.8 = (f32[4,64,128]{2,1,0:T(8,128)S(1)}, f32[4,64,128]{2,1,0:T(8,128)S(1)}, u32[]{:S(2)}, u32[]{:S(2)}) collective-permute-start(f32[4,64,128]{2,1,0:T(8,128)S(1)} %get-tuple-element.20), channel_id=1, source_target_pairs={{0,4},{2,6},{4,0},{6,2},{8,12},{10,14},{12,8},{14,10},{16,20},{18,... | collective-permute-start | bytes 393224 | tf_op jit(solution)/shard_map/ppermute | solution.py:153
  24.1 0.8 add_add_fusion.1.refs_0_
  24.9 4.0 %collective-permute-start.6 = (f32[64,64]{1,0:T(8,128)S(1)}, f32[64,64]{1,0:T(8,128)S(1)}, u32[]{:S(2)}, u32[]{:S(2)}) collective-permute-start(f32[64,64]{1,0:T(8,128)S(1)} %add_add_fusion.1.refs_0_), channel_id=1, source_target_pairs={{0,24},{2,26},{4,28},{6,30},{8,16},{10,18},{12,20},{14,22},{16,8},... | collective-permute-start | bytes 49160 | tf_op jit(solution)/shard_map/ppermute | solution.py:153
  28.9 1.5 %collective-permute-done.8 = f32[4,64,128]{2,1,0:T(8,128)S(1)} collective-permute-done((f32[4,64,128]{2,1,0:T(8,128)S(1)}, f32[4,64,128]{2,1,0:T(8,128)S(1)}, u32[]{:S(2)}, u32[]{:S(2)}) %collective-permute-start.8) | collective-permute-done | bytes 131104 | tf_op jit(solution)/shard_map/ppermute | solution.py:153
  30.3 0.9 fusion.7
  31.3 0.6 slice_bitcast_fusion.12
  31.9 3.3 %collective-permute-start.12 = (f32[1,64,128]{2,1,0:T(8,128)S(1)}, f32[1,64,128]{2,1,0:T(8,128)S(1)}, u32[]{:S(2)}, u32[]{:S(2)}) collective-permute-start(f32[1,64,128]{2,1,0:T(8,128)S(1)} %get-tuple-element.26), channel_id=1, source_target_pairs={{0,24},{2,26},{4,28},{6,30},{8,16},{10,18},{12,20},{14,22},{16,8},... | collective-permute-start | bytes 98312 | tf_op jit(solution)/shard_map/ppermute | solution.py:153
  35.2 1.0 collective-permute-start.10
  36.3 1.9 %collective-permute-start.5 = (f32[64,64]{1,0:T(8,128)S(1)}, f32[64,64]{1,0:T(8,128)S(1)}, u32[]{:S(2)}, u32[]{:S(2)}) collective-permute-start(f32[64,64]{1,0:T(8,128)S(1)} %add_add_fusion.1.refs_0_), channel_id=1, source_target_pairs={{0,16},{2,18},{4,20},{6,22},{8,24},{10,26},{12,28},{14,30},{16,0},... | collective-permute-start | bytes 49160 | tf_op jit(solution)/shard_map/ppermute | solution.py:153
  38.1 2.0 %collective-permute-start.4 = (f32[64,64]{1,0:T(8,128)S(1)}, f32[64,64]{1,0:T(8,128)S(1)}, u32[]{:S(2)}, u32[]{:S(2)}) collective-permute-start(f32[64,64]{1,0:T(8,128)S(1)} %add_add_fusion.1.refs_0_), channel_id=1, source_target_pairs={{0,8},{2,10},{4,12},{6,14},{8,0},{10,2},{12,4},{14,6},{16,24},{18,... | collective-permute-start | bytes 49160 | tf_op jit(solution)/shard_map/ppermute | solution.py:153
  40.2 0.9 collective-permute-done.5.refs_2_
  41.1 1.0 collective-permute-done.4.refs_1_
  42.1 0.5 copy-done.15
  42.7 4.8 %basis.3 = bf16[64,128]{1,0:T(8,128)(2,1)} custom-call(f32[64,64]{1,0:T(8,128)} %copy-done.3, f32[64,64]{1,0:T(8,128)} %copy-done.15, f32[64,64]{1,0:T(8,128)} %copy-done.13, f32[64,64]{1,0:T(8,128)} %copy-done.5, f32[64,128]{1,0:T(8,128)} %get-tuple-element.29.refs_4_, f32[64,128]{1,0:T(8,128)} %bitcast.117, f32[64,128]{1,0:T(8,128)} %bitcast.116, ...), custom_call_target="tpu_custom_call" | custom-call | tf_op jit(solution)/shard_map/basis/pallas_call | solution.py:214
  47.5 2.4 %collective-permute-start.15 = (bf16[1,64,128]{2,1,0:T(8,128)(2,1)}, bf16[1,64,128]{2,1,0:T(8,128)(2,1)S(1)}, u32[]{:S(2)}, u32[]{:S(2)}) collective-permute-start(bf16[1,64,128]{2,1,0:T(8,128)(2,1)} %bitcast.105), channel_id=1, source_target_pairs={{0,24},{2,26},{4,28},{6,30},{8,16},{10,18},{12,20},{14,22},{16,8},... | collective-permute-start | bytes 49160 | tf_op jit(solution)/shard_map/ppermute | solution.py:153
  49.9 1.1 %collective-permute-start.14 = (bf16[1,64,128]{2,1,0:T(8,128)(2,1)}, bf16[1,64,128]{2,1,0:T(8,128)(2,1)S(1)}, u32[]{:S(2)}, u32[]{:S(2)}) collective-permute-start(bf16[1,64,128]{2,1,0:T(8,128)(2,1)} %bitcast.106), channel_id=1, source_target_pairs={{0,16},{2,18},{4,20},{6,22},{8,24},{10,26},{12,28},{14,30},{16,0},... | collective-permute-start | bytes 49160 | tf_op jit(solution)/shard_map/ppermute | solution.py:153
  51.0 0.9 collective-permute-start.13
  51.9 1.4 %collective-permute-done.15 = bf16[1,64,128]{2,1,0:T(8,128)(2,1)S(1)} collective-permute-done((bf16[1,64,128]{2,1,0:T(8,128)(2,1)}, bf16[1,64,128]{2,1,0:T(8,128)(2,1)S(1)}, u32[]{:S(2)}, u32[]{:S(2)}) %collective-permute-start.15) | collective-permute-done | bytes 16416 | tf_op jit(solution)/shard_map/ppermute | solution.py:153
  53.3 1.5 %collective-permute-done.14 = bf16[1,64,128]{2,1,0:T(8,128)(2,1)S(1)} collective-permute-done((bf16[1,64,128]{2,1,0:T(8,128)(2,1)}, bf16[1,64,128]{2,1,0:T(8,128)(2,1)S(1)}, u32[]{:S(2)}, u32[]{:S(2)}) %collective-permute-start.14) | collective-permute-done | bytes 16416 | tf_op jit(solution)/shard_map/ppermute | solution.py:153
  54.7 0.2 collective-permute-done.13
  55.0 0.7 fusion.9
  55.7 1.1 %collective-permute-start.18 = (bf16[4,64,128]{2,1,0:T(8,128)(2,1)S(1)}, bf16[4,64,128]{2,1,0:T(8,128)(2,1)S(1)}, u32[]{:S(2)}, u32[]{:S(2)}) collective-permute-start(bf16[4,64,128]{2,1,0:T(8,128)(2,1)S(1)} %get-tuple-element.31), channel_id=1, source_target_pairs={{0,6},{2,4},{4,2},{6,0},{8,14},{10,12},{12,10},{14,8},{16,22},{18,... | collective-permute-start | bytes 196616 | tf_op jit(solution)/shard_map/ppermute | solution.py:153
  56.8 1.1 %collective-permute-start.17 = (bf16[4,64,128]{2,1,0:T(8,128)(2,1)S(1)}, bf16[4,64,128]{2,1,0:T(8,128)(2,1)S(1)}, u32[]{:S(2)}, u32[]{:S(2)}) collective-permute-start(bf16[4,64,128]{2,1,0:T(8,128)(2,1)S(1)} %get-tuple-element.31), channel_id=1, source_target_pairs={{0,4},{2,6},{4,0},{6,2},{8,12},{10,14},{12,8},{14,10},{16,20},{18,... | collective-permute-start | bytes 196616 | tf_op jit(solution)/shard_map/ppermute | solution.py:153
  57.9 1.4 %collective-permute-start.16 = (bf16[4,64,128]{2,1,0:T(8,128)(2,1)S(1)}, bf16[4,64,128]{2,1,0:T(8,128)(2,1)S(1)}, u32[]{:S(2)}, u32[]{:S(2)}) collective-permute-start(bf16[4,64,128]{2,1,0:T(8,128)(2,1)S(1)} %get-tuple-element.31), channel_id=1, source_target_pairs={{0,2},{2,0},{4,6},{6,4},{8,10},{10,8},{12,14},{14,12},{16,18},{18,... | collective-permute-start | bytes 196616 | tf_op jit(solution)/shard_map/ppermute | solution.py:153
  59.2 1.7 %collective-permute-done.18 = bf16[4,64,128]{2,1,0:T(8,128)(2,1)S(1)} collective-permute-done((bf16[4,64,128]{2,1,0:T(8,128)(2,1)S(1)}, bf16[4,64,128]{2,1,0:T(8,128)(2,1)S(1)}, u32[]{:S(2)}, u32[]{:S(2)}) %collective-permute-start.18) | collective-permute-done | bytes 65568 | tf_op jit(solution)/shard_map/ppermute | solution.py:153
  61.0 0.6 collective-permute-done.17
  61.6 0.5 collective-permute-done.16
  62.2 0.6 gather_fusion
  62.8 0.7 copy_bitcast_fusion.pieces
  63.6 4.4 %scores.1.own = f32[64,1024]{1,0:T(8,128)} custom-call(bf16[64,2048]{1,0:T(8,128)(2,1)} %copy_bitcast_fusion.pieces, bf16[1024,2048]{1,0:T(8,128)(2,1)} %get-tuple-element.10.x), custom_call_target="tpu_custom_call" | custom-call | tf_op jit(solution)/shard_map/scores/pallas_call | solution.py:223
  67.9 1.7 %collective-permute-done.19.other = f32[64,1024]{1,0:T(8,128)S(1)} collective-permute-done((f32[64,1024]{1,0:T(8,128)}, f32[64,1024]{1,0:T(8,128)S(1)}, u32[]{:S(2)}, u32[]{:S(2)}) %collective-permute-start.19) | collective-permute-done | bytes 262176 | tf_op jit(solution)/shard_map/ppermute | solution.py:196
  69.7 0.7 copy-done.1
  70.3 4.0 %share.3 = (f32[16,64,128]{2,1,0:T(8,128)}, f32[64,64]{1,0:T(8,128)}, f32[64,1024]{1,0:T(8,128)}) custom-call(s32[1]{0:T(128)} %bitcast.me, f32[64,1024]{1,0:T(8,128)} %scores.1.own, f32[64,1024]{1,0:T(8,128)} %copy-done.1, bf16[1024,2048]{1,0:T(8,128)(2,1)} %get-tuple-element.10.x), custom_call_target="tpu_custom_call" | custom-call | tf_op jit(solution)/shard_map/share/pallas_call | solution.py:201
  74.3 1.9 %collective-permute-start.22 = (f32[64,64]{1,0:T(8,128)}, f32[64,64]{1,0:T(8,128)S(1)}, u32[]{:S(2)}, u32[]{:S(2)}) collective-permute-start(f32[64,64]{1,0:T(8,128)} %get-tuple-element.13), channel_id=1, source_target_pairs={{0,6},{2,4},{4,2},{6,0},{8,14},{10,12},{12,10},{14,8},{16,22},{18,... | collective-permute-start | bytes 49160 | tf_op jit(solution)/shard_map/ppermute | solution.py:153
  76.2 0.9 collective-permute-start.21
  77.2 0.7 collective-permute-start.20
  77.8 1.1 %slice_bitcast_fusion.2 = (f32[4,64,128]{2,1,0:T(8,128)S(1)}, f32[4,64,128]{2,1,0:T(8,128)S(1)}, f32[4,64,128]{2,1,0:T(8,128)S(1)}) fusion(f32[4,4,64,128]{3,2,1,0:T(8,128)} %bitcast.101), kind=kLoop, calls=%fused_computation.5 | loop fusion | bytes 786432 | tf_op jit(solution)/shard_map/squeeze | solution.py:161
  78.9 1.4 %collective-permute-start.26 = (f32[4,64,128]{2,1,0:T(8,128)S(1)}, f32[4,64,128]{2,1,0:T(8,128)S(1)}, u32[]{:S(2)}, u32[]{:S(2)}) collective-permute-start(f32[4,64,128]{2,1,0:T(8,128)S(1)} %get-tuple-element.16), channel_id=1, source_target_pairs={{0,2},{2,0},{4,6},{6,4},{8,10},{10,8},{12,14},{14,12},{16,18},{18,... | collective-permute-start | bytes 393224 | tf_op jit(solution)/shard_map/ppermute | solution.py:153
  80.3 1.1 %collective-permute-start.27 = (f32[4,64,128]{2,1,0:T(8,128)S(1)}, f32[4,64,128]{2,1,0:T(8,128)S(1)}, u32[]{:S(2)}, u32[]{:S(2)}) collective-permute-start(f32[4,64,128]{2,1,0:T(8,128)S(1)} %get-tuple-element.17), channel_id=1, source_target_pairs={{0,4},{2,6},{4,0},{6,2},{8,12},{10,14},{12,8},{14,10},{16,20},{18,... | collective-permute-start | bytes 393224 | tf_op jit(solution)/shard_map/ppermute | solution.py:153
  81.4 1.0 collective-permute-start.28
  82.4 0.8 add_add_fusion.refs_0_
  83.2 1.5 %collective-permute-start.25 = (f32[64,64]{1,0:T(8,128)S(1)}, f32[64,64]{1,0:T(8,128)S(1)}, u32[]{:S(2)}, u32[]{:S(2)}) collective-permute-start(f32[64,64]{1,0:T(8,128)S(1)} %add_add_fusion.refs_0_), channel_id=1, source_target_pairs={{0,24},{2,26},{4,28},{6,30},{8,16},{10,18},{12,20},{14,22},{16,8},... | collective-permute-start | bytes 49160 | tf_op jit(solution)/shard_map/ppermute | solution.py:153
  84.9 3.1 %collective-permute-done.27 = f32[4,64,128]{2,1,0:T(8,128)S(1)} collective-permute-done((f32[4,64,128]{2,1,0:T(8,128)S(1)}, f32[4,64,128]{2,1,0:T(8,128)S(1)}, u32[]{:S(2)}, u32[]{:S(2)}) %collective-permute-start.27) | collective-permute-done | bytes 131104 | tf_op jit(solution)/shard_map/ppermute | solution.py:153
  88.0 0.9 fusion.3
  88.9 0.6 slice_bitcast_fusion.8
  89.5 1.4 %collective-permute-start.31 = (f32[1,64,128]{2,1,0:T(8,128)S(1)}, f32[1,64,128]{2,1,0:T(8,128)S(1)}, u32[]{:S(2)}, u32[]{:S(2)}) collective-permute-start(f32[1,64,128]{2,1,0:T(8,128)S(1)} %get-tuple-element.22), channel_id=1, source_target_pairs={{0,24},{2,26},{4,28},{6,30},{8,16},{10,18},{12,20},{14,22},{16,8},... | collective-permute-start | bytes 98312 | tf_op jit(solution)/shard_map/ppermute | solution.py:153
  90.9 1.0 collective-permute-start.30
  91.9 2.0 %collective-permute-start.29 = (f32[1,64,128]{2,1,0:T(8,128)S(1)}, f32[1,64,128]{2,1,0:T(8,128)S(1)}, u32[]{:S(2)}, u32[]{:S(2)}) collective-permute-start(f32[1,64,128]{2,1,0:T(8,128)S(1)} %get-tuple-element.24), channel_id=1, source_target_pairs={{0,8},{2,10},{4,12},{6,14},{8,0},{10,2},{12,4},{14,6},{16,24},{18,... | collective-permute-start | bytes 98312 | tf_op jit(solution)/shard_map/ppermute | solution.py:153
  93.9 0.9 collective-permute-start.24
  94.8 1.1 %collective-permute-start.23 = (f32[64,64]{1,0:T(8,128)S(1)}, f32[64,64]{1,0:T(8,128)S(1)}, u32[]{:S(2)}, u32[]{:S(2)}) collective-permute-start(f32[64,64]{1,0:T(8,128)S(1)} %add_add_fusion.refs_0_), channel_id=1, source_target_pairs={{0,8},{2,10},{4,12},{6,14},{8,0},{10,2},{12,4},{14,6},{16,24},{18,... | collective-permute-start | bytes 49160 | tf_op jit(solution)/shard_map/ppermute | solution.py:153
  95.9 2.9 %collective-permute-done.24.refs_2_ = f32[64,64]{1,0:T(8,128)S(1)} collective-permute-done((f32[64,64]{1,0:T(8,128)S(1)}, f32[64,64]{1,0:T(8,128)S(1)}, u32[]{:S(2)}, u32[]{:S(2)}) %collective-permute-start.24) | collective-permute-done | bytes 16416 | tf_op jit(solution)/shard_map/ppermute | solution.py:153
  98.8 0.3 collective-permute-done.23.refs_1_
  99.1 0.2 copy-done.11
  99.4 0.3 copy-done.14
  99.7 5.3 %final.1 = (bf16[64,1024]{1,0:T(8,128)(2,1)}, f32[64,128]{1,0:T(8,128)}) custom-call(f32[64,64]{1,0:T(8,128)} %copy-done.2, f32[64,64]{1,0:T(8,128)} %copy-done.14, f32[64,64]{1,0:T(8,128)} %copy-done.11, f32[64,64]{1,0:T(8,128)} %copy-done.4, f32[64,128]{1,0:T(8,128)} %get-tuple-element.25.refs_4_, f32[64,128]{1,0:T(8,128)} %bitcast.115, ...), custom_call_target="tpu_custom_call" | custom-call | tf_op jit(solution)/shard_map/final/pallas_call | solution.py:232
  (53 shorter events, 0.5 us)
Async XLA Ops:
  8.4 1.8 %collective-permute-start = (f32[64,1024]{1,0:T(8,128)}, f32[64,1024]{1,0:T(8,128)S(1)}, u32[]{:S(2)}, u32[]{:S(2)}) collective-permute-start(f32[64,1024]{1,0:T(8,128)} %get-tuple-element.9.own), channel_id=1, source_target_pairs={{0,1},{1,0},{2,3},{3,2},{4,5},{5,4},{6,7},{7,6},{8,9},{9,8},{10,11... | collective-permute-start | bytes 786440 | tf_op jit(solution)/shard_map/ppermute | solution.py:196
  10.2 0.7 copy-start
  14.9 9.1 %collective-permute-start.3 = (f32[64,64]{1,0:T(8,128)}, f32[64,64]{1,0:T(8,128)S(1)}, u32[]{:S(2)}, u32[]{:S(2)}) collective-permute-start(f32[64,64]{1,0:T(8,128)} %get-tuple-element.11), channel_id=1, source_target_pairs={{0,6},{2,4},{4,2},{6,0},{8,14},{10,12},{12,10},{14,8},{16,22},{18,... | collective-permute-start | bytes 49160 | tf_op jit(solution)/shard_map/ppermute | solution.py:153
  18.8 5.3 %collective-permute-start.2 = (f32[64,64]{1,0:T(8,128)}, f32[64,64]{1,0:T(8,128)S(1)}, u32[]{:S(2)}, u32[]{:S(2)}) collective-permute-start(f32[64,64]{1,0:T(8,128)} %get-tuple-element.11), channel_id=1, source_target_pairs={{0,4},{2,6},{4,0},{6,2},{8,12},{10,14},{12,8},{14,10},{16,20},{18,... | collective-permute-start | bytes 49160 | tf_op jit(solution)/shard_map/ppermute | solution.py:153
  19.4 4.7 %collective-permute-start.1 = (f32[64,64]{1,0:T(8,128)}, f32[64,64]{1,0:T(8,128)S(1)}, u32[]{:S(2)}, u32[]{:S(2)}) collective-permute-start(f32[64,64]{1,0:T(8,128)} %get-tuple-element.11), channel_id=1, source_target_pairs={{0,2},{2,0},{4,6},{6,4},{8,10},{10,8},{12,14},{14,12},{16,18},{18,... | collective-permute-start | bytes 49160 | tf_op jit(solution)/shard_map/ppermute | solution.py:153
  20.5 8.4 %collective-permute-start.7 = (f32[4,64,128]{2,1,0:T(8,128)S(1)}, f32[4,64,128]{2,1,0:T(8,128)S(1)}, u32[]{:S(2)}, u32[]{:S(2)}) collective-permute-start(f32[4,64,128]{2,1,0:T(8,128)S(1)} %get-tuple-element.19), channel_id=1, source_target_pairs={{0,2},{2,0},{4,6},{6,4},{8,10},{10,8},{12,14},{14,12},{16,18},{18,... | collective-permute-start | bytes 393224 | tf_op jit(solution)/shard_map/ppermute | solution.py:153
  22.5 7.8 %collective-permute-start.8 = (f32[4,64,128]{2,1,0:T(8,128)S(1)}, f32[4,64,128]{2,1,0:T(8,128)S(1)}, u32[]{:S(2)}, u32[]{:S(2)}) collective-permute-start(f32[4,64,128]{2,1,0:T(8,128)S(1)} %get-tuple-element.20), channel_id=1, source_target_pairs={{0,4},{2,6},{4,0},{6,2},{8,12},{10,14},{12,8},{14,10},{16,20},{18,... | collective-permute-start | bytes 393224 | tf_op jit(solution)/shard_map/ppermute | solution.py:153
  23.9 6.4 %collective-permute-start.9 = (f32[4,64,128]{2,1,0:T(8,128)S(1)}, f32[4,64,128]{2,1,0:T(8,128)S(1)}, u32[]{:S(2)}, u32[]{:S(2)}) collective-permute-start(f32[4,64,128]{2,1,0:T(8,128)S(1)} %get-tuple-element.21), channel_id=1, source_target_pairs={{0,6},{2,4},{4,2},{6,0},{8,14},{10,12},{12,10},{14,8},{16,22},{18,... | collective-permute-start | bytes 393224 | tf_op jit(solution)/shard_map/ppermute | solution.py:153
  24.9 17.2 %copy-start.3 = (f32[64,64]{1,0:T(8,128)}, f32[64,64]{1,0:T(8,128)S(1)}, u32[]{:S(2)}) copy-start(f32[64,64]{1,0:T(8,128)S(1)} %add_add_fusion.1.refs_0_) | copy-start | bytes 49156
  24.9 13.3 %collective-permute-start.6 = (f32[64,64]{1,0:T(8,128)S(1)}, f32[64,64]{1,0:T(8,128)S(1)}, u32[]{:S(2)}, u32[]{:S(2)}) collective-permute-start(f32[64,64]{1,0:T(8,128)S(1)} %add_add_fusion.1.refs_0_), channel_id=1, source_target_pairs={{0,24},{2,26},{4,28},{6,30},{8,16},{10,18},{12,20},{14,22},{16,8},... | collective-permute-start | bytes 49160 | tf_op jit(solution)/shard_map/ppermute | solution.py:153
  31.9 10.2 %collective-permute-start.12 = (f32[1,64,128]{2,1,0:T(8,128)S(1)}, f32[1,64,128]{2,1,0:T(8,128)S(1)}, u32[]{:S(2)}, u32[]{:S(2)}) collective-permute-start(f32[1,64,128]{2,1,0:T(8,128)S(1)} %get-tuple-element.26), channel_id=1, source_target_pairs={{0,24},{2,26},{4,28},{6,30},{8,16},{10,18},{12,20},{14,22},{16,8},... | collective-permute-start | bytes 98312 | tf_op jit(solution)/shard_map/ppermute | solution.py:153
  35.2 6.9 %collective-permute-start.11 = (f32[1,64,128]{2,1,0:T(8,128)S(1)}, f32[1,64,128]{2,1,0:T(8,128)S(1)}, u32[]{:S(2)}, u32[]{:S(2)}) collective-permute-start(f32[1,64,128]{2,1,0:T(8,128)S(1)} %get-tuple-element.27), channel_id=1, source_target_pairs={{0,16},{2,18},{4,20},{6,22},{8,24},{10,26},{12,28},{14,30},{16,0},... | collective-permute-start | bytes 98312 | tf_op jit(solution)/shard_map/ppermute | solution.py:153
  35.2 6.9 %collective-permute-start.10 = (f32[1,64,128]{2,1,0:T(8,128)S(1)}, f32[1,64,128]{2,1,0:T(8,128)S(1)}, u32[]{:S(2)}, u32[]{:S(2)}) collective-permute-start(f32[1,64,128]{2,1,0:T(8,128)S(1)} %get-tuple-element.28), channel_id=1, source_target_pairs={{0,8},{2,10},{4,12},{6,14},{8,0},{10,2},{12,4},{14,6},{16,24},{18,... | collective-permute-start | bytes 98312 | tf_op jit(solution)/shard_map/ppermute | solution.py:153
  36.3 4.8 %collective-permute-start.5 = (f32[64,64]{1,0:T(8,128)S(1)}, f32[64,64]{1,0:T(8,128)S(1)}, u32[]{:S(2)}, u32[]{:S(2)}) collective-permute-start(f32[64,64]{1,0:T(8,128)S(1)} %add_add_fusion.1.refs_0_), channel_id=1, source_target_pairs={{0,16},{2,18},{4,20},{6,22},{8,24},{10,26},{12,28},{14,30},{16,0},... | collective-permute-start | bytes 49160 | tf_op jit(solution)/shard_map/ppermute | solution.py:153
  38.1 4.0 %copy-start.5 = (f32[64,64]{1,0:T(8,128)}, f32[64,64]{1,0:T(8,128)S(1)}, u32[]{:S(2)}) copy-start(f32[64,64]{1,0:T(8,128)S(1)} %collective-permute-done.6.refs_3_) | copy-start | bytes 49156
  38.1 3.9 %collective-permute-start.4 = (f32[64,64]{1,0:T(8,128)S(1)}, f32[64,64]{1,0:T(8,128)S(1)}, u32[]{:S(2)}, u32[]{:S(2)}) collective-permute-start(f32[64,64]{1,0:T(8,128)S(1)} %add_add_fusion.1.refs_0_), channel_id=1, source_target_pairs={{0,8},{2,10},{4,12},{6,14},{8,0},{10,2},{12,4},{14,6},{16,24},{18,... | collective-permute-start | bytes 49160 | tf_op jit(solution)/shard_map/ppermute | solution.py:153
  41.1 1.0 copy-start.13
  42.1 0.6 copy-start.15
  42.1 0.6 copy-start.8
  42.1 0.6 copy-start.10
  42.1 0.6 copy-start.12
  47.5 5.7 %collective-permute-start.15 = (bf16[1,64,128]{2,1,0:T(8,128)(2,1)}, bf16[1,64,128]{2,1,0:T(8,128)(2,1)S(1)}, u32[]{:S(2)}, u32[]{:S(2)}) collective-permute-start(bf16[1,64,128]{2,1,0:T(8,128)(2,1)} %bitcast.105), channel_id=1, source_target_pairs={{0,24},{2,26},{4,28},{6,30},{8,16},{10,18},{12,20},{14,22},{16,8},... | collective-permute-start | bytes 49160 | tf_op jit(solution)/shard_map/ppermute | solution.py:153
  49.9 4.8 %collective-permute-start.14 = (bf16[1,64,128]{2,1,0:T(8,128)(2,1)}, bf16[1,64,128]{2,1,0:T(8,128)(2,1)S(1)}, u32[]{:S(2)}, u32[]{:S(2)}) collective-permute-start(bf16[1,64,128]{2,1,0:T(8,128)(2,1)} %bitcast.106), channel_id=1, source_target_pairs={{0,16},{2,18},{4,20},{6,22},{8,24},{10,26},{12,28},{14,30},{16,0},... | collective-permute-start | bytes 49160 | tf_op jit(solution)/shard_map/ppermute | solution.py:153
  51.0 3.9 %collective-permute-start.13 = (bf16[1,64,128]{2,1,0:T(8,128)(2,1)}, bf16[1,64,128]{2,1,0:T(8,128)(2,1)S(1)}, u32[]{:S(2)}, u32[]{:S(2)}) collective-permute-start(bf16[1,64,128]{2,1,0:T(8,128)(2,1)} %bitcast.107), channel_id=1, source_target_pairs={{0,8},{2,10},{4,12},{6,14},{8,0},{10,2},{12,4},{14,6},{16,24},{18,... | collective-permute-start | bytes 49160 | tf_op jit(solution)/shard_map/ppermute | solution.py:153
  55.7 5.3 %collective-permute-start.18 = (bf16[4,64,128]{2,1,0:T(8,128)(2,1)S(1)}, bf16[4,64,128]{2,1,0:T(8,128)(2,1)S(1)}, u32[]{:S(2)}, u32[]{:S(2)}) collective-permute-start(bf16[4,64,128]{2,1,0:T(8,128)(2,1)S(1)} %get-tuple-element.31), channel_id=1, source_target_pairs={{0,6},{2,4},{4,2},{6,0},{8,14},{10,12},{12,10},{14,8},{16,22},{18,... | collective-permute-start | bytes 196616 | tf_op jit(solution)/shard_map/ppermute | solution.py:153
  56.8 4.8 %collective-permute-start.17 = (bf16[4,64,128]{2,1,0:T(8,128)(2,1)S(1)}, bf16[4,64,128]{2,1,0:T(8,128)(2,1)S(1)}, u32[]{:S(2)}, u32[]{:S(2)}) collective-permute-start(bf16[4,64,128]{2,1,0:T(8,128)(2,1)S(1)} %get-tuple-element.31), channel_id=1, source_target_pairs={{0,4},{2,6},{4,0},{6,2},{8,12},{10,14},{12,8},{14,10},{16,20},{18,... | collective-permute-start | bytes 196616 | tf_op jit(solution)/shard_map/ppermute | solution.py:153
  57.9 4.3 %collective-permute-start.16 = (bf16[4,64,128]{2,1,0:T(8,128)(2,1)S(1)}, bf16[4,64,128]{2,1,0:T(8,128)(2,1)S(1)}, u32[]{:S(2)}, u32[]{:S(2)}) collective-permute-start(bf16[4,64,128]{2,1,0:T(8,128)(2,1)S(1)} %get-tuple-element.31), channel_id=1, source_target_pairs={{0,2},{2,0},{4,6},{6,4},{8,10},{10,8},{12,14},{14,12},{16,18},{18,... | collective-permute-start | bytes 196616 | tf_op jit(solution)/shard_map/ppermute | solution.py:153
  67.9 1.7 %collective-permute-start.19 = (f32[64,1024]{1,0:T(8,128)}, f32[64,1024]{1,0:T(8,128)S(1)}, u32[]{:S(2)}, u32[]{:S(2)}) collective-permute-start(f32[64,1024]{1,0:T(8,128)} %scores.1.own), channel_id=1, source_target_pairs={{0,1},{1,0},{2,3},{3,2},{4,5},{5,4},{6,7},{7,6},{8,9},{9,8},{10,11... | collective-permute-start | bytes 786440 | tf_op jit(solution)/shard_map/ppermute | solution.py:196
  69.7 0.7 copy-start.1
  74.3 7.1 %collective-permute-start.22 = (f32[64,64]{1,0:T(8,128)}, f32[64,64]{1,0:T(8,128)S(1)}, u32[]{:S(2)}, u32[]{:S(2)}) collective-permute-start(f32[64,64]{1,0:T(8,128)} %get-tuple-element.13), channel_id=1, source_target_pairs={{0,6},{2,4},{4,2},{6,0},{8,14},{10,12},{12,10},{14,8},{16,22},{18,... | collective-permute-start | bytes 49160 | tf_op jit(solution)/shard_map/ppermute | solution.py:153
  76.2 6.2 %collective-permute-start.21 = (f32[64,64]{1,0:T(8,128)}, f32[64,64]{1,0:T(8,128)S(1)}, u32[]{:S(2)}, u32[]{:S(2)}) collective-permute-start(f32[64,64]{1,0:T(8,128)} %get-tuple-element.13), channel_id=1, source_target_pairs={{0,4},{2,6},{4,0},{6,2},{8,12},{10,14},{12,8},{14,10},{16,20},{18,... | collective-permute-start | bytes 49160 | tf_op jit(solution)/shard_map/ppermute | solution.py:153
  77.2 5.3 %collective-permute-start.20 = (f32[64,64]{1,0:T(8,128)}, f32[64,64]{1,0:T(8,128)S(1)}, u32[]{:S(2)}, u32[]{:S(2)}) collective-permute-start(f32[64,64]{1,0:T(8,128)} %get-tuple-element.13), channel_id=1, source_target_pairs={{0,2},{2,0},{4,6},{6,4},{8,10},{10,8},{12,14},{14,12},{16,18},{18,... | collective-permute-start | bytes 49160 | tf_op jit(solution)/shard_map/ppermute | solution.py:153
  78.9 6.0 %collective-permute-start.26 = (f32[4,64,128]{2,1,0:T(8,128)S(1)}, f32[4,64,128]{2,1,0:T(8,128)S(1)}, u32[]{:S(2)}, u32[]{:S(2)}) collective-permute-start(f32[4,64,128]{2,1,0:T(8,128)S(1)} %get-tuple-element.16), channel_id=1, source_target_pairs={{0,2},{2,0},{4,6},{6,4},{8,10},{10,8},{12,14},{14,12},{16,18},{18,... | collective-permute-start | bytes 393224 | tf_op jit(solution)/shard_map/ppermute | solution.py:153
  80.3 7.7 %collective-permute-start.27 = (f32[4,64,128]{2,1,0:T(8,128)S(1)}, f32[4,64,128]{2,1,0:T(8,128)S(1)}, u32[]{:S(2)}, u32[]{:S(2)}) collective-permute-start(f32[4,64,128]{2,1,0:T(8,128)S(1)} %get-tuple-element.17), channel_id=1, source_target_pairs={{0,4},{2,6},{4,0},{6,2},{8,12},{10,14},{12,8},{14,10},{16,20},{18,... | collective-permute-start | bytes 393224 | tf_op jit(solution)/shard_map/ppermute | solution.py:153
  81.4 6.6 %collective-permute-start.28 = (f32[4,64,128]{2,1,0:T(8,128)S(1)}, f32[4,64,128]{2,1,0:T(8,128)S(1)}, u32[]{:S(2)}, u32[]{:S(2)}) collective-permute-start(f32[4,64,128]{2,1,0:T(8,128)S(1)} %get-tuple-element.18), channel_id=1, source_target_pairs={{0,6},{2,4},{4,2},{6,0},{8,14},{10,12},{12,10},{14,8},{16,22},{18,... | collective-permute-start | bytes 393224 | tf_op jit(solution)/shard_map/ppermute | solution.py:153
  83.2 15.9 %copy-start.2 = (f32[64,64]{1,0:T(8,128)}, f32[64,64]{1,0:T(8,128)S(1)}, u32[]{:S(2)}) copy-start(f32[64,64]{1,0:T(8,128)S(1)} %add_add_fusion.refs_0_) | copy-start | bytes 49156
  83.2 11.6 %collective-permute-start.25 = (f32[64,64]{1,0:T(8,128)S(1)}, f32[64,64]{1,0:T(8,128)S(1)}, u32[]{:S(2)}, u32[]{:S(2)}) collective-permute-start(f32[64,64]{1,0:T(8,128)S(1)} %add_add_fusion.refs_0_), channel_id=1, source_target_pairs={{0,24},{2,26},{4,28},{6,30},{8,16},{10,18},{12,20},{14,22},{16,8},... | collective-permute-start | bytes 49160 | tf_op jit(solution)/shard_map/ppermute | solution.py:153
  89.5 9.6 %collective-permute-start.31 = (f32[1,64,128]{2,1,0:T(8,128)S(1)}, f32[1,64,128]{2,1,0:T(8,128)S(1)}, u32[]{:S(2)}, u32[]{:S(2)}) collective-permute-start(f32[1,64,128]{2,1,0:T(8,128)S(1)} %get-tuple-element.22), channel_id=1, source_target_pairs={{0,24},{2,26},{4,28},{6,30},{8,16},{10,18},{12,20},{14,22},{16,8},... | collective-permute-start | bytes 98312 | tf_op jit(solution)/shard_map/ppermute | solution.py:153
  90.9 8.1 %collective-permute-start.30 = (f32[1,64,128]{2,1,0:T(8,128)S(1)}, f32[1,64,128]{2,1,0:T(8,128)S(1)}, u32[]{:S(2)}, u32[]{:S(2)}) collective-permute-start(f32[1,64,128]{2,1,0:T(8,128)S(1)} %get-tuple-element.23), channel_id=1, source_target_pairs={{0,16},{2,18},{4,20},{6,22},{8,24},{10,26},{12,28},{14,30},{16,0},... | collective-permute-start | bytes 98312 | tf_op jit(solution)/shard_map/ppermute | solution.py:153
  91.9 7.2 %collective-permute-start.29 = (f32[1,64,128]{2,1,0:T(8,128)S(1)}, f32[1,64,128]{2,1,0:T(8,128)S(1)}, u32[]{:S(2)}, u32[]{:S(2)}) collective-permute-start(f32[1,64,128]{2,1,0:T(8,128)S(1)} %get-tuple-element.24), channel_id=1, source_target_pairs={{0,8},{2,10},{4,12},{6,14},{8,0},{10,2},{12,4},{14,6},{16,24},{18,... | collective-permute-start | bytes 98312 | tf_op jit(solution)/shard_map/ppermute | solution.py:153
  93.9 4.8 %collective-permute-start.24 = (f32[64,64]{1,0:T(8,128)S(1)}, f32[64,64]{1,0:T(8,128)S(1)}, u32[]{:S(2)}, u32[]{:S(2)}) collective-permute-start(f32[64,64]{1,0:T(8,128)S(1)} %add_add_fusion.refs_0_), channel_id=1, source_target_pairs={{0,16},{2,18},{4,20},{6,22},{8,24},{10,26},{12,28},{14,30},{16,0},... | collective-permute-start | bytes 49160 | tf_op jit(solution)/shard_map/ppermute | solution.py:153
  94.8 4.3 %copy-start.4 = (f32[64,64]{1,0:T(8,128)}, f32[64,64]{1,0:T(8,128)S(1)}, u32[]{:S(2)}) copy-start(f32[64,64]{1,0:T(8,128)S(1)} %collective-permute-done.25.refs_3_) | copy-start | bytes 49156
  94.8 4.2 %collective-permute-start.23 = (f32[64,64]{1,0:T(8,128)S(1)}, f32[64,64]{1,0:T(8,128)S(1)}, u32[]{:S(2)}, u32[]{:S(2)}) collective-permute-start(f32[64,64]{1,0:T(8,128)S(1)} %add_add_fusion.refs_0_), channel_id=1, source_target_pairs={{0,8},{2,10},{4,12},{6,14},{8,0},{10,2},{12,4},{14,6},{16,24},{18,... | collective-permute-start | bytes 49160 | tf_op jit(solution)/shard_map/ppermute | solution.py:153
  98.8 0.6 copy-start.11
  99.1 0.6 copy-start.14
  99.1 0.6 copy-start.6
  99.1 0.6 copy-start.7
  99.1 0.6 copy-start.9

commit v2 on v1

--- a/solution.py
+++ b/solution.py
@@ -67,31 +67,71 @@
     s_ref[...] = dot(pieces[...], x[...], NT)
 
 
+def scores_parts_kernel(count, me, *refs):
+    parts, (x, s_ref, held) = refs[:count], refs[count:]
+    _, _, wide = parts[0].shape
+    for d in range(count):
+        for a in range(parts[d].shape[0]):
+            q = jnp.bitwise_xor(me[0], a * count + d)
+            held[:, pl.ds(pl.multiple_of(q * wide, wide), wide)] = parts[d][a]
+    s_ref[...] = dot(held[...], x[...], NT)
+
+
+def product(total, x):
+    k = total.shape[0]
+    high = total.astype(BF)
+    low = (total - high.astype(F32)).astype(BF)
+    both = jnp.concatenate([high, low], axis=0)
+    y = dot(both, x, NN)
+    g = dot(both, high, NT)
+    h = dot(both, low, NT)
+    return y[:k] + y[k:], (g[:k] + (g[k:] + h[:k])) + h[k:]
+
+
 def share_kernel(me, own, other, x, y_ref, gram_ref, total_ref=None):
     total = own[...] + other[...]
     if total_ref is not None:
         total_ref[...] = total
-    k = total.shape[0]
-    high = total.astype(BF)
-    low = (total - high.astype(F32)).astype(BF)
-    both = jnp.concatenate([high, low], axis=0)
-    g = dot(both, high, NT)
-    h = dot(both, low, NT)
-    gram_ref[...] = (g[:k] + (g[k:] + h[:k])) + h[k:]
-    y = dot(both, x[...], NN)
-    y = y[:k] + y[k:]
-    if len(y_ref.shape) == 2:
-        y_ref[...] = y
-    else:
-        n, _, wide = y_ref.shape
-        for q in range(n):
-            y_ref[jnp.bitwise_xor(me[0], q)] = y[:, q * wide : (q + 1) * wide]
-
-
-def lower_inverse(gram, block=8):
+    y_ref[...], gram_ref[...] = product(total, x[...])
+
+
+def packed_kernel(n, count, keep, me, own, other, x, *refs):
+    outs, y_ref = refs[:count], refs[-1]
+    total = own[...] + other[...]
+    if keep:
+        refs[count][...] = total
+    y, gram = product(total, x[...])
+    k = gram.shape[0]
+    wide = y_ref.shape[2]
+    for q in range(n):
+        y_ref[q] = y[:, q * wide : (q + 1) * wide]
+    eye = (lax.broadcasted_iota(jnp.int32, (k, k), 0) == lax.broadcasted_iota(jnp.int32, (k, k), 1)).astype(F32)
+    tail = jnp.concatenate([gram, eye * (1.0 / n)], axis=1)
+    left = n // count
+    for d in range(count):
+        for a in range(left):
+            outs[d][a] = y_ref[jnp.bitwise_xor(me[0], a * count + d)]
+        outs[d][left] = tail
+
+
+def mid_kernel(parts, count, *refs):
+    sources, outs = refs[:parts], refs[parts:]
+    left = (sources[0].shape[0] - 1) // count
+    tail = added([s.at[left * count] for s in sources])
+    for d in range(count):
+        for a in range(left):
+            outs[d][a] = added([s.at[a * count + d] for s in sources])
+        outs[d][left] = tail
+
+
+def with_identity(gram):
     k = gram.shape[0]
     eye = (lax.broadcasted_iota(jnp.int32, (k, k), 0) == lax.broadcasted_iota(jnp.int32, (k, k), 1)).astype(F32)
-    rest = jnp.concatenate([gram, eye], axis=1)
+    return jnp.concatenate([gram, eye], axis=1)
+
+
+def lower_inverse(rest, block=8):
+    k = rest.shape[0]
     wide = rest.shape[1]
     ids = lax.broadcasted_iota(jnp.int32, (block, wide), 0)
     done = []
@@ -126,16 +166,21 @@
     return total
 
 
-def basis_kernel(parts, *refs):
-    grams, pieces, out = refs[:parts], refs[parts : 2 * parts], refs[-1]
-    out[...] = solve(lower_inverse(added(grams)), added(pieces)).astype(BF)
-
-
-def final_kernel(parts, scale, *refs):
-    grams, pieces = refs[:parts], refs[parts : 2 * parts]
-    total, basis_ref, load_ref = refs[2 * parts :]
-    factor = lower_inverse(added(grams))
-    load_ref[...] = solve(factor, added(pieces))
+def gathered(parts, packed, refs):
+    if packed:
+        return added([r.at[1] for r in refs[:parts]]), added([r.at[0] for r in refs[:parts]]), refs[parts:]
+    return with_identity(added(refs[:parts])), added(refs[parts : 2 * parts]), refs[2 * parts :]
+
+
+def basis_kernel(parts, packed, *refs):
+    gram, piece, (out,) = gathered(parts, packed, refs)
+    out[...] = solve(lower_inverse(gram), piece).astype(BF)
+
+
+def final_kernel(parts, packed, scale, *refs):
+    gram, piece, (total, basis_ref, load_ref) = gathered(parts, packed, refs)
+    factor = lower_inverse(gram)
+    load_ref[...] = solve(factor, piece)
     basis_ref[...] = (solve(factor, total[...]) * scale).astype(BF)
 
 
@@ -166,11 +211,11 @@
 
 
 def gather(piece, n):
-    whole = piece[None]
+    parts = [piece[None]]
     for step, count in reversed(stages_of(n)):
+        whole = jnp.stack(parts, axis=1).reshape((-1,) + piece.shape)
         parts = [whole] + [hop(whole, d * step, n) for d in range(1, count)]
-        whole = jnp.stack(parts, axis=1).reshape((-1,) + piece.shape)
-    return whole
+    return parts
 
 
 def local(tiles, tile_row, tile_col, tile_count, start_basis):
@@ -180,7 +225,6 @@
     k, genes = start_basis.shape
     cells = ROW_BLOCKS * tile
     wide = genes // n
-    aligned = wide % 128 == 0
     me_ref = me.reshape(1)
 
     x, half = pl.pallas_call(
@@ -192,50 +236,84 @@
         name="dense",
     )(tile_row, tile_col, tile_count, tiles[0], start_basis)
 
+    stages = stages_of(n)
+    packed = wide == tile and 2 * k == wide
+
     def share(half, keep):
         other = lax.ppermute(half, "gene", [(0, 1), (1, 0)])
-        y_shape = (n, k, wide) if aligned else (k, genes)
-        shapes = [jax.ShapeDtypeStruct(y_shape, F32), jax.ShapeDtypeStruct((k, k), F32)]
-        if keep:
-            shapes.append(jax.ShapeDtypeStruct((k, cells), F32))
-        y, gram, *total = pl.pallas_call(
-            share_kernel,
-            out_shape=tuple(shapes),
-            in_specs=[SMEM, VMEM, VMEM, VMEM],
-            out_specs=(VMEM,) * len(shapes),
-            name="share",
-        )(me_ref, half, other, x)
-        if not aligned:
+        kept = [jax.ShapeDtypeStruct((k, cells), F32)] * keep
+        if not packed:
+            shapes = [jax.ShapeDtypeStruct((k, genes), F32), jax.ShapeDtypeStruct((k, k), F32)] + kept
+            y, gram, *total = pl.pallas_call(
+                share_kernel,
+                out_shape=tuple(shapes),
+                in_specs=[SMEM, VMEM, VMEM, VMEM],
+                out_specs=(VMEM,) * len(shapes),
+                name="share",
+            )(me_ref, half, other, x)
             y = jnp.transpose(y.reshape(k, n, wide), (1, 0, 2))[jnp.arange(n) ^ me]
-        grams, pieces = reduce_both(y, gram, n)
-        return grams, pieces, total
-
-    grams, pieces, _ = share(half, False)
+            grams, pieces = reduce_both(y, gram, n)
+            return grams + pieces, total
+        left = n
+        for at, (step, count) in enumerate(stages):
+            left = left // count
+            shapes = [jax.ShapeDtypeStruct((left + 1, k, wide), F32)] * count
+            if at == 0:
+                outs = pl.pallas_call(
+                    functools.partial(packed_kernel, n, count, keep),
+                    out_shape=tuple(shapes + kept),
+                    in_specs=[SMEM, VMEM, VMEM, VMEM],
+                    out_specs=(VMEM,) * (count + keep),
+                    scratch_shapes=[pltpu.VMEM((n, k, wide), F32)],
+                    name="share",
+                )(me_ref, half, other, x)
+                total = outs[count:]
+            else:
+                outs = pl.pallas_call(
+                    functools.partial(mid_kernel, len(parts), count),
+                    out_shape=tuple(shapes),
+                    in_specs=[VMEM] * len(parts),
+                    out_specs=(VMEM,) * count,
+                    name="mid",
+                )(*parts)
+            parts = [outs[0]] + [hop(outs[d], d * step, n) for d in range(1, count)]
+        return parts, total
+
+    parts, _ = share(half, 0)
+    last = stages[-1][1]
     piece = pl.pallas_call(
-        functools.partial(basis_kernel, len(grams)),
+        functools.partial(basis_kernel, last, packed),
         out_shape=jax.ShapeDtypeStruct((k, wide), BF),
-        in_specs=[VMEM] * (2 * len(grams)),
+        in_specs=[VMEM] * len(parts),
         out_specs=VMEM,
         name="basis",
-    )(*grams, *pieces)
-    whole = gather(piece, n)[jnp.arange(n) ^ me]
-    basis = jnp.transpose(whole, (1, 0, 2)).reshape(k, genes)
-    half = pl.pallas_call(
-        scores_kernel,
-        out_shape=jax.ShapeDtypeStruct((k, cells), F32),
-        in_specs=[VMEM, VMEM],
-        out_specs=VMEM,
-        name="scores",
-    )(basis, x)
-    grams, pieces, (total,) = share(half, True)
+    )(*parts)
+    parts = gather(piece, n)
+    half_shape = jax.ShapeDtypeStruct((k, cells), F32)
+    if packed:
+        half = pl.pallas_call(
+            functools.partial(scores_parts_kernel, len(parts)),
+            out_shape=half_shape,
+            in_specs=[SMEM] + [VMEM] * (len(parts) + 1),
+            out_specs=VMEM,
+            scratch_shapes=[pltpu.VMEM((k, genes), BF)],
+            name="scores",
+        )(me_ref, *parts, x)
+    else:
+        whole = jnp.stack(parts, axis=1).reshape(n, k, wide)[jnp.arange(n) ^ me]
+        basis = jnp.transpose(whole, (1, 0, 2)).reshape(k, genes)
+        half = pl.pallas_call(
+            scores_kernel, out_shape=half_shape, in_specs=[VMEM, VMEM], out_specs=VMEM, name="scores"
+        )(basis, x)
+    parts, (total,) = share(half, 1)
     scale = float(n * cells) ** 0.5
     return pl.pallas_call(
-        functools.partial(final_kernel, len(grams), scale),
+        functools.partial(final_kernel, last, packed, scale),
         out_shape=(jax.ShapeDtypeStruct((k, cells), BF), jax.ShapeDtypeStruct((k, wide), F32)),
-        in_specs=[VMEM] * (2 * len(grams) + 1),
+        in_specs=[VMEM] * (len(parts) + 1),
         out_specs=(VMEM, VMEM),
         name="final",
-    )(*grams, *pieces, total)
+    )(*parts, total)
 
 
 def solution(mesh):

time: 106 us -> 101 us (0.953)
  starting transfers between devices: 43.5 us -> 25.5 us
  waiting for transfers between devices: 19.1 us -> 34.7 us
  Pallas kernels: 29.6 us -> 33.4 us
  other arithmetic: 4.21 us -> 0.73 us
  local copies, waits for them, and re-layouts: 7.25 us -> 4.77 us
    ppermute x30 -> x18, starting transfers between devices: 43.3 us -> 24.8 us  [hop(): return lax.ppermute(value, 'cell', [(i, i ^ distance) for i in range(n)])]
    ppermute x30 -> x18, waiting for transfers between devices: 15.8 us -> 31.6 us  [hop(): return lax.ppermute(value, 'cell', [(i, i ^ distance) for i in range(n)])]
    pallas_call x5 -> x7, Pallas kernels: 22.5 us -> 26.6 us  [the longest x2 8.3 us: share(): pl.pallas_call(functools.partial(packed_kernel, n, count, keep), out_shap...]
    squeeze x4 -> x0, local copies, waits for them, and re-layouts: 3.33 us -> none  [reduce_both(): pieces = [y[:, 0]] + [hop(y[:, d], d * step, n) for d in range(1, count)]]
    unnamed x32 -> x36, local copies, waits for them, and re-layouts: 2.56 us -> 4.77 us
    add x2 -> x0, other arithmetic: 1.54 us -> none  [reduce_both(): y, gram = (sum(pieces[1:], pieces[0]), sum(grams[1:], grams[0]))]
    reshape x2 -> x1, other arithmetic: 1.89 us -> 0.73 us  [gather(): whole = jnp.stack(parts, axis=1).reshape((-1,) + piece.shape)]
  transfers between devices with their start and end apart: 32 -> 20, of which waited for: 15 -> 18; matrix products, arithmetic and copies ran while one was open for 6% -> 0% of each run, Pallas kernels for 0% -> 0%
where the time goes in v2:
time: 101 us; the launch traced here: 100 us
  waiting for transfers between devices  34.7 us (34%)
  Pallas kernels  33.4 us (33%)
  starting transfers between devices  25.5 us (25%)
  local copies, waits for them, and re-layouts  4.77 us (5%)
  between operations  1.35 us (1%)
    ppermute x18, waiting for transfers between devices, hop(): return lax.ppermute(value, 'cell', [(i, i ^ distance) for i in range(n)])  31.6 us
    ppermute x18, starting transfers between devices, hop(): return lax.ppermute(value, 'cell', [(i, i ^ distance) for i in range(n)])  24.8 us
    pallas_call x2, Pallas kernels, share(): pl.pallas_call(functools.partial(packed_kernel, n, count, keep), out_shap...  8.3 us
    pallas_call x1, Pallas kernels, local(): pl.pallas_call(dense_kernel, out_shape=(jax.ShapeDtypeStruct((cells, gene...  6.79 us
    pallas_call x1, Pallas kernels, local(): pl.pallas_call(functools.partial(final_kernel, last, packed, scale), out_...  5.25 us
    pallas_call x1, Pallas kernels, local(): pl.pallas_call(functools.partial(basis_kernel, last, packed), out_shape=j...  4.82 us
    unnamed x36, local copies, waits for them, and re-layouts  4.77 us
    pallas_call x1, Pallas kernels, local(): pl.pallas_call(functools.partial(scores_parts_kernel, len(parts)), out_sh...  4.46 us
  transfers between devices with their start and end apart: 20, of which 18 were waited for; matrix products, arithmetic and copies ran while one was open for 0% of the time, Pallas kernels for 0%

profile of v2, /device:TPU:0, one launch (start us, length us, event | category | flops | bytes accessed | tf_op | source)
XLA Modules:
  0.0 100.4 jit_solution(11923460311460518462)
XLA Ops:
  1.3 6.8 %dense.1 = (bf16[1024,2048]{1,0:T(8,128)(2,1)}, f32[64,1024]{1,0:T(8,128)}) custom-call(s32[1,64]{1,0:T(1,128)} %row.1, s32[1,64]{1,0:T(1,128)} %col.1, s32[1,1]{1,0:T(1,128)S(6)} %copy.7.count, bf16[64,128,128]{2,1,0:T(8,128)(2,1)} %bitcast.9, bf16[64,2048]{1,0:T(8,128)(2,1)} %basis.2), custom_call_target="tpu_custom_call" | custom-call | tf_op jit(solution)/shard_map/dense/pallas_call | solution.py:230
  8.1 0.7 collective-permute-start
  8.8 1.4 %collective-permute-done.other = f32[64,1024]{1,0:T(8,128)S(1)} collective-permute-done((f32[64,1024]{1,0:T(8,128)}, f32[64,1024]{1,0:T(8,128)S(1)}, u32[]{:S(2)}, u32[]{:S(2)}) %collective-permute-start) | collective-permute-done | bytes 262176 | tf_op jit(solution)/shard_map/ppermute | solution.py:243
  10.1 0.7 copy-done.1
  10.8 4.1 %share.2 = (f32[5,64,128]{2,1,0:T(8,128)}, f32[5,64,128]{2,1,0:T(8,128)}, f32[5,64,128]{2,1,0:T(8,128)}, f32[5,64,128]{2,1,0:T(8,128)}) custom-call(s32[1]{0:T(128)} %bitcast.me, f32[64,1024]{1,0:T(8,128)} %get-tuple-element.21.own, f32[64,1024]{1,0:T(8,128)} %copy-done.1, bf16[1024,2048]{1,0:T(8,128)(2,1)} %get-tuple-element.22.x.refs_4_), custom_call_target="tpu_custom_call" | custom-call | tf_op jit(solution)/shard_map/share/pallas_call | solution.py:262
  15.0 3.1 %collective-permute-start.1 = (f32[5,64,128]{2,1,0:T(8,128)}, f32[5,64,128]{2,1,0:T(8,128)S(1)}, u32[]{:S(2)}, u32[]{:S(2)}) collective-permute-start(f32[5,64,128]{2,1,0:T(8,128)} %get-tuple-element.24), channel_id=1, source_target_pairs={{0,2},{2,0},{4,6},{6,4},{8,10},{10,8},{12,14},{14,12},{16,18},{18,... | collective-permute-start | bytes 491528 | tf_op jit(solution)/shard_map/ppermute | solution.py:198
  18.1 1.4 %collective-permute-start.2 = (f32[5,64,128]{2,1,0:T(8,128)}, f32[5,64,128]{2,1,0:T(8,128)S(1)}, u32[]{:S(2)}, u32[]{:S(2)}) collective-permute-start(f32[5,64,128]{2,1,0:T(8,128)} %get-tuple-element.25), channel_id=1, source_target_pairs={{0,4},{2,6},{4,0},{6,2},{8,12},{10,14},{12,8},{14,10},{16,20},{18,... | collective-permute-start | bytes 491528 | tf_op jit(solution)/shard_map/ppermute | solution.py:198
  19.5 0.0 collective-permute-start.3
  19.5 3.8 %collective-permute-done.1.refs_1_ = f32[5,64,128]{2,1,0:T(8,128)S(1)} collective-permute-done((f32[5,64,128]{2,1,0:T(8,128)}, f32[5,64,128]{2,1,0:T(8,128)S(1)}, u32[]{:S(2)}, u32[]{:S(2)}) %collective-permute-start.1) | collective-permute-done | bytes 163872 | tf_op jit(solution)/shard_map/ppermute | solution.py:198
  23.3 4.4 %collective-permute-done.2.refs_2_ = f32[5,64,128]{2,1,0:T(8,128)S(1)} collective-permute-done((f32[5,64,128]{2,1,0:T(8,128)}, f32[5,64,128]{2,1,0:T(8,128)S(1)}, u32[]{:S(2)}, u32[]{:S(2)}) %collective-permute-start.2) | collective-permute-done | bytes 163872 | tf_op jit(solution)/shard_map/ppermute | solution.py:198
  27.8 0.0 collective-permute-done.3.refs_3_
  27.8 0.0 copy-done.3
  27.8 0.7 copy-done.5
  28.4 0.1 copy-done.7
  28.5 1.9 %mid.2 = (f32[2,64,128]{2,1,0:T(8,128)}, f32[2,64,128]{2,1,0:T(8,128)}, f32[2,64,128]{2,1,0:T(8,128)}, f32[2,64,128]{2,1,0:T(8,128)}) custom-call(f32[5,64,128]{2,1,0:T(8,128)} %get-tuple-element.23.refs_0_, f32[5,64,128]{2,1,0:T(8,128)} %copy-done.3, f32[5,64,128]{2,1,0:T(8,128)} %copy-done.5, f32[5,64,128]{2,1,0:T(8,128)} %copy-done.7), custom_call_target="tpu_custom_call" | custom-call | tf_op jit(solution)/shard_map/mid/pallas_call | solution.py:272
  30.4 1.4 %collective-permute-start.4 = (f32[2,64,128]{2,1,0:T(8,128)}, f32[2,64,128]{2,1,0:T(8,128)S(1)}, u32[]{:S(2)}, u32[]{:S(2)}) collective-permute-start(f32[2,64,128]{2,1,0:T(8,128)} %get-tuple-element.28), channel_id=1, source_target_pairs={{0,8},{2,10},{4,12},{6,14},{8,0},{10,2},{12,4},{14,6},{16,24},{18,... | collective-permute-start | bytes 196616 | tf_op jit(solution)/shard_map/ppermute | solution.py:198
  31.8 2.5 %collective-permute-start.5 = (f32[2,64,128]{2,1,0:T(8,128)}, f32[2,64,128]{2,1,0:T(8,128)S(1)}, u32[]{:S(2)}, u32[]{:S(2)}) collective-permute-start(f32[2,64,128]{2,1,0:T(8,128)} %get-tuple-element.29), channel_id=1, source_target_pairs={{0,16},{2,18},{4,20},{6,22},{8,24},{10,26},{12,28},{14,30},{16,0},... | collective-permute-start | bytes 196616 | tf_op jit(solution)/shard_map/ppermute | solution.py:198
  34.3 0.5 collective-permute-start.6
  34.8 0.8 collective-permute-done.4.refs_1_
  35.5 3.0 %collective-permute-done.5.refs_2_ = f32[2,64,128]{2,1,0:T(8,128)S(1)} collective-permute-done((f32[2,64,128]{2,1,0:T(8,128)}, f32[2,64,128]{2,1,0:T(8,128)S(1)}, u32[]{:S(2)}, u32[]{:S(2)}) %collective-permute-start.5) | collective-permute-done | bytes 65568 | tf_op jit(solution)/shard_map/ppermute | solution.py:198
  38.6 2.0 %collective-permute-done.6.refs_3_ = f32[2,64,128]{2,1,0:T(8,128)S(1)} collective-permute-done((f32[2,64,128]{2,1,0:T(8,128)}, f32[2,64,128]{2,1,0:T(8,128)S(1)}, u32[]{:S(2)}, u32[]{:S(2)}) %collective-permute-start.6) | collective-permute-done | bytes 65568 | tf_op jit(solution)/shard_map/ppermute | solution.py:198
  40.5 0.0 copy-done.12
  40.6 0.0 copy-done.13
  40.6 0.6 copy-done.14
  41.2 4.8 %basis.3 = bf16[64,128]{1,0:T(8,128)(2,1)} custom-call(f32[2,64,128]{2,1,0:T(8,128)} %get-tuple-element.27.refs_0_, f32[2,64,128]{2,1,0:T(8,128)} %copy-done.12, f32[2,64,128]{2,1,0:T(8,128)} %copy-done.13, f32[2,64,128]{2,1,0:T(8,128)} %copy-done.14), custom_call_target="tpu_custom_call" | custom-call | tf_op jit(solution)/shard_map/basis/pallas_call | solution.py:284
  46.0 1.2 %collective-permute-start.9 = (bf16[1,64,128]{2,1,0:T(8,128)(2,1)}, bf16[1,64,128]{2,1,0:T(8,128)(2,1)S(1)}, u32[]{:S(2)}, u32[]{:S(2)}) collective-permute-start(bf16[1,64,128]{2,1,0:T(8,128)(2,1)} %bitcast.10), channel_id=1, source_target_pairs={{0,24},{2,26},{4,28},{6,30},{8,16},{10,18},{12,20},{14,22},{16,8},... | collective-permute-start | bytes 49160 | tf_op jit(solution)/shard_map/ppermute | solution.py:198
  47.2 0.0 collective-permute-start.8
  47.2 3.2 %collective-permute-start.7 = (bf16[1,64,128]{2,1,0:T(8,128)(2,1)}, bf16[1,64,128]{2,1,0:T(8,128)(2,1)S(1)}, u32[]{:S(2)}, u32[]{:S(2)}) collective-permute-start(bf16[1,64,128]{2,1,0:T(8,128)(2,1)} %bitcast.12), channel_id=1, source_target_pairs={{0,8},{2,10},{4,12},{6,14},{8,0},{10,2},{12,4},{14,6},{16,24},{18,... | collective-permute-start | bytes 49160 | tf_op jit(solution)/shard_map/ppermute | solution.py:198
  50.4 1.4 %collective-permute-done.9 = bf16[1,64,128]{2,1,0:T(8,128)(2,1)S(1)} collective-permute-done((bf16[1,64,128]{2,1,0:T(8,128)(2,1)}, bf16[1,64,128]{2,1,0:T(8,128)(2,1)S(1)}, u32[]{:S(2)}, u32[]{:S(2)}) %collective-permute-start.9) | collective-permute-done | bytes 16416 | tf_op jit(solution)/shard_map/ppermute | solution.py:198
  51.8 0.4 collective-permute-done.8
  52.1 0.2 collective-permute-done.7
  52.4 0.7 maximum_bitcast_fusion.refs_0_
  53.1 0.0 copy-start
  53.1 1.5 %collective-permute-start.12 = (bf16[4,64,128]{2,1,0:T(8,128)(2,1)S(1)}, bf16[4,64,128]{2,1,0:T(8,128)(2,1)S(1)}, u32[]{:S(2)}, u32[]{:S(2)}) collective-permute-start(bf16[4,64,128]{2,1,0:T(8,128)(2,1)S(1)} %maximum_bitcast_fusion.refs_0_), channel_id=1, source_target_pairs={{0,6},{2,4},{4,2},{6,0},{8,14},{10,12},{12,10},{14,8},{16,22},{18,... | collective-permute-start | bytes 196616 | tf_op jit(solution)/shard_map/ppermute | solution.py:198
  54.6 1.4 %collective-permute-start.11 = (bf16[4,64,128]{2,1,0:T(8,128)(2,1)S(1)}, bf16[4,64,128]{2,1,0:T(8,128)(2,1)S(1)}, u32[]{:S(2)}, u32[]{:S(2)}) collective-permute-start(bf16[4,64,128]{2,1,0:T(8,128)(2,1)S(1)} %maximum_bitcast_fusion.refs_0_), channel_id=1, source_target_pairs={{0,4},{2,6},{4,0},{6,2},{8,12},{10,14},{12,8},{14,10},{16,20},{18,... | collective-permute-start | bytes 196616 | tf_op jit(solution)/shard_map/ppermute | solution.py:198
  56.0 0.7 collective-permute-start.10
  56.6 1.7 %collective-permute-done.12.refs_3_ = bf16[4,64,128]{2,1,0:T(8,128)(2,1)S(1)} collective-permute-done((bf16[4,64,128]{2,1,0:T(8,128)(2,1)S(1)}, bf16[4,64,128]{2,1,0:T(8,128)(2,1)S(1)}, u32[]{:S(2)}, u32[]{:S(2)}) %collective-permute-start.12) | collective-permute-done | bytes 65568 | tf_op jit(solution)/shard_map/ppermute | solution.py:198
  58.3 0.7 collective-permute-done.11.refs_2_
  59.0 1.2 %collective-permute-done.10.refs_1_ = bf16[4,64,128]{2,1,0:T(8,128)(2,1)S(1)} collective-permute-done((bf16[4,64,128]{2,1,0:T(8,128)(2,1)S(1)}, bf16[4,64,128]{2,1,0:T(8,128)(2,1)S(1)}, u32[]{:S(2)}, u32[]{:S(2)}) %collective-permute-start.10) | collective-permute-done | bytes 65568 | tf_op jit(solution)/shard_map/ppermute | solution.py:198
  60.3 0.0 copy-done
  60.3 0.6 copy-done.11
  60.9 4.5 %scores.1.own = f32[64,1024]{1,0:T(8,128)} custom-call(s32[1]{0:T(128)} %bitcast.me, bf16[4,64,128]{2,1,0:T(8,128)(2,1)} %copy-done, bf16[4,64,128]{2,1,0:T(8,128)(2,1)} %copy-done.11, bf16[4,64,128]{2,1,0:T(8,128)(2,1)} %copy-done.10, bf16[4,64,128]{2,1,0:T(8,128)(2,1)} %copy-done.9, bf16[1024,2048]{1,0:T(8,128)(2,1)} %get-tuple-element.22.x.refs_4_), custom_call_target="tpu_custom_call" | custom-call | tf_op jit(solution)/shard_map/scores/pallas_call | solution.py:294
  65.3 0.0 collective-permute-start.13
  65.4 1.7 %collective-permute-done.13.other = f32[64,1024]{1,0:T(8,128)S(1)} collective-permute-done((f32[64,1024]{1,0:T(8,128)}, f32[64,1024]{1,0:T(8,128)S(1)}, u32[]{:S(2)}, u32[]{:S(2)}) %collective-permute-start.13) | collective-permute-done | bytes 262176 | tf_op jit(solution)/shard_map/ppermute | solution.py:243
  67.1 0.7 copy-done.2
  67.8 4.2 %share.3 = (f32[5,64,128]{2,1,0:T(8,128)}, f32[5,64,128]{2,1,0:T(8,128)}, f32[5,64,128]{2,1,0:T(8,128)}, f32[5,64,128]{2,1,0:T(8,128)}, f32[64,1024]{1,0:T(8,128)}) custom-call(s32[1]{0:T(128)} %bitcast.me, f32[64,1024]{1,0:T(8,128)} %scores.1.own, f32[64,1024]{1,0:T(8,128)} %copy-done.2, bf16[1024,2048]{1,0:T(8,128)(2,1)} %get-tuple-element.22.x.refs_4_), custom_call_target="tpu_custom_call" | custom-call | tf_op jit(solution)/shard_map/share/pallas_call | solution.py:262
  72.0 0.9 collective-permute-start.14
  73.0 1.4 %collective-permute-start.15 = (f32[5,64,128]{2,1,0:T(8,128)}, f32[5,64,128]{2,1,0:T(8,128)S(1)}, u32[]{:S(2)}, u32[]{:S(2)}) collective-permute-start(f32[5,64,128]{2,1,0:T(8,128)} %get-tuple-element.33), channel_id=1, source_target_pairs={{0,4},{2,6},{4,0},{6,2},{8,12},{10,14},{12,8},{14,10},{16,20},{18,... | collective-permute-start | bytes 491528 | tf_op jit(solution)/shard_map/ppermute | solution.py:198
  74.4 1.1 %collective-permute-start.16 = (f32[5,64,128]{2,1,0:T(8,128)}, f32[5,64,128]{2,1,0:T(8,128)S(1)}, u32[]{:S(2)}, u32[]{:S(2)}) collective-permute-start(f32[5,64,128]{2,1,0:T(8,128)} %get-tuple-element.34), channel_id=1, source_target_pairs={{0,6},{2,4},{4,2},{6,0},{8,14},{10,12},{12,10},{14,8},{16,22},{18,... | collective-permute-start | bytes 491528 | tf_op jit(solution)/shard_map/ppermute | solution.py:198
  75.5 3.8 %collective-permute-done.14.refs_1_ = f32[5,64,128]{2,1,0:T(8,128)S(1)} collective-permute-done((f32[5,64,128]{2,1,0:T(8,128)}, f32[5,64,128]{2,1,0:T(8,128)S(1)}, u32[]{:S(2)}, u32[]{:S(2)}) %collective-permute-start.14) | collective-permute-done | bytes 163872 | tf_op jit(solution)/shard_map/ppermute | solution.py:198
  79.3 3.4 %collective-permute-done.15.refs_2_ = f32[5,64,128]{2,1,0:T(8,128)S(1)} collective-permute-done((f32[5,64,128]{2,1,0:T(8,128)}, f32[5,64,128]{2,1,0:T(8,128)S(1)}, u32[]{:S(2)}, u32[]{:S(2)}) %collective-permute-start.15) | collective-permute-done | bytes 163872 | tf_op jit(solution)/shard_map/ppermute | solution.py:198
  82.6 0.0 collective-permute-done.16.refs_3_
  82.7 0.7 copy-done.6
  83.3 0.1 copy-done.8
  83.4 1.9 %mid.3 = (f32[2,64,128]{2,1,0:T(8,128)}, f32[2,64,128]{2,1,0:T(8,128)}, f32[2,64,128]{2,1,0:T(8,128)}, f32[2,64,128]{2,1,0:T(8,128)}) custom-call(f32[5,64,128]{2,1,0:T(8,128)} %get-tuple-element.31.refs_0_, f32[5,64,128]{2,1,0:T(8,128)} %copy-done.4, f32[5,64,128]{2,1,0:T(8,128)} %copy-done.6, f32[5,64,128]{2,1,0:T(8,128)} %copy-done.8), custom_call_target="tpu_custom_call" | custom-call | tf_op jit(solution)/shard_map/mid/pallas_call | solution.py:272
  85.2 2.0 %collective-permute-start.17 = (f32[2,64,128]{2,1,0:T(8,128)}, f32[2,64,128]{2,1,0:T(8,128)S(1)}, u32[]{:S(2)}, u32[]{:S(2)}) collective-permute-start(f32[2,64,128]{2,1,0:T(8,128)} %get-tuple-element.36), channel_id=1, source_target_pairs={{0,8},{2,10},{4,12},{6,14},{8,0},{10,2},{12,4},{14,6},{16,24},{18,... | collective-permute-start | bytes 196616 | tf_op jit(solution)/shard_map/ppermute | solution.py:198
  87.2 0.9 collective-permute-start.18
  88.1 1.5 %collective-permute-start.19 = (f32[2,64,128]{2,1,0:T(8,128)}, f32[2,64,128]{2,1,0:T(8,128)S(1)}, u32[]{:S(2)}, u32[]{:S(2)}) collective-permute-start(f32[2,64,128]{2,1,0:T(8,128)} %get-tuple-element.38), channel_id=1, source_target_pairs={{0,24},{2,26},{4,28},{6,30},{8,16},{10,18},{12,20},{14,22},{16,8},... | collective-permute-start | bytes 196616 | tf_op jit(solution)/shard_map/ppermute | solution.py:198
  89.6 0.1 collective-permute-done.17.refs_1_
  89.8 4.0 %collective-permute-done.18.refs_2_ = f32[2,64,128]{2,1,0:T(8,128)S(1)} collective-permute-done((f32[2,64,128]{2,1,0:T(8,128)}, f32[2,64,128]{2,1,0:T(8,128)S(1)}, u32[]{:S(2)}, u32[]{:S(2)}) %collective-permute-start.18) | collective-permute-done | bytes 65568 | tf_op jit(solution)/shard_map/ppermute | solution.py:198
  93.8 0.7 collective-permute-done.19.refs_3_
  94.5 0.0 copy-done.16
  94.5 0.6 copy-done.17
  95.1 5.3 %final.1 = (bf16[64,1024]{1,0:T(8,128)(2,1)}, f32[64,128]{1,0:T(8,128)}) custom-call(f32[2,64,128]{2,1,0:T(8,128)} %get-tuple-element.35.refs_0_, f32[2,64,128]{2,1,0:T(8,128)} %copy-done.15, f32[2,64,128]{2,1,0:T(8,128)} %copy-done.16, f32[2,64,128]{2,1,0:T(8,128)} %copy-done.17, f32[64,1024]{1,0:T(8,128)} %get-tuple-element.39.refs_4_), custom_call_target="tpu_custom_call" | custom-call | tf_op jit(solution)/shard_map/final/pallas_call | solution.py:310
  (21 shorter events, 0.0 us)
Async XLA Ops:
  8.1 2.1 %collective-permute-start = (f32[64,1024]{1,0:T(8,128)}, f32[64,1024]{1,0:T(8,128)S(1)}, u32[]{:S(2)}, u32[]{:S(2)}) collective-permute-start(f32[64,1024]{1,0:T(8,128)} %get-tuple-element.21.own), channel_id=1, source_target_pairs={{0,1},{1,0},{2,3},{3,2},{4,5},{5,4},{6,7},{7,6},{8,9},{9,8},{10,11... | collective-permute-start | bytes 786440 | tf_op jit(solution)/shard_map/ppermute | solution.py:243
  10.1 0.7 copy-start.1
  15.0 8.4 %collective-permute-start.1 = (f32[5,64,128]{2,1,0:T(8,128)}, f32[5,64,128]{2,1,0:T(8,128)S(1)}, u32[]{:S(2)}, u32[]{:S(2)}) collective-permute-start(f32[5,64,128]{2,1,0:T(8,128)} %get-tuple-element.24), channel_id=1, source_target_pairs={{0,2},{2,0},{4,6},{6,4},{8,10},{10,8},{12,14},{14,12},{16,18},{18,... | collective-permute-start | bytes 491528 | tf_op jit(solution)/shard_map/ppermute | solution.py:198
  18.1 9.7 %collective-permute-start.2 = (f32[5,64,128]{2,1,0:T(8,128)}, f32[5,64,128]{2,1,0:T(8,128)S(1)}, u32[]{:S(2)}, u32[]{:S(2)}) collective-permute-start(f32[5,64,128]{2,1,0:T(8,128)} %get-tuple-element.25), channel_id=1, source_target_pairs={{0,4},{2,6},{4,0},{6,2},{8,12},{10,14},{12,8},{14,10},{16,20},{18,... | collective-permute-start | bytes 491528 | tf_op jit(solution)/shard_map/ppermute | solution.py:198
  19.5 8.3 %collective-permute-start.3 = (f32[5,64,128]{2,1,0:T(8,128)}, f32[5,64,128]{2,1,0:T(8,128)S(1)}, u32[]{:S(2)}, u32[]{:S(2)}) collective-permute-start(f32[5,64,128]{2,1,0:T(8,128)} %get-tuple-element.26), channel_id=1, source_target_pairs={{0,6},{2,4},{4,2},{6,0},{8,14},{10,12},{12,10},{14,8},{16,22},{18,... | collective-permute-start | bytes 491528 | tf_op jit(solution)/shard_map/ppermute | solution.py:198
  23.3 4.4 %copy-start.3 = (f32[5,64,128]{2,1,0:T(8,128)}, f32[5,64,128]{2,1,0:T(8,128)S(1)}, u32[]{:S(2)}) copy-start(f32[5,64,128]{2,1,0:T(8,128)S(1)} %collective-permute-done.1.refs_1_) | copy-start | bytes 491524
  27.8 0.7 copy-start.5
  27.8 0.7 copy-start.7
  30.4 5.2 %collective-permute-start.4 = (f32[2,64,128]{2,1,0:T(8,128)}, f32[2,64,128]{2,1,0:T(8,128)S(1)}, u32[]{:S(2)}, u32[]{:S(2)}) collective-permute-start(f32[2,64,128]{2,1,0:T(8,128)} %get-tuple-element.28), channel_id=1, source_target_pairs={{0,8},{2,10},{4,12},{6,14},{8,0},{10,2},{12,4},{14,6},{16,24},{18,... | collective-permute-start | bytes 196616 | tf_op jit(solution)/shard_map/ppermute | solution.py:198
  31.8 6.8 %collective-permute-start.5 = (f32[2,64,128]{2,1,0:T(8,128)}, f32[2,64,128]{2,1,0:T(8,128)S(1)}, u32[]{:S(2)}, u32[]{:S(2)}) collective-permute-start(f32[2,64,128]{2,1,0:T(8,128)} %get-tuple-element.29), channel_id=1, source_target_pairs={{0,16},{2,18},{4,20},{6,22},{8,24},{10,26},{12,28},{14,30},{16,0},... | collective-permute-start | bytes 196616 | tf_op jit(solution)/shard_map/ppermute | solution.py:198
  34.3 6.3 %collective-permute-start.6 = (f32[2,64,128]{2,1,0:T(8,128)}, f32[2,64,128]{2,1,0:T(8,128)S(1)}, u32[]{:S(2)}, u32[]{:S(2)}) collective-permute-start(f32[2,64,128]{2,1,0:T(8,128)} %get-tuple-element.30), channel_id=1, source_target_pairs={{0,24},{2,26},{4,28},{6,30},{8,16},{10,18},{12,20},{14,22},{16,8},... | collective-permute-start | bytes 196616 | tf_op jit(solution)/shard_map/ppermute | solution.py:198
  35.5 5.0 %copy-start.12 = (f32[2,64,128]{2,1,0:T(8,128)}, f32[2,64,128]{2,1,0:T(8,128)S(1)}, u32[]{:S(2)}) copy-start(f32[2,64,128]{2,1,0:T(8,128)S(1)} %collective-permute-done.4.refs_1_) | copy-start | bytes 196612
  38.6 2.0 %copy-start.13 = (f32[2,64,128]{2,1,0:T(8,128)}, f32[2,64,128]{2,1,0:T(8,128)S(1)}, u32[]{:S(2)}) copy-start(f32[2,64,128]{2,1,0:T(8,128)S(1)} %collective-permute-done.5.refs_2_) | copy-start | bytes 196612
  40.5 0.6 copy-start.14
  46.0 5.7 %collective-permute-start.9 = (bf16[1,64,128]{2,1,0:T(8,128)(2,1)}, bf16[1,64,128]{2,1,0:T(8,128)(2,1)S(1)}, u32[]{:S(2)}, u32[]{:S(2)}) collective-permute-start(bf16[1,64,128]{2,1,0:T(8,128)(2,1)} %bitcast.10), channel_id=1, source_target_pairs={{0,24},{2,26},{4,28},{6,30},{8,16},{10,18},{12,20},{14,22},{16,8},... | collective-permute-start | bytes 49160 | tf_op jit(solution)/shard_map/ppermute | solution.py:198
  47.2 4.9 %collective-permute-start.8 = (bf16[1,64,128]{2,1,0:T(8,128)(2,1)}, bf16[1,64,128]{2,1,0:T(8,128)(2,1)S(1)}, u32[]{:S(2)}, u32[]{:S(2)}) collective-permute-start(bf16[1,64,128]{2,1,0:T(8,128)(2,1)} %bitcast.11), channel_id=1, source_target_pairs={{0,16},{2,18},{4,20},{6,22},{8,24},{10,26},{12,28},{14,30},{16,0},... | collective-permute-start | bytes 49160 | tf_op jit(solution)/shard_map/ppermute | solution.py:198
  47.2 5.2 %collective-permute-start.7 = (bf16[1,64,128]{2,1,0:T(8,128)(2,1)}, bf16[1,64,128]{2,1,0:T(8,128)(2,1)S(1)}, u32[]{:S(2)}, u32[]{:S(2)}) collective-permute-start(bf16[1,64,128]{2,1,0:T(8,128)(2,1)} %bitcast.12), channel_id=1, source_target_pairs={{0,8},{2,10},{4,12},{6,14},{8,0},{10,2},{12,4},{14,6},{16,24},{18,... | collective-permute-start | bytes 49160 | tf_op jit(solution)/shard_map/ppermute | solution.py:198
  53.1 7.2 %copy-start = (bf16[4,64,128]{2,1,0:T(8,128)(2,1)}, bf16[4,64,128]{2,1,0:T(8,128)(2,1)S(1)}, u32[]{:S(2)}) copy-start(bf16[4,64,128]{2,1,0:T(8,128)(2,1)S(1)} %maximum_bitcast_fusion.refs_0_) | copy-start | bytes 196612
  53.1 5.2 %collective-permute-start.12 = (bf16[4,64,128]{2,1,0:T(8,128)(2,1)S(1)}, bf16[4,64,128]{2,1,0:T(8,128)(2,1)S(1)}, u32[]{:S(2)}, u32[]{:S(2)}) collective-permute-start(bf16[4,64,128]{2,1,0:T(8,128)(2,1)S(1)} %maximum_bitcast_fusion.refs_0_), channel_id=1, source_target_pairs={{0,6},{2,4},{4,2},{6,0},{8,14},{10,12},{12,10},{14,8},{16,22},{18,... | collective-permute-start | bytes 196616 | tf_op jit(solution)/shard_map/ppermute | solution.py:198
  54.6 4.4 %collective-permute-start.11 = (bf16[4,64,128]{2,1,0:T(8,128)(2,1)S(1)}, bf16[4,64,128]{2,1,0:T(8,128)(2,1)S(1)}, u32[]{:S(2)}, u32[]{:S(2)}) collective-permute-start(bf16[4,64,128]{2,1,0:T(8,128)(2,1)S(1)} %maximum_bitcast_fusion.refs_0_), channel_id=1, source_target_pairs={{0,4},{2,6},{4,0},{6,2},{8,12},{10,14},{12,8},{14,10},{16,20},{18,... | collective-permute-start | bytes 196616 | tf_op jit(solution)/shard_map/ppermute | solution.py:198
  56.0 4.3 %collective-permute-start.10 = (bf16[4,64,128]{2,1,0:T(8,128)(2,1)S(1)}, bf16[4,64,128]{2,1,0:T(8,128)(2,1)S(1)}, u32[]{:S(2)}, u32[]{:S(2)}) collective-permute-start(bf16[4,64,128]{2,1,0:T(8,128)(2,1)S(1)} %maximum_bitcast_fusion.refs_0_), channel_id=1, source_target_pairs={{0,2},{2,0},{4,6},{6,4},{8,10},{10,8},{12,14},{14,12},{16,18},{18,... | collective-permute-start | bytes 196616 | tf_op jit(solution)/shard_map/ppermute | solution.py:198
  58.3 1.9 %copy-start.9 = (bf16[4,64,128]{2,1,0:T(8,128)(2,1)}, bf16[4,64,128]{2,1,0:T(8,128)(2,1)S(1)}, u32[]{:S(2)}) copy-start(bf16[4,64,128]{2,1,0:T(8,128)(2,1)S(1)} %collective-permute-done.12.refs_3_) | copy-start | bytes 196612
  59.0 1.2 %copy-start.10 = (bf16[4,64,128]{2,1,0:T(8,128)(2,1)}, bf16[4,64,128]{2,1,0:T(8,128)(2,1)S(1)}, u32[]{:S(2)}) copy-start(bf16[4,64,128]{2,1,0:T(8,128)(2,1)S(1)} %collective-permute-done.11.refs_2_) | copy-start | bytes 196612
  60.3 0.6 copy-start.11
  65.3 1.7 %collective-permute-start.13 = (f32[64,1024]{1,0:T(8,128)}, f32[64,1024]{1,0:T(8,128)S(1)}, u32[]{:S(2)}, u32[]{:S(2)}) collective-permute-start(f32[64,1024]{1,0:T(8,128)} %scores.1.own), channel_id=1, source_target_pairs={{0,1},{1,0},{2,3},{3,2},{4,5},{5,4},{6,7},{7,6},{8,9},{9,8},{10,11... | collective-permute-start | bytes 786440 | tf_op jit(solution)/shard_map/ppermute | solution.py:243
  67.1 0.7 copy-start.2
  72.0 7.3 %collective-permute-start.14 = (f32[5,64,128]{2,1,0:T(8,128)}, f32[5,64,128]{2,1,0:T(8,128)S(1)}, u32[]{:S(2)}, u32[]{:S(2)}) collective-permute-start(f32[5,64,128]{2,1,0:T(8,128)} %get-tuple-element.32), channel_id=1, source_target_pairs={{0,2},{2,0},{4,6},{6,4},{8,10},{10,8},{12,14},{14,12},{16,18},{18,... | collective-permute-start | bytes 491528 | tf_op jit(solution)/shard_map/ppermute | solution.py:198
  73.0 9.7 %collective-permute-start.15 = (f32[5,64,128]{2,1,0:T(8,128)}, f32[5,64,128]{2,1,0:T(8,128)S(1)}, u32[]{:S(2)}, u32[]{:S(2)}) collective-permute-start(f32[5,64,128]{2,1,0:T(8,128)} %get-tuple-element.33), channel_id=1, source_target_pairs={{0,4},{2,6},{4,0},{6,2},{8,12},{10,14},{12,8},{14,10},{16,20},{18,... | collective-permute-start | bytes 491528 | tf_op jit(solution)/shard_map/ppermute | solution.py:198
  74.4 8.3 %collective-permute-start.16 = (f32[5,64,128]{2,1,0:T(8,128)}, f32[5,64,128]{2,1,0:T(8,128)S(1)}, u32[]{:S(2)}, u32[]{:S(2)}) collective-permute-start(f32[5,64,128]{2,1,0:T(8,128)} %get-tuple-element.34), channel_id=1, source_target_pairs={{0,6},{2,4},{4,2},{6,0},{8,14},{10,12},{12,10},{14,8},{16,22},{18,... | collective-permute-start | bytes 491528 | tf_op jit(solution)/shard_map/ppermute | solution.py:198
  79.3 3.4 %copy-start.4 = (f32[5,64,128]{2,1,0:T(8,128)}, f32[5,64,128]{2,1,0:T(8,128)S(1)}, u32[]{:S(2)}) copy-start(f32[5,64,128]{2,1,0:T(8,128)S(1)} %collective-permute-done.14.refs_1_) | copy-start | bytes 491524
  82.6 0.7 copy-start.6
  82.7 0.7 copy-start.8
  85.2 4.5 %collective-permute-start.17 = (f32[2,64,128]{2,1,0:T(8,128)}, f32[2,64,128]{2,1,0:T(8,128)S(1)}, u32[]{:S(2)}, u32[]{:S(2)}) collective-permute-start(f32[2,64,128]{2,1,0:T(8,128)} %get-tuple-element.36), channel_id=1, source_target_pairs={{0,8},{2,10},{4,12},{6,14},{8,0},{10,2},{12,4},{14,6},{16,24},{18,... | collective-permute-start | bytes 196616 | tf_op jit(solution)/shard_map/ppermute | solution.py:198
  87.2 6.5 %collective-permute-start.18 = (f32[2,64,128]{2,1,0:T(8,128)}, f32[2,64,128]{2,1,0:T(8,128)S(1)}, u32[]{:S(2)}, u32[]{:S(2)}) collective-permute-start(f32[2,64,128]{2,1,0:T(8,128)} %get-tuple-element.37), channel_id=1, source_target_pairs={{0,16},{2,18},{4,20},{6,22},{8,24},{10,26},{12,28},{14,30},{16,0},... | collective-permute-start | bytes 196616 | tf_op jit(solution)/shard_map/ppermute | solution.py:198
  88.1 6.4 %collective-permute-start.19 = (f32[2,64,128]{2,1,0:T(8,128)}, f32[2,64,128]{2,1,0:T(8,128)S(1)}, u32[]{:S(2)}, u32[]{:S(2)}) collective-permute-start(f32[2,64,128]{2,1,0:T(8,128)} %get-tuple-element.38), channel_id=1, source_target_pairs={{0,24},{2,26},{4,28},{6,30},{8,16},{10,18},{12,20},{14,22},{16,8},... | collective-permute-start | bytes 196616 | tf_op jit(solution)/shard_map/ppermute | solution.py:198
  89.8 4.8 %copy-start.15 = (f32[2,64,128]{2,1,0:T(8,128)}, f32[2,64,128]{2,1,0:T(8,128)S(1)}, u32[]{:S(2)}) copy-start(f32[2,64,128]{2,1,0:T(8,128)S(1)} %collective-permute-done.17.refs_1_) | copy-start | bytes 196612
  93.8 0.7 copy-start.16
  94.5 0.6 copy-start.17

commit v3 on v2

--- a/solution.py
+++ b/solution.py
@@ -17,6 +17,9 @@
 VMEM = pl.BlockSpec(memory_space=pltpu.VMEM)
 SMEM = pl.BlockSpec(memory_space=pltpu.SMEM)
 ANY = pl.BlockSpec(memory_space=pl.ANY)
+
+
+PARAMS = pltpu.CompilerParams(vmem_limit_bytes=24 * 1024 * 1024)
 
 
 def dot(a, b, dims, precision=None):
@@ -229,10 +232,11 @@
 
     x, half = pl.pallas_call(
         dense_kernel,
-        out_shape=(jax.ShapeDtypeStruct((cells, genes), BF), jax.ShapeDtypeStruct((k, cells), F32)),
+        out_shape=(pltpu.VMEM((cells, genes), BF), jax.ShapeDtypeStruct((k, cells), F32)),
         in_specs=[SMEM, SMEM, SMEM, ANY, VMEM],
         out_specs=(VMEM, VMEM),
         scratch_shapes=[pltpu.SMEM((ROW_BLOCKS * (genes // tile),), jnp.int32), pltpu.SemaphoreType.DMA((slots,))],
+        compiler_params=PARAMS,
         name="dense",
     )(tile_row, tile_col, tile_count, tiles[0], start_basis)
 
@@ -249,6 +253,7 @@
                 out_shape=tuple(shapes),
                 in_specs=[SMEM, VMEM, VMEM, VMEM],
                 out_specs=(VMEM,) * len(shapes),
+                compiler_params=PARAMS,
                 name="share",
             )(me_ref, half, other, x)
             y = jnp.transpose(y.reshape(k, n, wide), (1, 0, 2))[jnp.arange(n) ^ me]
@@ -265,6 +270,7 @@
                     in_specs=[SMEM, VMEM, VMEM, VMEM],
                     out_specs=(VMEM,) * (count + keep),
                     scratch_shapes=[pltpu.VMEM((n, k, wide), F32)],
+                    compiler_params=PARAMS,
                     name="share",
                 )(me_ref, half, other, x)
                 total = outs[count:]
@@ -274,6 +280,7 @@
                     out_shape=tuple(shapes),
                     in_specs=[VMEM] * len(parts),
                     out_specs=(VMEM,) * count,
+                    compiler_params=PARAMS,
                     name="mid",
                 )(*parts)
             parts = [outs[0]] + [hop(outs[d], d * step, n) for d in range(1, count)]
@@ -286,6 +293,7 @@
         out_shape=jax.ShapeDtypeStruct((k, wide), BF),
         in_specs=[VMEM] * len(parts),
         out_specs=VMEM,
+        compiler_params=PARAMS,
         name="basis",
     )(*parts)
     parts = gather(piece, n)
@@ -297,13 +305,14 @@
             in_specs=[SMEM] + [VMEM] * (len(parts) + 1),
             out_specs=VMEM,
             scratch_shapes=[pltpu.VMEM((k, genes), BF)],
+            compiler_params=PARAMS,
             name="scores",
         )(me_ref, *parts, x)
     else:
         whole = jnp.stack(parts, axis=1).reshape(n, k, wide)[jnp.arange(n) ^ me]
         basis = jnp.transpose(whole, (1, 0, 2)).reshape(k, genes)
         half = pl.pallas_call(
-            scores_kernel, out_shape=half_shape, in_specs=[VMEM, VMEM], out_specs=VMEM, name="scores"
+            scores_kernel, out_shape=half_shape, in_specs=[VMEM, VMEM], out_specs=VMEM, compiler_params=PARAMS, name="scores"
         )(basis, x)
     parts, (total,) = share(half, 1)
     scale = float(n * cells) ** 0.5
@@ -312,6 +321,7 @@
         out_shape=(jax.ShapeDtypeStruct((k, cells), BF), jax.ShapeDtypeStruct((k, wide), F32)),
         in_specs=[VMEM] * (len(parts) + 1),
         out_specs=(VMEM, VMEM),
+        compiler_params=PARAMS,
         name="final",
     )(*parts, total)
 

time: 101 us -> 84.9 us (0.84)
  Pallas kernels: 33.4 us -> 16.5 us
  local copies, waits for them, and re-layouts: 4.77 us -> 7.99 us
  waiting for transfers between devices: 34.7 us -> 32.9 us
    pallas_call x2, Pallas kernels: 8.3 us -> 1.8 us  [share(): pl.pallas_call(functools.partial(packed_kernel, n, count, keep), out_shap...]
    pallas_call x2, Pallas kernels: 3.73 us -> 0.07 us  [share(): pl.pallas_call(functools.partial(mid_kernel, len(parts), count), out_shap...]
    unnamed x36 -> x14, local copies, waits for them, and re-layouts: 4.77 us -> 7.99 us
    pallas_call x1, Pallas kernels: 4.46 us -> 1.41 us  [local(): pl.pallas_call(functools.partial(scores_parts_kernel, len(parts)), out_sh...]
    pallas_call x1, Pallas kernels: 4.82 us -> 3.21 us  [local(): pl.pallas_call(functools.partial(basis_kernel, last, packed), out_shape=j...]
    ppermute x18, waiting for transfers between devices: 31.6 us -> 30.3 us  [hop(): return lax.ppermute(value, 'cell', [(i, i ^ distance) for i in range(n)])]
    pallas_call x1, Pallas kernels: 5.25 us -> 4.16 us  [local(): pl.pallas_call(functools.partial(final_kernel, last, packed, scale), out_...]
  transfers between devices with their start and end apart: 20 -> 20, of which waited for: 18 -> 17; matrix products, arithmetic and copies ran while one was open for 0% -> 0% of each run, Pallas kernels for 0% -> 0%
where the time goes in v3:
time: 84.9 us; the launch traced here: 84.6 us
  waiting for transfers between devices  32.9 us (39%)
  starting transfers between devices  25.7 us (30%)
  Pallas kernels  16.5 us (19%)
  local copies, waits for them, and re-layouts  7.99 us (9%)
  between operations  1.36 us (2%)
    ppermute x18, waiting for transfers between devices, hop(): return lax.ppermute(value, 'cell', [(i, i ^ distance) for i in range(n)])  30.3 us
    ppermute x18, starting transfers between devices, hop(): return lax.ppermute(value, 'cell', [(i, i ^ distance) for i in range(n)])  24.8 us
    unnamed x14, local copies, waits for them, and re-layouts  7.99 us
    pallas_call x1, Pallas kernels, local(): pl.pallas_call(dense_kernel, out_shape=(pltpu.VMEM((cells, genes), BF), j...  5.88 us
    pallas_call x1, Pallas kernels, local(): pl.pallas_call(functools.partial(final_kernel, last, packed, scale), out_...  4.16 us
    pallas_call x1, Pallas kernels, local(): pl.pallas_call(functools.partial(basis_kernel, last, packed), out_shape=j...  3.21 us
    ppermute x2, waiting for transfers between devices, share(): other = lax.ppermute(half, 'gene', [(0, 1), (1, 0)])  2.68 us
    pallas_call x2, Pallas kernels, share(): pl.pallas_call(functools.partial(packed_kernel, n, count, keep), out_shap...  1.8 us
  transfers between devices with their start and end apart: 20, of which 17 were waited for; matrix products, arithmetic and copies ran while one was open for 0% of the time, Pallas kernels for 0%

profile of v3, /device:TPU:0, one launch (start us, length us, event | category | flops | bytes accessed | tf_op | source)
XLA Modules:
  0.0 84.6 jit_solution(13331852607177903246)
XLA Ops:
  1.3 0.0 copy-start.3
  1.3 1.6 %copy-done.3 = bf16[1,64,128,128]{3,2,1,0:T(8,128)(2,1)S(1)} copy-done((bf16[1,64,128,128]{3,2,1,0:T(8,128)(2,1)S(1)}, bf16[1,64,128,128]{3,2,1,0:T(8,128)(2,1)}, u32[]{:S(2)}) %copy-start.3) | copy-done | bytes 2097176
  2.9 0.0 copy-start.4
  2.9 0.9 %copy-done.4 = bf16[64,2048]{1,0:T(8,128)(2,1)S(1)} copy-done((bf16[64,2048]{1,0:T(8,128)(2,1)S(1)}, bf16[64,2048]{1,0:T(8,128)(2,1)}, u32[]{:S(2)}) %copy-start.4) | copy-done | bytes 262168
  3.8 0.0 copy-start.5
  3.8 0.7 copy-done.5
  4.5 0.0 copy-start.6
  4.5 0.7 copy-done.6
  5.1 5.9 %dense.1 = (bf16[1024,2048]{1,0:T(8,128)(2,1)S(1)}, f32[64,1024]{1,0:T(8,128)S(1)}) custom-call(s32[1,64]{1,0:T(1,128)S(1)} %copy-done.5, s32[1,64]{1,0:T(1,128)S(1)} %copy-done.6, s32[1,1]{1,0:T(1,128)S(6)} %copy.7.count, bf16[64,128,128]{2,1,0:T(8,128)(2,1)S(1)} %bitcast.9, bf16[64,2048]{1,0:T(8,128)(2,1)S(1)} %copy-done.4), custom_call_target="tpu_custom_call" | custom-call | tf_op jit(solution)/shard_map/dense/pallas_call | solution.py:233
  11.0 0.0 copy-start
  11.0 2.0 %copy-done = bf16[1024,2048]{1,0:T(8,128)(2,1)} copy-done((bf16[1024,2048]{1,0:T(8,128)(2,1)}, bf16[1024,2048]{1,0:T(8,128)(2,1)S(1)}, u32[]{:S(2)}) %copy-start) | copy-done | bytes 4194328
  13.0 0.8 collective-permute-start
  13.8 1.2 %collective-permute-done.other = f32[64,1024]{1,0:T(8,128)S(1)} collective-permute-done((f32[64,1024]{1,0:T(8,128)S(1)}, f32[64,1024]{1,0:T(8,128)S(1)}, u32[]{:S(2)}, u32[]{:S(2)}) %collective-permute-start) | collective-permute-done | bytes 262176 | tf_op jit(solution)/shard_map/ppermute | solution.py:247
  15.0 0.0 copy-start.1
  15.0 2.2 %copy-done.1 = bf16[1024,2048]{1,0:T(8,128)(2,1)S(1)} copy-done((bf16[1024,2048]{1,0:T(8,128)(2,1)S(1)}, bf16[1024,2048]{1,0:T(8,128)(2,1)}, u32[]{:S(2)}) %copy-start.1) | copy-done | bytes 4194328
  17.2 0.0 copy-start.2
  17.2 0.9 %share.2 = (f32[5,64,128]{2,1,0:T(8,128)S(1)}, f32[5,64,128]{2,1,0:T(8,128)S(1)}, f32[5,64,128]{2,1,0:T(8,128)S(1)}, f32[5,64,128]{2,1,0:T(8,128)S(1)}) custom-call(s32[1]{0:T(128)} %bitcast.me, f32[64,1024]{1,0:T(8,128)S(1)} %get-tuple-element.21.own, f32[64,1024]{1,0:T(8,128)S(1)} %collective-permute-done.other, bf16[1024,2048]{1,0:T(8,128)(2,1)S(1)} %copy-done.1), custom_call_target="tpu_custom_call" | custom-call | tf_op jit(solution)/shard_map/share/pallas_call | solution.py:267
  18.1 2.5 %collective-permute-start.1 = (f32[5,64,128]{2,1,0:T(8,128)S(1)}, f32[5,64,128]{2,1,0:T(8,128)S(1)}, u32[]{:S(2)}, u32[]{:S(2)}) collective-permute-start(f32[5,64,128]{2,1,0:T(8,128)S(1)} %get-tuple-element.24), channel_id=1, source_target_pairs={{0,2},{2,0},{4,6},{6,4},{8,10},{10,8},{12,14},{14,12},{16,18},{18,... | collective-permute-start | bytes 491528 | tf_op jit(solution)/shard_map/ppermute | solution.py:201
  20.6 1.7 %collective-permute-start.2 = (f32[5,64,128]{2,1,0:T(8,128)S(1)}, f32[5,64,128]{2,1,0:T(8,128)S(1)}, u32[]{:S(2)}, u32[]{:S(2)}) collective-permute-start(f32[5,64,128]{2,1,0:T(8,128)S(1)} %get-tuple-element.25), channel_id=1, source_target_pairs={{0,4},{2,6},{4,0},{6,2},{8,12},{10,14},{12,8},{14,10},{16,20},{18,... | collective-permute-start | bytes 491528 | tf_op jit(solution)/shard_map/ppermute | solution.py:201
  22.3 0.1 collective-permute-start.3
  22.3 3.3 %collective-permute-done.1.refs_1_ = f32[5,64,128]{2,1,0:T(8,128)S(1)} collective-permute-done((f32[5,64,128]{2,1,0:T(8,128)S(1)}, f32[5,64,128]{2,1,0:T(8,128)S(1)}, u32[]{:S(2)}, u32[]{:S(2)}) %collective-permute-start.1) | collective-permute-done | bytes 163872 | tf_op jit(solution)/shard_map/ppermute | solution.py:201
  25.6 3.6 %collective-permute-done.2.refs_2_ = f32[5,64,128]{2,1,0:T(8,128)S(1)} collective-permute-done((f32[5,64,128]{2,1,0:T(8,128)S(1)}, f32[5,64,128]{2,1,0:T(8,128)S(1)}, u32[]{:S(2)}, u32[]{:S(2)}) %collective-permute-start.2) | collective-permute-done | bytes 163872 | tf_op jit(solution)/shard_map/ppermute | solution.py:201
  29.2 0.8 collective-permute-done.3.refs_3_
  30.1 1.9 %collective-permute-start.4 = (f32[2,64,128]{2,1,0:T(8,128)S(1)}, f32[2,64,128]{2,1,0:T(8,128)S(1)}, u32[]{:S(2)}, u32[]{:S(2)}) collective-permute-start(f32[2,64,128]{2,1,0:T(8,128)S(1)} %get-tuple-element.28), channel_id=1, source_target_pairs={{0,8},{2,10},{4,12},{6,14},{8,0},{10,2},{12,4},{14,6},{16,24},{18,... | collective-permute-start | bytes 196616 | tf_op jit(solution)/shard_map/ppermute | solution.py:201
  32.0 2.4 %collective-permute-start.5 = (f32[2,64,128]{2,1,0:T(8,128)S(1)}, f32[2,64,128]{2,1,0:T(8,128)S(1)}, u32[]{:S(2)}, u32[]{:S(2)}) collective-permute-start(f32[2,64,128]{2,1,0:T(8,128)S(1)} %get-tuple-element.29), channel_id=1, source_target_pairs={{0,16},{2,18},{4,20},{6,22},{8,24},{10,26},{12,28},{14,30},{16,0},... | collective-permute-start | bytes 196616 | tf_op jit(solution)/shard_map/ppermute | solution.py:201
  34.4 0.1 collective-permute-start.6
  34.6 0.0 collective-permute-done.4.refs_1_
  34.6 4.1 %collective-permute-done.5.refs_2_ = f32[2,64,128]{2,1,0:T(8,128)S(1)} collective-permute-done((f32[2,64,128]{2,1,0:T(8,128)S(1)}, f32[2,64,128]{2,1,0:T(8,128)S(1)}, u32[]{:S(2)}, u32[]{:S(2)}) %collective-permute-start.5) | collective-permute-done | bytes 65568 | tf_op jit(solution)/shard_map/ppermute | solution.py:201
  38.6 1.9 %collective-permute-done.6.refs_3_ = f32[2,64,128]{2,1,0:T(8,128)S(1)} collective-permute-done((f32[2,64,128]{2,1,0:T(8,128)S(1)}, f32[2,64,128]{2,1,0:T(8,128)S(1)}, u32[]{:S(2)}, u32[]{:S(2)}) %collective-permute-start.6) | collective-permute-done | bytes 65568 | tf_op jit(solution)/shard_map/ppermute | solution.py:201
  40.5 3.2 %basis.3 = bf16[64,128]{1,0:T(8,128)(2,1)S(1)} custom-call(f32[2,64,128]{2,1,0:T(8,128)S(1)} %get-tuple-element.27.refs_0_, f32[2,64,128]{2,1,0:T(8,128)S(1)} %collective-permute-done.4.refs_1_, f32[2,64,128]{2,1,0:T(8,128)S(1)} %collective-permute-done.5.refs_2_, f32[2,64,128]{2,1,0:T(8,128)S(1)} %collective-permute-done.6.refs_3_), custom_call_target="tpu_custom_call" | custom-call | tf_op jit(solution)/shard_map/basis/pallas_call | solution.py:291
  43.7 1.2 %collective-permute-start.9 = (bf16[1,64,128]{2,1,0:T(8,128)(2,1)S(1)}, bf16[1,64,128]{2,1,0:T(8,128)(2,1)S(1)}, u32[]{:S(2)}, u32[]{:S(2)}) collective-permute-start(bf16[1,64,128]{2,1,0:T(8,128)(2,1)S(1)} %bitcast.10), channel_id=1, source_target_pairs={{0,24},{2,26},{4,28},{6,30},{8,16},{10,18},{12,20},{14,22},{16,8},... | collective-permute-start | bytes 49160 | tf_op jit(solution)/shard_map/ppermute | solution.py:201
  44.9 0.0 collective-permute-start.8
  44.9 3.3 %collective-permute-start.7 = (bf16[1,64,128]{2,1,0:T(8,128)(2,1)S(1)}, bf16[1,64,128]{2,1,0:T(8,128)(2,1)S(1)}, u32[]{:S(2)}, u32[]{:S(2)}) collective-permute-start(bf16[1,64,128]{2,1,0:T(8,128)(2,1)S(1)} %bitcast.12), channel_id=1, source_target_pairs={{0,8},{2,10},{4,12},{6,14},{8,0},{10,2},{12,4},{14,6},{16,24},{18,... | collective-permute-start | bytes 49160 | tf_op jit(solution)/shard_map/ppermute | solution.py:201
  48.2 1.1 %collective-permute-done.9 = bf16[1,64,128]{2,1,0:T(8,128)(2,1)S(1)} collective-permute-done((bf16[1,64,128]{2,1,0:T(8,128)(2,1)S(1)}, bf16[1,64,128]{2,1,0:T(8,128)(2,1)S(1)}, u32[]{:S(2)}, u32[]{:S(2)}) %collective-permute-start.9) | collective-permute-done | bytes 16416 | tf_op jit(solution)/shard_map/ppermute | solution.py:201
  49.3 0.4 collective-permute-done.8
  49.7 0.2 collective-permute-done.7
  49.9 1.6 %collective-permute-start.12 = (bf16[4,64,128]{2,1,0:T(8,128)(2,1)S(1)}, bf16[4,64,128]{2,1,0:T(8,128)(2,1)S(1)}, u32[]{:S(2)}, u32[]{:S(2)}) collective-permute-start(bf16[4,64,128]{2,1,0:T(8,128)(2,1)S(1)} %maximum_bitcast_fusion.refs_0_), channel_id=1, source_target_pairs={{0,6},{2,4},{4,2},{6,0},{8,14},{10,12},{12,10},{14,8},{16,22},{18,... | collective-permute-start | bytes 196616 | tf_op jit(solution)/shard_map/ppermute | solution.py:201
  51.5 1.5 %collective-permute-start.11 = (bf16[4,64,128]{2,1,0:T(8,128)(2,1)S(1)}, bf16[4,64,128]{2,1,0:T(8,128)(2,1)S(1)}, u32[]{:S(2)}, u32[]{:S(2)}) collective-permute-start(bf16[4,64,128]{2,1,0:T(8,128)(2,1)S(1)} %maximum_bitcast_fusion.refs_0_), channel_id=1, source_target_pairs={{0,4},{2,6},{4,0},{6,2},{8,12},{10,14},{12,8},{14,10},{16,20},{18,... | collective-permute-start | bytes 196616 | tf_op jit(solution)/shard_map/ppermute | solution.py:201
  52.9 0.5 collective-permute-start.10
  53.5 1.7 %collective-permute-done.12.refs_3_ = bf16[4,64,128]{2,1,0:T(8,128)(2,1)S(1)} collective-permute-done((bf16[4,64,128]{2,1,0:T(8,128)(2,1)S(1)}, bf16[4,64,128]{2,1,0:T(8,128)(2,1)S(1)}, u32[]{:S(2)}, u32[]{:S(2)}) %collective-permute-start.12) | collective-permute-done | bytes 65568 | tf_op jit(solution)/shard_map/ppermute | solution.py:201
  55.1 0.7 collective-permute-done.11.refs_2_
  55.8 1.4 %collective-permute-done.10.refs_1_ = bf16[4,64,128]{2,1,0:T(8,128)(2,1)S(1)} collective-permute-done((bf16[4,64,128]{2,1,0:T(8,128)(2,1)S(1)}, bf16[4,64,128]{2,1,0:T(8,128)(2,1)S(1)}, u32[]{:S(2)}, u32[]{:S(2)}) %collective-permute-start.10) | collective-permute-done | bytes 65568 | tf_op jit(solution)/shard_map/ppermute | solution.py:201
  57.2 0.0 copy-done.2
  57.2 1.4 %scores.1.own = f32[64,1024]{1,0:T(8,128)S(1)} custom-call(s32[1]{0:T(128)} %bitcast.me, bf16[4,64,128]{2,1,0:T(8,128)(2,1)S(1)} %maximum_bitcast_fusion.refs_0_, bf16[4,64,128]{2,1,0:T(8,128)(2,1)S(1)} %collective-permute-done.10.refs_1_, bf16[4,64,128]{2,1,0:T(8,128)(2,1)S(1)} %collective-permute-done.11.refs_2_, ...), custom_call_target="tpu_custom_call" | custom-call | tf_op jit(solution)/shard_map/scores/pallas_call | solution.py:302
  58.6 0.1 collective-permute-start.13
  58.7 1.5 %collective-permute-done.13.other = f32[64,1024]{1,0:T(8,128)S(1)} collective-permute-done((f32[64,1024]{1,0:T(8,128)S(1)}, f32[64,1024]{1,0:T(8,128)S(1)}, u32[]{:S(2)}, u32[]{:S(2)}) %collective-permute-start.13) | collective-permute-done | bytes 262176 | tf_op jit(solution)/shard_map/ppermute | solution.py:247
  60.2 0.9 %share.3 = (f32[5,64,128]{2,1,0:T(8,128)S(1)}, f32[5,64,128]{2,1,0:T(8,128)S(1)}, f32[5,64,128]{2,1,0:T(8,128)S(1)}, f32[5,64,128]{2,1,0:T(8,128)S(1)}, f32[64,1024]{1,0:T(8,128)S(1)}) custom-call(s32[1]{0:T(128)} %bitcast.me, f32[64,1024]{1,0:T(8,128)S(1)} %scores.1.own, f32[64,1024]{1,0:T(8,128)S(1)} %collective-permute-done.13.other, ...), custom_call_target="tpu_custom_call" | custom-call | tf_op jit(solution)/shard_map/share/pallas_call | solution.py:267
  61.1 0.6 collective-permute-start.14
  61.7 1.7 %collective-permute-start.15 = (f32[5,64,128]{2,1,0:T(8,128)S(1)}, f32[5,64,128]{2,1,0:T(8,128)S(1)}, u32[]{:S(2)}, u32[]{:S(2)}) collective-permute-start(f32[5,64,128]{2,1,0:T(8,128)S(1)} %get-tuple-element.33), channel_id=1, source_target_pairs={{0,4},{2,6},{4,0},{6,2},{8,12},{10,14},{12,8},{14,10},{16,20},{18,... | collective-permute-start | bytes 491528 | tf_op jit(solution)/shard_map/ppermute | solution.py:201
  63.4 1.3 %collective-permute-start.16 = (f32[5,64,128]{2,1,0:T(8,128)S(1)}, f32[5,64,128]{2,1,0:T(8,128)S(1)}, u32[]{:S(2)}, u32[]{:S(2)}) collective-permute-start(f32[5,64,128]{2,1,0:T(8,128)S(1)} %get-tuple-element.34), channel_id=1, source_target_pairs={{0,6},{2,4},{4,2},{6,0},{8,14},{10,12},{12,10},{14,8},{16,22},{18,... | collective-permute-start | bytes 491528 | tf_op jit(solution)/shard_map/ppermute | solution.py:201
  64.7 3.6 %collective-permute-done.14.refs_1_ = f32[5,64,128]{2,1,0:T(8,128)S(1)} collective-permute-done((f32[5,64,128]{2,1,0:T(8,128)S(1)}, f32[5,64,128]{2,1,0:T(8,128)S(1)}, u32[]{:S(2)}, u32[]{:S(2)}) %collective-permute-start.14) | collective-permute-done | bytes 163872 | tf_op jit(solution)/shard_map/ppermute | solution.py:201
  68.3 2.9 %collective-permute-done.15.refs_2_ = f32[5,64,128]{2,1,0:T(8,128)S(1)} collective-permute-done((f32[5,64,128]{2,1,0:T(8,128)S(1)}, f32[5,64,128]{2,1,0:T(8,128)S(1)}, u32[]{:S(2)}, u32[]{:S(2)}) %collective-permute-start.15) | collective-permute-done | bytes 163872 | tf_op jit(solution)/shard_map/ppermute | solution.py:201
  71.2 0.0 collective-permute-done.16.refs_3_
  71.3 2.1 %collective-permute-start.17 = (f32[2,64,128]{2,1,0:T(8,128)S(1)}, f32[2,64,128]{2,1,0:T(8,128)S(1)}, u32[]{:S(2)}, u32[]{:S(2)}) collective-permute-start(f32[2,64,128]{2,1,0:T(8,128)S(1)} %get-tuple-element.36), channel_id=1, source_target_pairs={{0,8},{2,10},{4,12},{6,14},{8,0},{10,2},{12,4},{14,6},{16,24},{18,... | collective-permute-start | bytes 196616 | tf_op jit(solution)/shard_map/ppermute | solution.py:201
  73.3 0.9 %collective-permute-start.18 = (f32[2,64,128]{2,1,0:T(8,128)S(1)}, f32[2,64,128]{2,1,0:T(8,128)S(1)}, u32[]{:S(2)}, u32[]{:S(2)}) collective-permute-start(f32[2,64,128]{2,1,0:T(8,128)S(1)} %get-tuple-element.37), channel_id=1, source_target_pairs={{0,16},{2,18},{4,20},{6,22},{8,24},{10,26},{12,28},{14,30},{16,0},... | collective-permute-start | bytes 196616 | tf_op jit(solution)/shard_map/ppermute | solution.py:201
  74.2 1.5 %collective-permute-start.19 = (f32[2,64,128]{2,1,0:T(8,128)S(1)}, f32[2,64,128]{2,1,0:T(8,128)S(1)}, u32[]{:S(2)}, u32[]{:S(2)}) collective-permute-start(f32[2,64,128]{2,1,0:T(8,128)S(1)} %get-tuple-element.38), channel_id=1, source_target_pairs={{0,24},{2,26},{4,28},{6,30},{8,16},{10,18},{12,20},{14,22},{16,8},... | collective-permute-start | bytes 196616 | tf_op jit(solution)/shard_map/ppermute | solution.py:201
  75.8 0.0 collective-permute-done.17.refs_1_
  75.8 3.9 %collective-permute-done.18.refs_2_ = f32[2,64,128]{2,1,0:T(8,128)S(1)} collective-permute-done((f32[2,64,128]{2,1,0:T(8,128)S(1)}, f32[2,64,128]{2,1,0:T(8,128)S(1)}, u32[]{:S(2)}, u32[]{:S(2)}) %collective-permute-start.18) | collective-permute-done | bytes 65568 | tf_op jit(solution)/shard_map/ppermute | solution.py:201
  79.6 0.8 collective-permute-done.19.refs_3_
  80.4 4.2 %final.1 = (bf16[64,1024]{1,0:T(8,128)(2,1)}, f32[64,128]{1,0:T(8,128)}) custom-call(f32[2,64,128]{2,1,0:T(8,128)S(1)} %get-tuple-element.35.refs_0_, f32[2,64,128]{2,1,0:T(8,128)S(1)} %collective-permute-done.17.refs_1_, f32[2,64,128]{2,1,0:T(8,128)S(1)} %collective-permute-done.18.refs_2_, f32[2,64,128]{2,1,0:T(8,128)S(1)} %collective-permute-done.19.refs_3_, ...), custom_call_target="tpu_custom_call" | custom-call | tf_op jit(solution)/shard_map/final/pallas_call | solution.py:319
  (3 shorter events, 0.1 us)
Async XLA Ops:
  1.3 1.6 %copy-start.3 = (bf16[1,64,128,128]{3,2,1,0:T(8,128)(2,1)S(1)}, bf16[1,64,128,128]{3,2,1,0:T(8,128)(2,1)}, u32[]{:S(2)}) copy-start(bf16[1,64,128,128]{3,2,1,0:T(8,128)(2,1)} %param.5) | copy-start | bytes 6291460
  2.9 0.9 %copy-start.4 = (bf16[64,2048]{1,0:T(8,128)(2,1)S(1)}, bf16[64,2048]{1,0:T(8,128)(2,1)}, u32[]{:S(2)}) copy-start(bf16[64,2048]{1,0:T(8,128)(2,1)} %basis.2) | copy-start | bytes 786436
  3.8 0.7 copy-start.5
  4.5 0.7 copy-start.6
  11.0 2.0 %copy-start = (bf16[1024,2048]{1,0:T(8,128)(2,1)}, bf16[1024,2048]{1,0:T(8,128)(2,1)S(1)}, u32[]{:S(2)}) copy-start(bf16[1024,2048]{1,0:T(8,128)(2,1)S(1)} %get-tuple-element.22.x.refs_4_) | copy-start | bytes 12582916
  13.0 2.0 %collective-permute-start = (f32[64,1024]{1,0:T(8,128)S(1)}, f32[64,1024]{1,0:T(8,128)S(1)}, u32[]{:S(2)}, u32[]{:S(2)}) collective-permute-start(f32[64,1024]{1,0:T(8,128)S(1)} %get-tuple-element.21.own), channel_id=1, source_target_pairs={{0,1},{1,0},{2,3},{3,2},{4,5},{5,4},{6,7},{7,6},{8,9},{9,8},{10,11... | collective-permute-start | bytes 786440 | tf_op jit(solution)/shard_map/ppermute | solution.py:247
  15.0 2.2 %copy-start.1 = (bf16[1024,2048]{1,0:T(8,128)(2,1)S(1)}, bf16[1024,2048]{1,0:T(8,128)(2,1)}, u32[]{:S(2)}) copy-start(bf16[1024,2048]{1,0:T(8,128)(2,1)} %copy-done) | copy-start | bytes 12582916
  17.2 40.0 %copy-start.2 = (bf16[1024,2048]{1,0:T(8,128)(2,1)S(1)}, bf16[1024,2048]{1,0:T(8,128)(2,1)}, u32[]{:S(2)}) copy-start(bf16[1024,2048]{1,0:T(8,128)(2,1)} %copy-done) | copy-start | bytes 12582916
  18.1 7.5 %collective-permute-start.1 = (f32[5,64,128]{2,1,0:T(8,128)S(1)}, f32[5,64,128]{2,1,0:T(8,128)S(1)}, u32[]{:S(2)}, u32[]{:S(2)}) collective-permute-start(f32[5,64,128]{2,1,0:T(8,128)S(1)} %get-tuple-element.24), channel_id=1, source_target_pairs={{0,2},{2,0},{4,6},{6,4},{8,10},{10,8},{12,14},{14,12},{16,18},{18,... | collective-permute-start | bytes 491528 | tf_op jit(solution)/shard_map/ppermute | solution.py:201
  20.6 8.7 %collective-permute-start.2 = (f32[5,64,128]{2,1,0:T(8,128)S(1)}, f32[5,64,128]{2,1,0:T(8,128)S(1)}, u32[]{:S(2)}, u32[]{:S(2)}) collective-permute-start(f32[5,64,128]{2,1,0:T(8,128)S(1)} %get-tuple-element.25), channel_id=1, source_target_pairs={{0,4},{2,6},{4,0},{6,2},{8,12},{10,14},{12,8},{14,10},{16,20},{18,... | collective-permute-start | bytes 491528 | tf_op jit(solution)/shard_map/ppermute | solution.py:201
  22.3 7.8 %collective-permute-start.3 = (f32[5,64,128]{2,1,0:T(8,128)S(1)}, f32[5,64,128]{2,1,0:T(8,128)S(1)}, u32[]{:S(2)}, u32[]{:S(2)}) collective-permute-start(f32[5,64,128]{2,1,0:T(8,128)S(1)} %get-tuple-element.26), channel_id=1, source_target_pairs={{0,6},{2,4},{4,2},{6,0},{8,14},{10,12},{12,10},{14,8},{16,22},{18,... | collective-permute-start | bytes 491528 | tf_op jit(solution)/shard_map/ppermute | solution.py:201
  30.1 4.5 %collective-permute-start.4 = (f32[2,64,128]{2,1,0:T(8,128)S(1)}, f32[2,64,128]{2,1,0:T(8,128)S(1)}, u32[]{:S(2)}, u32[]{:S(2)}) collective-permute-start(f32[2,64,128]{2,1,0:T(8,128)S(1)} %get-tuple-element.28), channel_id=1, source_target_pairs={{0,8},{2,10},{4,12},{6,14},{8,0},{10,2},{12,4},{14,6},{16,24},{18,... | collective-permute-start | bytes 196616 | tf_op jit(solution)/shard_map/ppermute | solution.py:201
  32.0 6.6 %collective-permute-start.5 = (f32[2,64,128]{2,1,0:T(8,128)S(1)}, f32[2,64,128]{2,1,0:T(8,128)S(1)}, u32[]{:S(2)}, u32[]{:S(2)}) collective-permute-start(f32[2,64,128]{2,1,0:T(8,128)S(1)} %get-tuple-element.29), channel_id=1, source_target_pairs={{0,16},{2,18},{4,20},{6,22},{8,24},{10,26},{12,28},{14,30},{16,0},... | collective-permute-start | bytes 196616 | tf_op jit(solution)/shard_map/ppermute | solution.py:201
  34.4 6.1 %collective-permute-start.6 = (f32[2,64,128]{2,1,0:T(8,128)S(1)}, f32[2,64,128]{2,1,0:T(8,128)S(1)}, u32[]{:S(2)}, u32[]{:S(2)}) collective-permute-start(f32[2,64,128]{2,1,0:T(8,128)S(1)} %get-tuple-element.30), channel_id=1, source_target_pairs={{0,24},{2,26},{4,28},{6,30},{8,16},{10,18},{12,20},{14,22},{16,8},... | collective-permute-start | bytes 196616 | tf_op jit(solution)/shard_map/ppermute | solution.py:201
  43.7 5.6 %collective-permute-start.9 = (bf16[1,64,128]{2,1,0:T(8,128)(2,1)S(1)}, bf16[1,64,128]{2,1,0:T(8,128)(2,1)S(1)}, u32[]{:S(2)}, u32[]{:S(2)}) collective-permute-start(bf16[1,64,128]{2,1,0:T(8,128)(2,1)S(1)} %bitcast.10), channel_id=1, source_target_pairs={{0,24},{2,26},{4,28},{6,30},{8,16},{10,18},{12,20},{14,22},{16,8},... | collective-permute-start | bytes 49160 | tf_op jit(solution)/shard_map/ppermute | solution.py:201
  44.9 4.8 %collective-permute-start.8 = (bf16[1,64,128]{2,1,0:T(8,128)(2,1)S(1)}, bf16[1,64,128]{2,1,0:T(8,128)(2,1)S(1)}, u32[]{:S(2)}, u32[]{:S(2)}) collective-permute-start(bf16[1,64,128]{2,1,0:T(8,128)(2,1)S(1)} %bitcast.11), channel_id=1, source_target_pairs={{0,16},{2,18},{4,20},{6,22},{8,24},{10,26},{12,28},{14,30},{16,0},... | collective-permute-start | bytes 49160 | tf_op jit(solution)/shard_map/ppermute | solution.py:201
  44.9 5.0 %collective-permute-start.7 = (bf16[1,64,128]{2,1,0:T(8,128)(2,1)S(1)}, bf16[1,64,128]{2,1,0:T(8,128)(2,1)S(1)}, u32[]{:S(2)}, u32[]{:S(2)}) collective-permute-start(bf16[1,64,128]{2,1,0:T(8,128)(2,1)S(1)} %bitcast.12), channel_id=1, source_target_pairs={{0,8},{2,10},{4,12},{6,14},{8,0},{10,2},{12,4},{14,6},{16,24},{18,... | collective-permute-start | bytes 49160 | tf_op jit(solution)/shard_map/ppermute | solution.py:201
  49.9 5.2 %collective-permute-start.12 = (bf16[4,64,128]{2,1,0:T(8,128)(2,1)S(1)}, bf16[4,64,128]{2,1,0:T(8,128)(2,1)S(1)}, u32[]{:S(2)}, u32[]{:S(2)}) collective-permute-start(bf16[4,64,128]{2,1,0:T(8,128)(2,1)S(1)} %maximum_bitcast_fusion.refs_0_), channel_id=1, source_target_pairs={{0,6},{2,4},{4,2},{6,0},{8,14},{10,12},{12,10},{14,8},{16,22},{18,... | collective-permute-start | bytes 196616 | tf_op jit(solution)/shard_map/ppermute | solution.py:201
  51.5 4.4 %collective-permute-start.11 = (bf16[4,64,128]{2,1,0:T(8,128)(2,1)S(1)}, bf16[4,64,128]{2,1,0:T(8,128)(2,1)S(1)}, u32[]{:S(2)}, u32[]{:S(2)}) collective-permute-start(bf16[4,64,128]{2,1,0:T(8,128)(2,1)S(1)} %maximum_bitcast_fusion.refs_0_), channel_id=1, source_target_pairs={{0,4},{2,6},{4,0},{6,2},{8,12},{10,14},{12,8},{14,10},{16,20},{18,... | collective-permute-start | bytes 196616 | tf_op jit(solution)/shard_map/ppermute | solution.py:201
  52.9 4.3 %collective-permute-start.10 = (bf16[4,64,128]{2,1,0:T(8,128)(2,1)S(1)}, bf16[4,64,128]{2,1,0:T(8,128)(2,1)S(1)}, u32[]{:S(2)}, u32[]{:S(2)}) collective-permute-start(bf16[4,64,128]{2,1,0:T(8,128)(2,1)S(1)} %maximum_bitcast_fusion.refs_0_), channel_id=1, source_target_pairs={{0,2},{2,0},{4,6},{6,4},{8,10},{10,8},{12,14},{14,12},{16,18},{18,... | collective-permute-start | bytes 196616 | tf_op jit(solution)/shard_map/ppermute | solution.py:201
  58.6 1.6 %collective-permute-start.13 = (f32[64,1024]{1,0:T(8,128)S(1)}, f32[64,1024]{1,0:T(8,128)S(1)}, u32[]{:S(2)}, u32[]{:S(2)}) collective-permute-start(f32[64,1024]{1,0:T(8,128)S(1)} %scores.1.own), channel_id=1, source_target_pairs={{0,1},{1,0},{2,3},{3,2},{4,5},{5,4},{6,7},{7,6},{8,9},{9,8},{10,11... | collective-permute-start | bytes 786440 | tf_op jit(solution)/shard_map/ppermute | solution.py:247
  61.1 7.1 %collective-permute-start.14 = (f32[5,64,128]{2,1,0:T(8,128)S(1)}, f32[5,64,128]{2,1,0:T(8,128)S(1)}, u32[]{:S(2)}, u32[]{:S(2)}) collective-permute-start(f32[5,64,128]{2,1,0:T(8,128)S(1)} %get-tuple-element.32), channel_id=1, source_target_pairs={{0,2},{2,0},{4,6},{6,4},{8,10},{10,8},{12,14},{14,12},{16,18},{18,... | collective-permute-start | bytes 491528 | tf_op jit(solution)/shard_map/ppermute | solution.py:201
  61.7 9.5 %collective-permute-start.15 = (f32[5,64,128]{2,1,0:T(8,128)S(1)}, f32[5,64,128]{2,1,0:T(8,128)S(1)}, u32[]{:S(2)}, u32[]{:S(2)}) collective-permute-start(f32[5,64,128]{2,1,0:T(8,128)S(1)} %get-tuple-element.33), channel_id=1, source_target_pairs={{0,4},{2,6},{4,0},{6,2},{8,12},{10,14},{12,8},{14,10},{16,20},{18,... | collective-permute-start | bytes 491528 | tf_op jit(solution)/shard_map/ppermute | solution.py:201
  63.4 7.8 %collective-permute-start.16 = (f32[5,64,128]{2,1,0:T(8,128)S(1)}, f32[5,64,128]{2,1,0:T(8,128)S(1)}, u32[]{:S(2)}, u32[]{:S(2)}) collective-permute-start(f32[5,64,128]{2,1,0:T(8,128)S(1)} %get-tuple-element.34), channel_id=1, source_target_pairs={{0,6},{2,4},{4,2},{6,0},{8,14},{10,12},{12,10},{14,8},{16,22},{18,... | collective-permute-start | bytes 491528 | tf_op jit(solution)/shard_map/ppermute | solution.py:201
  71.3 4.5 %collective-permute-start.17 = (f32[2,64,128]{2,1,0:T(8,128)S(1)}, f32[2,64,128]{2,1,0:T(8,128)S(1)}, u32[]{:S(2)}, u32[]{:S(2)}) collective-permute-start(f32[2,64,128]{2,1,0:T(8,128)S(1)} %get-tuple-element.36), channel_id=1, source_target_pairs={{0,8},{2,10},{4,12},{6,14},{8,0},{10,2},{12,4},{14,6},{16,24},{18,... | collective-permute-start | bytes 196616 | tf_op jit(solution)/shard_map/ppermute | solution.py:201
  73.3 6.3 %collective-permute-start.18 = (f32[2,64,128]{2,1,0:T(8,128)S(1)}, f32[2,64,128]{2,1,0:T(8,128)S(1)}, u32[]{:S(2)}, u32[]{:S(2)}) collective-permute-start(f32[2,64,128]{2,1,0:T(8,128)S(1)} %get-tuple-element.37), channel_id=1, source_target_pairs={{0,16},{2,18},{4,20},{6,22},{8,24},{10,26},{12,28},{14,30},{16,0},... | collective-permute-start | bytes 196616 | tf_op jit(solution)/shard_map/ppermute | solution.py:201
  74.2 6.2 %collective-permute-start.19 = (f32[2,64,128]{2,1,0:T(8,128)S(1)}, f32[2,64,128]{2,1,0:T(8,128)S(1)}, u32[]{:S(2)}, u32[]{:S(2)}) collective-permute-start(f32[2,64,128]{2,1,0:T(8,128)S(1)} %get-tuple-element.38), channel_id=1, source_target_pairs={{0,24},{2,26},{4,28},{6,30},{8,16},{10,18},{12,20},{14,22},{16,8},... | collective-permute-start | bytes 196616 | tf_op jit(solution)/shard_map/ppermute | solution.py:201

commit v4 on v3

--- a/solution.py
+++ b/solution.py
@@ -26,43 +26,25 @@
     return lax.dot_general(a, b, dims, precision=precision, preferred_element_type=F32)
 
 
-def dense_kernel(row, col, count, tiles, basis, x_ref, s_ref, held, sems):
+def dense_kernel(row, col, count, tiles, basis, x_ref, s_ref, sems):
     tile = tiles.shape[-1]
-    rows = x_ref.shape[0] // tile
-    cols = x_ref.shape[1] // tile
-
-    def place(r, c):
-        return x_ref.at[pl.ds(pl.multiple_of(r * tile, tile), tile), pl.ds(pl.multiple_of(c * tile, tile), tile)]
+    slots = tiles.shape[0]
+    x_ref[...] = jnp.zeros(x_ref.shape, BF)
 
     def copy(s):
-        return pltpu.make_async_copy(tiles.at[s], place(row[0, s], col[0, s]), sems.at[s])
-
-    for i in range(rows * cols):
-        held[i] = 0
-    live = count[0, 0]
-
-    def start(s, _):
-        copy(s).start()
-        held[row[0, s] * cols + col[0, s]] = 1
-        return 0
-
-    lax.fori_loop(0, live, start, 0)
-
-    def clear(i, _):
-        @pl.when(held[i] == 0)
+        r, c = pl.multiple_of(row[0, s] * tile, tile), pl.multiple_of(col[0, s] * tile, tile)
+        return pltpu.make_async_copy(tiles.at[s], x_ref.at[pl.ds(r, tile), pl.ds(c, tile)], sems.at[s])
+
+    for s in range(slots):
+        @pl.when(s < count[0, 0])
         def _():
-            spot = place(i // cols, lax.rem(i, cols))
-            spot[...] = jnp.zeros((tile, tile), BF)
-
-        return 0
-
-    lax.fori_loop(0, rows * cols, clear, 0)
-
-    def finish(s, _):
-        copy(s).wait()
-        return 0
-
-    lax.fori_loop(0, live, finish, 0)
+            copy(s).start()
+
+    for s in range(slots):
+        @pl.when(s < count[0, 0])
+        def _():
+            copy(s).wait()
+
     s_ref[...] = dot(basis[...], x_ref[...], NT)
 
 
@@ -235,10 +217,11 @@
         out_shape=(pltpu.VMEM((cells, genes), BF), jax.ShapeDtypeStruct((k, cells), F32)),
         in_specs=[SMEM, SMEM, SMEM, ANY, VMEM],
         out_specs=(VMEM, VMEM),
-        scratch_shapes=[pltpu.SMEM((ROW_BLOCKS * (genes // tile),), jnp.int32), pltpu.SemaphoreType.DMA((slots,))],
+        scratch_shapes=[pltpu.SemaphoreType.DMA((slots,))],
         compiler_params=PARAMS,
         name="dense",
-    )(tile_row, tile_col, tile_count, tiles[0], start_basis)
+    )(tile_row, tile_col, tile_count, pltpu.with_memory_space_constraint(tiles[0], pltpu.HBM), start_basis)
+    x = pltpu.with_memory_space_constraint(x, pltpu.VMEM)
 
     stages = stages_of(n)
     packed = wide == tile and 2 * k == wide

time: 84.9 us -> 81.4 us (0.959)
  Pallas kernels: 16.5 us -> 14.4 us
  local copies, waits for them, and re-layouts: 7.99 us -> 6.39 us
    pallas_call x1, Pallas kernels: 5.88 us -> 3.77 us  [local(): pl.pallas_call(dense_kernel, out_shape=(pltpu.VMEM((cells, genes), BF), j...]
    unnamed x14 -> x12, local copies, waits for them, and re-layouts: 7.99 us -> 6.39 us
  transfers between devices with their start and end apart: 20 -> 20, of which waited for: 17 -> 18; matrix products, arithmetic and copies ran while one was open for 0% -> 0% of each run, Pallas kernels for 0% -> 0%
where the time goes in v4:
time: 81.4 us; the launch traced here: 81.1 us
  waiting for transfers between devices  33 us (41%)
  starting transfers between devices  25.9 us (32%)
  Pallas kernels  14.4 us (18%)
  local copies, waits for them, and re-layouts  6.39 us (8%)
  between operations  1.36 us (2%)
    ppermute x18, waiting for transfers between devices, hop(): return lax.ppermute(value, 'cell', [(i, i ^ distance) for i in range(n)])  30.4 us
    ppermute x18, starting transfers between devices, hop(): return lax.ppermute(value, 'cell', [(i, i ^ distance) for i in range(n)])  25.2 us
    unnamed x12, local copies, waits for them, and re-layouts  6.39 us
    pallas_call x1, Pallas kernels, local(): pl.pallas_call(functools.partial(final_kernel, last, packed, scale), out_...  4.16 us
    pallas_call x1, Pallas kernels, local(): pl.pallas_call(dense_kernel, out_shape=(pltpu.VMEM((cells, genes), BF), j...  3.77 us
    pallas_call x1, Pallas kernels, local(): pl.pallas_call(functools.partial(basis_kernel, last, packed), out_shape=j...  3.21 us
    ppermute x2, waiting for transfers between devices, share(): other = lax.ppermute(half, 'gene', [(0, 1), (1, 0)])  2.68 us
    pallas_call x2, Pallas kernels, share(): pl.pallas_call(functools.partial(packed_kernel, n, count, keep), out_shap...  1.8 us
  transfers between devices with their start and end apart: 20, of which 18 were waited for; matrix products, arithmetic and copies ran while one was open for 0% of the time, Pallas kernels for 0%

profile of v4, /device:TPU:0, one launch (start us, length us, event | category | flops | bytes accessed | tf_op | source)
XLA Modules:
  0.0 81.1 jit_solution(16906116353754522214)
XLA Ops:
  1.3 0.0 copy-start.3
  1.3 0.9 %copy-done.3 = bf16[64,2048]{1,0:T(8,128)(2,1)S(1)} copy-done((bf16[64,2048]{1,0:T(8,128)(2,1)S(1)}, bf16[64,2048]{1,0:T(8,128)(2,1)}, u32[]{:S(2)}) %copy-start.3) | copy-done | bytes 262168
  2.2 0.0 copy-start.4
  2.2 0.7 copy-done.4
  2.9 0.0 copy-start.5
  2.9 0.7 copy-done.5
  3.5 3.8 %dense.1 = (bf16[1024,2048]{1,0:T(8,128)(2,1)S(1)}, f32[64,1024]{1,0:T(8,128)S(1)}) custom-call(s32[1,64]{1,0:T(1,128)S(1)} %copy-done.4, s32[1,64]{1,0:T(1,128)S(1)} %copy-done.5, s32[1,1]{1,0:T(1,128)S(6)} %copy.7.count, bf16[64,128,128]{2,1,0:T(8,128)(2,1)} %bitcast.13, bf16[64,2048]{1,0:T(8,128)(2,1)S(1)} %copy-done.3), custom_call_target="tpu_custom_call" | custom-call | tf_op jit(solution)/shard_map/dense/pallas_call | solution.py:215
  7.3 0.0 copy-start
  7.3 1.9 %copy-done = bf16[1024,2048]{1,0:T(8,128)(2,1)} copy-done((bf16[1024,2048]{1,0:T(8,128)(2,1)}, bf16[1024,2048]{1,0:T(8,128)(2,1)S(1)}, u32[]{:S(2)}) %copy-start) | copy-done | bytes 4194328
  9.3 0.6 collective-permute-start
  9.9 1.2 %collective-permute-done.other = f32[64,1024]{1,0:T(8,128)S(1)} collective-permute-done((f32[64,1024]{1,0:T(8,128)S(1)}, f32[64,1024]{1,0:T(8,128)S(1)}, u32[]{:S(2)}, u32[]{:S(2)}) %collective-permute-start) | collective-permute-done | bytes 262176 | tf_op jit(solution)/shard_map/ppermute | solution.py:230
  11.1 0.0 copy-start.1
  11.1 2.2 %copy-done.1 = bf16[1024,2048]{1,0:T(8,128)(2,1)S(1)} copy-done((bf16[1024,2048]{1,0:T(8,128)(2,1)S(1)}, bf16[1024,2048]{1,0:T(8,128)(2,1)}, u32[]{:S(2)}) %copy-start.1) | copy-done | bytes 4194328
  13.2 0.0 copy-start.2
  13.3 0.9 %share.2 = (f32[5,64,128]{2,1,0:T(8,128)S(1)}, f32[5,64,128]{2,1,0:T(8,128)S(1)}, f32[5,64,128]{2,1,0:T(8,128)S(1)}, f32[5,64,128]{2,1,0:T(8,128)S(1)}) custom-call(s32[1]{0:T(128)} %bitcast.me, f32[64,1024]{1,0:T(8,128)S(1)} %get-tuple-element.21.own, f32[64,1024]{1,0:T(8,128)S(1)} %collective-permute-done.other, bf16[1024,2048]{1,0:T(8,128)(2,1)S(1)} %copy-done.1), custom_call_target="tpu_custom_call" | custom-call | tf_op jit(solution)/shard_map/share/pallas_call | solution.py:250
  14.2 2.9 %collective-permute-start.1 = (f32[5,64,128]{2,1,0:T(8,128)S(1)}, f32[5,64,128]{2,1,0:T(8,128)S(1)}, u32[]{:S(2)}, u32[]{:S(2)}) collective-permute-start(f32[5,64,128]{2,1,0:T(8,128)S(1)} %get-tuple-element.24), channel_id=1, source_target_pairs={{0,2},{2,0},{4,6},{6,4},{8,10},{10,8},{12,14},{14,12},{16,18},{18,... | collective-permute-start | bytes 491528 | tf_op jit(solution)/shard_map/ppermute | solution.py:183
  17.1 1.5 %collective-permute-start.2 = (f32[5,64,128]{2,1,0:T(8,128)S(1)}, f32[5,64,128]{2,1,0:T(8,128)S(1)}, u32[]{:S(2)}, u32[]{:S(2)}) collective-permute-start(f32[5,64,128]{2,1,0:T(8,128)S(1)} %get-tuple-element.25), channel_id=1, source_target_pairs={{0,4},{2,6},{4,0},{6,2},{8,12},{10,14},{12,8},{14,10},{16,20},{18,... | collective-permute-start | bytes 491528 | tf_op jit(solution)/shard_map/ppermute | solution.py:183
  18.6 0.2 collective-permute-start.3
  18.8 3.4 %collective-permute-done.1.refs_1_ = f32[5,64,128]{2,1,0:T(8,128)S(1)} collective-permute-done((f32[5,64,128]{2,1,0:T(8,128)S(1)}, f32[5,64,128]{2,1,0:T(8,128)S(1)}, u32[]{:S(2)}, u32[]{:S(2)}) %collective-permute-start.1) | collective-permute-done | bytes 163872 | tf_op jit(solution)/shard_map/ppermute | solution.py:183
  22.1 3.4 %collective-permute-done.2.refs_2_ = f32[5,64,128]{2,1,0:T(8,128)S(1)} collective-permute-done((f32[5,64,128]{2,1,0:T(8,128)S(1)}, f32[5,64,128]{2,1,0:T(8,128)S(1)}, u32[]{:S(2)}, u32[]{:S(2)}) %collective-permute-start.2) | collective-permute-done | bytes 163872 | tf_op jit(solution)/shard_map/ppermute | solution.py:183
  25.6 1.0 %collective-permute-done.3.refs_3_ = f32[5,64,128]{2,1,0:T(8,128)S(1)} collective-permute-done((f32[5,64,128]{2,1,0:T(8,128)S(1)}, f32[5,64,128]{2,1,0:T(8,128)S(1)}, u32[]{:S(2)}, u32[]{:S(2)}) %collective-permute-start.3) | collective-permute-done | bytes 163872 | tf_op jit(solution)/shard_map/ppermute | solution.py:183
  26.6 1.6 %collective-permute-start.4 = (f32[2,64,128]{2,1,0:T(8,128)S(1)}, f32[2,64,128]{2,1,0:T(8,128)S(1)}, u32[]{:S(2)}, u32[]{:S(2)}) collective-permute-start(f32[2,64,128]{2,1,0:T(8,128)S(1)} %get-tuple-element.28), channel_id=1, source_target_pairs={{0,8},{2,10},{4,12},{6,14},{8,0},{10,2},{12,4},{14,6},{16,24},{18,... | collective-permute-start | bytes 196616 | tf_op jit(solution)/shard_map/ppermute | solution.py:183
  28.2 2.8 %collective-permute-start.5 = (f32[2,64,128]{2,1,0:T(8,128)S(1)}, f32[2,64,128]{2,1,0:T(8,128)S(1)}, u32[]{:S(2)}, u32[]{:S(2)}) collective-permute-start(f32[2,64,128]{2,1,0:T(8,128)S(1)} %get-tuple-element.29), channel_id=1, source_target_pairs={{0,16},{2,18},{4,20},{6,22},{8,24},{10,26},{12,28},{14,30},{16,0},... | collective-permute-start | bytes 196616 | tf_op jit(solution)/shard_map/ppermute | solution.py:183
  31.0 0.1 collective-permute-start.6
  31.1 0.5 collective-permute-done.4.refs_1_
  31.6 3.3 %collective-permute-done.5.refs_2_ = f32[2,64,128]{2,1,0:T(8,128)S(1)} collective-permute-done((f32[2,64,128]{2,1,0:T(8,128)S(1)}, f32[2,64,128]{2,1,0:T(8,128)S(1)}, u32[]{:S(2)}, u32[]{:S(2)}) %collective-permute-start.5) | collective-permute-done | bytes 65568 | tf_op jit(solution)/shard_map/ppermute | solution.py:183
  34.9 2.2 %collective-permute-done.6.refs_3_ = f32[2,64,128]{2,1,0:T(8,128)S(1)} collective-permute-done((f32[2,64,128]{2,1,0:T(8,128)S(1)}, f32[2,64,128]{2,1,0:T(8,128)S(1)}, u32[]{:S(2)}, u32[]{:S(2)}) %collective-permute-start.6) | collective-permute-done | bytes 65568 | tf_op jit(solution)/shard_map/ppermute | solution.py:183
  37.1 3.2 %basis.3 = bf16[64,128]{1,0:T(8,128)(2,1)S(1)} custom-call(f32[2,64,128]{2,1,0:T(8,128)S(1)} %get-tuple-element.27.refs_0_, f32[2,64,128]{2,1,0:T(8,128)S(1)} %collective-permute-done.4.refs_1_, f32[2,64,128]{2,1,0:T(8,128)S(1)} %collective-permute-done.5.refs_2_, f32[2,64,128]{2,1,0:T(8,128)S(1)} %collective-permute-done.6.refs_3_), custom_call_target="tpu_custom_call" | custom-call | tf_op jit(solution)/shard_map/basis/pallas_call | solution.py:274
  40.3 1.1 %collective-permute-start.9 = (bf16[1,64,128]{2,1,0:T(8,128)(2,1)S(1)}, bf16[1,64,128]{2,1,0:T(8,128)(2,1)S(1)}, u32[]{:S(2)}, u32[]{:S(2)}) collective-permute-start(bf16[1,64,128]{2,1,0:T(8,128)(2,1)S(1)} %bitcast.9), channel_id=1, source_target_pairs={{0,24},{2,26},{4,28},{6,30},{8,16},{10,18},{12,20},{14,22},{16,8},... | collective-permute-start | bytes 49160 | tf_op jit(solution)/shard_map/ppermute | solution.py:183
  41.4 0.0 collective-permute-start.8
  41.4 3.4 %collective-permute-start.7 = (bf16[1,64,128]{2,1,0:T(8,128)(2,1)S(1)}, bf16[1,64,128]{2,1,0:T(8,128)(2,1)S(1)}, u32[]{:S(2)}, u32[]{:S(2)}) collective-permute-start(bf16[1,64,128]{2,1,0:T(8,128)(2,1)S(1)} %bitcast.11), channel_id=1, source_target_pairs={{0,8},{2,10},{4,12},{6,14},{8,0},{10,2},{12,4},{14,6},{16,24},{18,... | collective-permute-start | bytes 49160 | tf_op jit(solution)/shard_map/ppermute | solution.py:183
  44.7 1.1 %collective-permute-done.9 = bf16[1,64,128]{2,1,0:T(8,128)(2,1)S(1)} collective-permute-done((bf16[1,64,128]{2,1,0:T(8,128)(2,1)S(1)}, bf16[1,64,128]{2,1,0:T(8,128)(2,1)S(1)}, u32[]{:S(2)}, u32[]{:S(2)}) %collective-permute-start.9) | collective-permute-done | bytes 16416 | tf_op jit(solution)/shard_map/ppermute | solution.py:183
  45.9 0.4 collective-permute-done.8
  46.2 0.2 collective-permute-done.7
  46.5 1.6 %collective-permute-start.12 = (bf16[4,64,128]{2,1,0:T(8,128)(2,1)S(1)}, bf16[4,64,128]{2,1,0:T(8,128)(2,1)S(1)}, u32[]{:S(2)}, u32[]{:S(2)}) collective-permute-start(bf16[4,64,128]{2,1,0:T(8,128)(2,1)S(1)} %maximum_bitcast_fusion.refs_0_), channel_id=1, source_target_pairs={{0,6},{2,4},{4,2},{6,0},{8,14},{10,12},{12,10},{14,8},{16,22},{18,... | collective-permute-start | bytes 196616 | tf_op jit(solution)/shard_map/ppermute | solution.py:183
  48.0 1.3 %collective-permute-start.11 = (bf16[4,64,128]{2,1,0:T(8,128)(2,1)S(1)}, bf16[4,64,128]{2,1,0:T(8,128)(2,1)S(1)}, u32[]{:S(2)}, u32[]{:S(2)}) collective-permute-start(bf16[4,64,128]{2,1,0:T(8,128)(2,1)S(1)} %maximum_bitcast_fusion.refs_0_), channel_id=1, source_target_pairs={{0,4},{2,6},{4,0},{6,2},{8,12},{10,14},{12,8},{14,10},{16,20},{18,... | collective-permute-start | bytes 196616 | tf_op jit(solution)/shard_map/ppermute | solution.py:183
  49.3 0.7 collective-permute-start.10
  50.0 1.7 %collective-permute-done.12.refs_3_ = bf16[4,64,128]{2,1,0:T(8,128)(2,1)S(1)} collective-permute-done((bf16[4,64,128]{2,1,0:T(8,128)(2,1)S(1)}, bf16[4,64,128]{2,1,0:T(8,128)(2,1)S(1)}, u32[]{:S(2)}, u32[]{:S(2)}) %collective-permute-start.12) | collective-permute-done | bytes 65568 | tf_op jit(solution)/shard_map/ppermute | solution.py:183
  51.7 0.7 collective-permute-done.11.refs_2_
  52.4 1.1 %collective-permute-done.10.refs_1_ = bf16[4,64,128]{2,1,0:T(8,128)(2,1)S(1)} collective-permute-done((bf16[4,64,128]{2,1,0:T(8,128)(2,1)S(1)}, bf16[4,64,128]{2,1,0:T(8,128)(2,1)S(1)}, u32[]{:S(2)}, u32[]{:S(2)}) %collective-permute-start.10) | collective-permute-done | bytes 65568 | tf_op jit(solution)/shard_map/ppermute | solution.py:183
  53.5 0.0 copy-done.2
  53.5 1.4 %scores.1.own = f32[64,1024]{1,0:T(8,128)S(1)} custom-call(s32[1]{0:T(128)} %bitcast.me, bf16[4,64,128]{2,1,0:T(8,128)(2,1)S(1)} %maximum_bitcast_fusion.refs_0_, bf16[4,64,128]{2,1,0:T(8,128)(2,1)S(1)} %collective-permute-done.10.refs_1_, bf16[4,64,128]{2,1,0:T(8,128)(2,1)S(1)} %collective-permute-done.11.refs_2_, ...), custom_call_target="tpu_custom_call" | custom-call | tf_op jit(solution)/shard_map/scores/pallas_call | solution.py:285
  55.0 0.1 collective-permute-start.13
  55.0 1.5 %collective-permute-done.13.other = f32[64,1024]{1,0:T(8,128)S(1)} collective-permute-done((f32[64,1024]{1,0:T(8,128)S(1)}, f32[64,1024]{1,0:T(8,128)S(1)}, u32[]{:S(2)}, u32[]{:S(2)}) %collective-permute-start.13) | collective-permute-done | bytes 262176 | tf_op jit(solution)/shard_map/ppermute | solution.py:230
  56.6 0.9 %share.3 = (f32[5,64,128]{2,1,0:T(8,128)S(1)}, f32[5,64,128]{2,1,0:T(8,128)S(1)}, f32[5,64,128]{2,1,0:T(8,128)S(1)}, f32[5,64,128]{2,1,0:T(8,128)S(1)}, f32[64,1024]{1,0:T(8,128)S(1)}) custom-call(s32[1]{0:T(128)} %bitcast.me, f32[64,1024]{1,0:T(8,128)S(1)} %scores.1.own, f32[64,1024]{1,0:T(8,128)S(1)} %collective-permute-done.13.other, ...), custom_call_target="tpu_custom_call" | custom-call | tf_op jit(solution)/shard_map/share/pallas_call | solution.py:250
  57.5 0.8 %collective-permute-start.14 = (f32[5,64,128]{2,1,0:T(8,128)S(1)}, f32[5,64,128]{2,1,0:T(8,128)S(1)}, u32[]{:S(2)}, u32[]{:S(2)}) collective-permute-start(f32[5,64,128]{2,1,0:T(8,128)S(1)} %get-tuple-element.32), channel_id=1, source_target_pairs={{0,2},{2,0},{4,6},{6,4},{8,10},{10,8},{12,14},{14,12},{16,18},{18,... | collective-permute-start | bytes 491528 | tf_op jit(solution)/shard_map/ppermute | solution.py:183
  58.3 1.6 %collective-permute-start.15 = (f32[5,64,128]{2,1,0:T(8,128)S(1)}, f32[5,64,128]{2,1,0:T(8,128)S(1)}, u32[]{:S(2)}, u32[]{:S(2)}) collective-permute-start(f32[5,64,128]{2,1,0:T(8,128)S(1)} %get-tuple-element.33), channel_id=1, source_target_pairs={{0,4},{2,6},{4,0},{6,2},{8,12},{10,14},{12,8},{14,10},{16,20},{18,... | collective-permute-start | bytes 491528 | tf_op jit(solution)/shard_map/ppermute | solution.py:183
  59.9 1.2 %collective-permute-start.16 = (f32[5,64,128]{2,1,0:T(8,128)S(1)}, f32[5,64,128]{2,1,0:T(8,128)S(1)}, u32[]{:S(2)}, u32[]{:S(2)}) collective-permute-start(f32[5,64,128]{2,1,0:T(8,128)S(1)} %get-tuple-element.34), channel_id=1, source_target_pairs={{0,6},{2,4},{4,2},{6,0},{8,14},{10,12},{12,10},{14,8},{16,22},{18,... | collective-permute-start | bytes 491528 | tf_op jit(solution)/shard_map/ppermute | solution.py:183
  61.0 3.6 %collective-permute-done.14.refs_1_ = f32[5,64,128]{2,1,0:T(8,128)S(1)} collective-permute-done((f32[5,64,128]{2,1,0:T(8,128)S(1)}, f32[5,64,128]{2,1,0:T(8,128)S(1)}, u32[]{:S(2)}, u32[]{:S(2)}) %collective-permute-start.14) | collective-permute-done | bytes 163872 | tf_op jit(solution)/shard_map/ppermute | solution.py:183
  64.6 3.2 %collective-permute-done.15.refs_2_ = f32[5,64,128]{2,1,0:T(8,128)S(1)} collective-permute-done((f32[5,64,128]{2,1,0:T(8,128)S(1)}, f32[5,64,128]{2,1,0:T(8,128)S(1)}, u32[]{:S(2)}, u32[]{:S(2)}) %collective-permute-start.15) | collective-permute-done | bytes 163872 | tf_op jit(solution)/shard_map/ppermute | solution.py:183
  67.8 0.0 collective-permute-done.16.refs_3_
  67.8 2.1 %collective-permute-start.17 = (f32[2,64,128]{2,1,0:T(8,128)S(1)}, f32[2,64,128]{2,1,0:T(8,128)S(1)}, u32[]{:S(2)}, u32[]{:S(2)}) collective-permute-start(f32[2,64,128]{2,1,0:T(8,128)S(1)} %get-tuple-element.36), channel_id=1, source_target_pairs={{0,8},{2,10},{4,12},{6,14},{8,0},{10,2},{12,4},{14,6},{16,24},{18,... | collective-permute-start | bytes 196616 | tf_op jit(solution)/shard_map/ppermute | solution.py:183
  69.9 0.9 %collective-permute-start.18 = (f32[2,64,128]{2,1,0:T(8,128)S(1)}, f32[2,64,128]{2,1,0:T(8,128)S(1)}, u32[]{:S(2)}, u32[]{:S(2)}) collective-permute-start(f32[2,64,128]{2,1,0:T(8,128)S(1)} %get-tuple-element.37), channel_id=1, source_target_pairs={{0,16},{2,18},{4,20},{6,22},{8,24},{10,26},{12,28},{14,30},{16,0},... | collective-permute-start | bytes 196616 | tf_op jit(solution)/shard_map/ppermute | solution.py:183
  70.8 1.5 %collective-permute-start.19 = (f32[2,64,128]{2,1,0:T(8,128)S(1)}, f32[2,64,128]{2,1,0:T(8,128)S(1)}, u32[]{:S(2)}, u32[]{:S(2)}) collective-permute-start(f32[2,64,128]{2,1,0:T(8,128)S(1)} %get-tuple-element.38), channel_id=1, source_target_pairs={{0,24},{2,26},{4,28},{6,30},{8,16},{10,18},{12,20},{14,22},{16,8},... | collective-permute-start | bytes 196616 | tf_op jit(solution)/shard_map/ppermute | solution.py:183
  72.3 0.0 collective-permute-done.17.refs_1_
  72.3 3.9 %collective-permute-done.18.refs_2_ = f32[2,64,128]{2,1,0:T(8,128)S(1)} collective-permute-done((f32[2,64,128]{2,1,0:T(8,128)S(1)}, f32[2,64,128]{2,1,0:T(8,128)S(1)}, u32[]{:S(2)}, u32[]{:S(2)}) %collective-permute-start.18) | collective-permute-done | bytes 65568 | tf_op jit(solution)/shard_map/ppermute | solution.py:183
  76.2 0.7 collective-permute-done.19.refs_3_
  77.0 4.2 %final.1 = (bf16[64,1024]{1,0:T(8,128)(2,1)}, f32[64,128]{1,0:T(8,128)}) custom-call(f32[2,64,128]{2,1,0:T(8,128)S(1)} %get-tuple-element.35.refs_0_, f32[2,64,128]{2,1,0:T(8,128)S(1)} %collective-permute-done.17.refs_1_, f32[2,64,128]{2,1,0:T(8,128)S(1)} %collective-permute-done.18.refs_2_, f32[2,64,128]{2,1,0:T(8,128)S(1)} %collective-permute-done.19.refs_3_, ...), custom_call_target="tpu_custom_call" | custom-call | tf_op jit(solution)/shard_map/final/pallas_call | solution.py:302
  (3 shorter events, 0.1 us)
Async XLA Ops:
  1.3 1.0 %copy-start.3 = (bf16[64,2048]{1,0:T(8,128)(2,1)S(1)}, bf16[64,2048]{1,0:T(8,128)(2,1)}, u32[]{:S(2)}) copy-start(bf16[64,2048]{1,0:T(8,128)(2,1)} %basis.2) | copy-start | bytes 786436
  2.2 0.7 copy-start.4
  2.9 0.7 copy-start.5
  7.3 2.0 %copy-start = (bf16[1024,2048]{1,0:T(8,128)(2,1)}, bf16[1024,2048]{1,0:T(8,128)(2,1)S(1)}, u32[]{:S(2)}) copy-start(bf16[1024,2048]{1,0:T(8,128)(2,1)S(1)} %get-tuple-element.22.x.refs_4_) | copy-start | bytes 12582916
  9.3 1.8 %collective-permute-start = (f32[64,1024]{1,0:T(8,128)S(1)}, f32[64,1024]{1,0:T(8,128)S(1)}, u32[]{:S(2)}, u32[]{:S(2)}) collective-permute-start(f32[64,1024]{1,0:T(8,128)S(1)} %get-tuple-element.21.own), channel_id=1, source_target_pairs={{0,1},{1,0},{2,3},{3,2},{4,5},{5,4},{6,7},{7,6},{8,9},{9,8},{10,11... | collective-permute-start | bytes 786440 | tf_op jit(solution)/shard_map/ppermute | solution.py:230
  11.1 2.2 %copy-start.1 = (bf16[1024,2048]{1,0:T(8,128)(2,1)S(1)}, bf16[1024,2048]{1,0:T(8,128)(2,1)}, u32[]{:S(2)}) copy-start(bf16[1024,2048]{1,0:T(8,128)(2,1)} %copy-done) | copy-start | bytes 12582916
  13.2 40.3 %copy-start.2 = (bf16[1024,2048]{1,0:T(8,128)(2,1)S(1)}, bf16[1024,2048]{1,0:T(8,128)(2,1)}, u32[]{:S(2)}) copy-start(bf16[1024,2048]{1,0:T(8,128)(2,1)} %copy-done) | copy-start | bytes 12582916
  14.2 8.0 %collective-permute-start.1 = (f32[5,64,128]{2,1,0:T(8,128)S(1)}, f32[5,64,128]{2,1,0:T(8,128)S(1)}, u32[]{:S(2)}, u32[]{:S(2)}) collective-permute-start(f32[5,64,128]{2,1,0:T(8,128)S(1)} %get-tuple-element.24), channel_id=1, source_target_pairs={{0,2},{2,0},{4,6},{6,4},{8,10},{10,8},{12,14},{14,12},{16,18},{18,... | collective-permute-start | bytes 491528 | tf_op jit(solution)/shard_map/ppermute | solution.py:183
  17.1 8.5 %collective-permute-start.2 = (f32[5,64,128]{2,1,0:T(8,128)S(1)}, f32[5,64,128]{2,1,0:T(8,128)S(1)}, u32[]{:S(2)}, u32[]{:S(2)}) collective-permute-start(f32[5,64,128]{2,1,0:T(8,128)S(1)} %get-tuple-element.25), channel_id=1, source_target_pairs={{0,4},{2,6},{4,0},{6,2},{8,12},{10,14},{12,8},{14,10},{16,20},{18,... | collective-permute-start | bytes 491528 | tf_op jit(solution)/shard_map/ppermute | solution.py:183
  18.6 8.0 %collective-permute-start.3 = (f32[5,64,128]{2,1,0:T(8,128)S(1)}, f32[5,64,128]{2,1,0:T(8,128)S(1)}, u32[]{:S(2)}, u32[]{:S(2)}) collective-permute-start(f32[5,64,128]{2,1,0:T(8,128)S(1)} %get-tuple-element.26), channel_id=1, source_target_pairs={{0,6},{2,4},{4,2},{6,0},{8,14},{10,12},{12,10},{14,8},{16,22},{18,... | collective-permute-start | bytes 491528 | tf_op jit(solution)/shard_map/ppermute | solution.py:183
  26.6 5.0 %collective-permute-start.4 = (f32[2,64,128]{2,1,0:T(8,128)S(1)}, f32[2,64,128]{2,1,0:T(8,128)S(1)}, u32[]{:S(2)}, u32[]{:S(2)}) collective-permute-start(f32[2,64,128]{2,1,0:T(8,128)S(1)} %get-tuple-element.28), channel_id=1, source_target_pairs={{0,8},{2,10},{4,12},{6,14},{8,0},{10,2},{12,4},{14,6},{16,24},{18,... | collective-permute-start | bytes 196616 | tf_op jit(solution)/shard_map/ppermute | solution.py:183
  28.2 6.7 %collective-permute-start.5 = (f32[2,64,128]{2,1,0:T(8,128)S(1)}, f32[2,64,128]{2,1,0:T(8,128)S(1)}, u32[]{:S(2)}, u32[]{:S(2)}) collective-permute-start(f32[2,64,128]{2,1,0:T(8,128)S(1)} %get-tuple-element.29), channel_id=1, source_target_pairs={{0,16},{2,18},{4,20},{6,22},{8,24},{10,26},{12,28},{14,30},{16,0},... | collective-permute-start | bytes 196616 | tf_op jit(solution)/shard_map/ppermute | solution.py:183
  31.0 6.1 %collective-permute-start.6 = (f32[2,64,128]{2,1,0:T(8,128)S(1)}, f32[2,64,128]{2,1,0:T(8,128)S(1)}, u32[]{:S(2)}, u32[]{:S(2)}) collective-permute-start(f32[2,64,128]{2,1,0:T(8,128)S(1)} %get-tuple-element.30), channel_id=1, source_target_pairs={{0,24},{2,26},{4,28},{6,30},{8,16},{10,18},{12,20},{14,22},{16,8},... | collective-permute-start | bytes 196616 | tf_op jit(solution)/shard_map/ppermute | solution.py:183
  40.3 5.6 %collective-permute-start.9 = (bf16[1,64,128]{2,1,0:T(8,128)(2,1)S(1)}, bf16[1,64,128]{2,1,0:T(8,128)(2,1)S(1)}, u32[]{:S(2)}, u32[]{:S(2)}) collective-permute-start(bf16[1,64,128]{2,1,0:T(8,128)(2,1)S(1)} %bitcast.9), channel_id=1, source_target_pairs={{0,24},{2,26},{4,28},{6,30},{8,16},{10,18},{12,20},{14,22},{16,8},... | collective-permute-start | bytes 49160 | tf_op jit(solution)/shard_map/ppermute | solution.py:183
  41.4 4.9 %collective-permute-start.8 = (bf16[1,64,128]{2,1,0:T(8,128)(2,1)S(1)}, bf16[1,64,128]{2,1,0:T(8,128)(2,1)S(1)}, u32[]{:S(2)}, u32[]{:S(2)}) collective-permute-start(bf16[1,64,128]{2,1,0:T(8,128)(2,1)S(1)} %bitcast.10), channel_id=1, source_target_pairs={{0,16},{2,18},{4,20},{6,22},{8,24},{10,26},{12,28},{14,30},{16,0},... | collective-permute-start | bytes 49160 | tf_op jit(solution)/shard_map/ppermute | solution.py:183
  41.4 5.1 %collective-permute-start.7 = (bf16[1,64,128]{2,1,0:T(8,128)(2,1)S(1)}, bf16[1,64,128]{2,1,0:T(8,128)(2,1)S(1)}, u32[]{:S(2)}, u32[]{:S(2)}) collective-permute-start(bf16[1,64,128]{2,1,0:T(8,128)(2,1)S(1)} %bitcast.11), channel_id=1, source_target_pairs={{0,8},{2,10},{4,12},{6,14},{8,0},{10,2},{12,4},{14,6},{16,24},{18,... | collective-permute-start | bytes 49160 | tf_op jit(solution)/shard_map/ppermute | solution.py:183
  46.5 5.2 %collective-permute-start.12 = (bf16[4,64,128]{2,1,0:T(8,128)(2,1)S(1)}, bf16[4,64,128]{2,1,0:T(8,128)(2,1)S(1)}, u32[]{:S(2)}, u32[]{:S(2)}) collective-permute-start(bf16[4,64,128]{2,1,0:T(8,128)(2,1)S(1)} %maximum_bitcast_fusion.refs_0_), channel_id=1, source_target_pairs={{0,6},{2,4},{4,2},{6,0},{8,14},{10,12},{12,10},{14,8},{16,22},{18,... | collective-permute-start | bytes 196616 | tf_op jit(solution)/shard_map/ppermute | solution.py:183
  48.0 4.4 %collective-permute-start.11 = (bf16[4,64,128]{2,1,0:T(8,128)(2,1)S(1)}, bf16[4,64,128]{2,1,0:T(8,128)(2,1)S(1)}, u32[]{:S(2)}, u32[]{:S(2)}) collective-permute-start(bf16[4,64,128]{2,1,0:T(8,128)(2,1)S(1)} %maximum_bitcast_fusion.refs_0_), channel_id=1, source_target_pairs={{0,4},{2,6},{4,0},{6,2},{8,12},{10,14},{12,8},{14,10},{16,20},{18,... | collective-permute-start | bytes 196616 | tf_op jit(solution)/shard_map/ppermute | solution.py:183
  49.3 4.3 %collective-permute-start.10 = (bf16[4,64,128]{2,1,0:T(8,128)(2,1)S(1)}, bf16[4,64,128]{2,1,0:T(8,128)(2,1)S(1)}, u32[]{:S(2)}, u32[]{:S(2)}) collective-permute-start(bf16[4,64,128]{2,1,0:T(8,128)(2,1)S(1)} %maximum_bitcast_fusion.refs_0_), channel_id=1, source_target_pairs={{0,2},{2,0},{4,6},{6,4},{8,10},{10,8},{12,14},{14,12},{16,18},{18,... | collective-permute-start | bytes 196616 | tf_op jit(solution)/shard_map/ppermute | solution.py:183
  55.0 1.6 %collective-permute-start.13 = (f32[64,1024]{1,0:T(8,128)S(1)}, f32[64,1024]{1,0:T(8,128)S(1)}, u32[]{:S(2)}, u32[]{:S(2)}) collective-permute-start(f32[64,1024]{1,0:T(8,128)S(1)} %scores.1.own), channel_id=1, source_target_pairs={{0,1},{1,0},{2,3},{3,2},{4,5},{5,4},{6,7},{7,6},{8,9},{9,8},{10,11... | collective-permute-start | bytes 786440 | tf_op jit(solution)/shard_map/ppermute | solution.py:230
  57.5 7.1 %collective-permute-start.14 = (f32[5,64,128]{2,1,0:T(8,128)S(1)}, f32[5,64,128]{2,1,0:T(8,128)S(1)}, u32[]{:S(2)}, u32[]{:S(2)}) collective-permute-start(f32[5,64,128]{2,1,0:T(8,128)S(1)} %get-tuple-element.32), channel_id=1, source_target_pairs={{0,2},{2,0},{4,6},{6,4},{8,10},{10,8},{12,14},{14,12},{16,18},{18,... | collective-permute-start | bytes 491528 | tf_op jit(solution)/shard_map/ppermute | solution.py:183
  58.3 9.5 %collective-permute-start.15 = (f32[5,64,128]{2,1,0:T(8,128)S(1)}, f32[5,64,128]{2,1,0:T(8,128)S(1)}, u32[]{:S(2)}, u32[]{:S(2)}) collective-permute-start(f32[5,64,128]{2,1,0:T(8,128)S(1)} %get-tuple-element.33), channel_id=1, source_target_pairs={{0,4},{2,6},{4,0},{6,2},{8,12},{10,14},{12,8},{14,10},{16,20},{18,... | collective-permute-start | bytes 491528 | tf_op jit(solution)/shard_map/ppermute | solution.py:183
  59.9 7.9 %collective-permute-start.16 = (f32[5,64,128]{2,1,0:T(8,128)S(1)}, f32[5,64,128]{2,1,0:T(8,128)S(1)}, u32[]{:S(2)}, u32[]{:S(2)}) collective-permute-start(f32[5,64,128]{2,1,0:T(8,128)S(1)} %get-tuple-element.34), channel_id=1, source_target_pairs={{0,6},{2,4},{4,2},{6,0},{8,14},{10,12},{12,10},{14,8},{16,22},{18,... | collective-permute-start | bytes 491528 | tf_op jit(solution)/shard_map/ppermute | solution.py:183
  67.8 4.5 %collective-permute-start.17 = (f32[2,64,128]{2,1,0:T(8,128)S(1)}, f32[2,64,128]{2,1,0:T(8,128)S(1)}, u32[]{:S(2)}, u32[]{:S(2)}) collective-permute-start(f32[2,64,128]{2,1,0:T(8,128)S(1)} %get-tuple-element.36), channel_id=1, source_target_pairs={{0,8},{2,10},{4,12},{6,14},{8,0},{10,2},{12,4},{14,6},{16,24},{18,... | collective-permute-start | bytes 196616 | tf_op jit(solution)/shard_map/ppermute | solution.py:183
  69.9 6.3 %collective-permute-start.18 = (f32[2,64,128]{2,1,0:T(8,128)S(1)}, f32[2,64,128]{2,1,0:T(8,128)S(1)}, u32[]{:S(2)}, u32[]{:S(2)}) collective-permute-start(f32[2,64,128]{2,1,0:T(8,128)S(1)} %get-tuple-element.37), channel_id=1, source_target_pairs={{0,16},{2,18},{4,20},{6,22},{8,24},{10,26},{12,28},{14,30},{16,0},... | collective-permute-start | bytes 196616 | tf_op jit(solution)/shard_map/ppermute | solution.py:183
  70.8 6.2 %collective-permute-start.19 = (f32[2,64,128]{2,1,0:T(8,128)S(1)}, f32[2,64,128]{2,1,0:T(8,128)S(1)}, u32[]{:S(2)}, u32[]{:S(2)}) collective-permute-start(f32[2,64,128]{2,1,0:T(8,128)S(1)} %get-tuple-element.38), channel_id=1, source_target_pairs={{0,24},{2,26},{4,28},{6,30},{8,16},{10,18},{12,20},{14,22},{16,8},... | collective-permute-start | bytes 196616 | tf_op jit(solution)/shard_map/ppermute | solution.py:183
